TPU v7x, 32 devices: a whole 2x2x4 slice. The times are simulated.
32 devices in a mesh: dp: 4 (over x, core), ctx: 8 (over z, y).
Axes of the slice: x: 2, y: 2, z: 4, core: 2. Of those that a mesh axis runs over, the one named last changes fastest.
Arguments:
- frames: bfloat16 [4, 40, 16, 16, 512], P('dp', 'ctx'), may hold values from -6 to 6
- stream: bfloat16 [4, 40, 64, 3072], P('dp', 'ctx'), may hold values from -6 to 6
- video_frames: int32 [4], P('dp'), may hold values from 1 to 40
- conv_weight: bfloat16 [3, 3, 3, 512, 512], replicated, may hold values from -0.0546875 to 0.0546875
- latent_weight: bfloat16 [512, 16], replicated, may hold values from -0.25 to 0.25
- embed_weight: bfloat16 [64, 3072], replicated, may hold values from -0.75 to 0.75
- norm_gain: float32 [3072], replicated, may hold values from 0.25 to 1.75
- qkv_weight: bfloat16 [3072, 4608], P('ctx', 'dp'), may hold values from -0.109375 to 0.109375
Outputs:
- section: bfloat16 [4, 40, 16, 16, 512], P('dp', 'ctx')
- mixed: bfloat16 [4, 40, 64, 1536], P('dp', 'ctx')
All inputs are finite; a program needn't handle non-finite values.
Results may differ from a plain program's by a relative error of at most 0.0061.
Values may be sent and summed in bfloat16 or wider, within the bound.
No kernel may reach another device: no remote copies, remote signals or barrier semaphores. Data moves between devices by JAX's collectives and lax.ppermute only.
A program may use at most 128 MiB of HBM per device.

v0:
```python
import jax
import jax.numpy as jnp
from jax import lax
from jax.sharding import PartitionSpec as P

HD = 128


def passed_along(value, axis, steps):
    count = lax.axis_size(axis)
    leading, last = (max(0, -steps), min(count, count - steps))
    return lax.ppermute(value, axis, [(source, source + steps) for source in range(leading, last)])


def attend(lengths, block):
    head_size = block.shape[-1] // 3
    slots = block.shape[1]
    query = block[..., 0:head_size]
    keys = block[..., head_size : 2 * head_size]
    values = block[..., 2 * head_size : 3 * head_size]
    scores = jnp.einsum(
        "gtphd,gsphd->gphts", query, keys, preferred_element_type=jnp.float32
    ) * head_size ** (-0.5)
    frame_ids = jnp.arange(slots, dtype=jnp.int32)
    video = frame_ids[None, :] < lengths[:, None]
    allowed = (
        video[:, :, None] & video[:, None, :] | (frame_ids[:, None] == frame_ids[None, :])[None]
    )
    scores = jnp.where(allowed[:, None, None], scores, -1e30)
    top = jnp.max(scores, axis=-1, keepdims=True)
    expo = jnp.exp(scores - top)
    probs = (expo / jnp.sum(expo, axis=-1, keepdims=True)).astype(jnp.bfloat16)
    out = jnp.einsum(
        "gphts,gsphd->gtphd", probs, values, preferred_element_type=jnp.float32
    ).astype(jnp.bfloat16)
    return lax.all_to_all(out, "ctx", split_axis=1, concat_axis=2, tiled=True)


def on_device(
    frames, stream, video_frames, conv_weight, latent_weight, embed_weight, norm_gain, qkv_weight
):
    f_dev, height, width, channels = (
        frames.shape[1],
        frames.shape[2],
        frames.shape[3],
        frames.shape[4],
    )
    width_model = stream.shape[3]
    tokens_frame = stream.shape[2]
    act = jax.nn.silu(frames.astype(jnp.float32)).astype(jnp.bfloat16)
    past = passed_along(act[:, f_dev - 2 :], "ctx", 1)
    joined = jnp.concatenate([past, act], axis=1)[0]
    padded = jnp.pad(joined, ((0, 0), (1, 1), (1, 1), (0, 0)))
    length = video_frames[0]
    frame_ids = lax.axis_index("ctx") * f_dev + jnp.arange(f_dev, dtype=jnp.int32)
    cells = f_dev * height * width
    total = jnp.zeros((cells, channels), jnp.float32)
    for lag in range(3):
        part = jnp.zeros((cells, channels), jnp.float32)
        for row in range(3):
            for col in range(3):
                slab = padded[
                    2 - lag : 2 - lag + f_dev, row : row + height, col : col + width, :
                ].reshape(-1, channels)
                part = part + jnp.dot(
                    slab, conv_weight[lag, row, col], preferred_element_type=jnp.float32
                )
        if lag == 0:
            total = part
        else:
            valid = ((frame_ids < length) & (frame_ids >= lag)).astype(jnp.float32)
            total = total + part * jnp.repeat(valid, height * width)[:, None]
    section = (frames.astype(jnp.float32) + total.reshape(frames.shape)).astype(jnp.bfloat16)
    latent = jnp.dot(
        section.reshape(-1, channels), latent_weight, preferred_element_type=jnp.float32
    ).astype(jnp.bfloat16)
    lat_size = latent.shape[1]
    latent = latent.reshape(f_dev, height // 2, 2, width // 2, 2, lat_size).transpose(
        0, 1, 3, 2, 4, 5
    )
    patches = latent.reshape(-1, 4 * lat_size)
    embedded = jnp.dot(patches, embed_weight, preferred_element_type=jnp.float32) + stream.reshape(
        -1, width_model
    ).astype(jnp.float32)
    scale = lax.rsqrt(jnp.mean(embedded * embedded, axis=-1, keepdims=True) + 1e-06)
    normed = (embedded * scale * norm_gain).astype(jnp.bfloat16)
    head_size = HD
    gathered, lengths = (
        lax.all_gather(normed.reshape(1, -1, width_model), "dp", axis=0, tiled=True),
        lax.all_gather(video_frames, "dp", axis=0, tiled=True),
    )
    group_count = gathered.shape[0]
    all_rows = gathered.reshape(-1, width_model)
    qkv = jnp.dot(
        all_rows,
        lax.all_gather(qkv_weight, "ctx", axis=0, tiled=True),
        preferred_element_type=jnp.float32,
    )
    qkv = qkv.astype(jnp.bfloat16).reshape(
        group_count, f_dev, tokens_frame, qkv_weight.shape[1] // (3 * head_size), 3 * head_size
    )
    mixed = attend(lengths, lax.all_to_all(qkv, "ctx", split_axis=2, concat_axis=1, tiled=True))
    mixed = lax.all_to_all(mixed, "dp", split_axis=0, concat_axis=3, tiled=True)
    return (section, mixed.reshape(1, f_dev, tokens_frame, -1))


def solution(mesh):
    return jax.shard_map(
        on_device,
        mesh=mesh,
        in_specs=(
            P("dp", "ctx", None, None, None),
            P("dp", "ctx", None, None),
            P("dp"),
            P(),
            P(),
            P(),
            P(),
            P("ctx", "dp"),
        ),
        out_specs=(P("dp", "ctx", None, None, None), P("dp", "ctx", None, None)),
        check_vma=False,
    )
```

profile of v0, /device:TPU:0, one launch (start us, length us, event | category | flops | bytes accessed | tf_op | source)
XLA Modules:
  0.0 400.9 jit_solution(8055720071462258511)
XLA Ops:
  7.2 2.1 fusion.8
  9.4 4.9 %collective-permute-start = (bf16[1,2,16,16,512]{4,3,2,1,0:T(8,128)(2,1)S(1)}, bf16[1,2,16,16,512]{4,3,2,1,0:T(8,128)(2,1)S(1)}, u32[]{:S(2)}, u32[]{:S(2)}) collective-permute-start(bf16[1,2,16,16,512]{4,3,2,1,0:T(8,128)(2,1)S(1)} %slice.235), channel_id=1, source_target_pairs={{0,1},{1,2},{2,3},{3,4},{4,5},{5,6},{6,7},{8,9},{9,10},{10,11},{11... | collective-permute-start | bytes 1572872 | tf_op jit(solution)/shard_map/ppermute | solution.py:12
  15.2 10.3 %collective-permute-done = bf16[1,2,16,16,512]{4,3,2,1,0:T(8,128)(2,1)S(1)} collective-permute-done((bf16[1,2,16,16,512]{4,3,2,1,0:T(8,128)(2,1)S(1)}, bf16[1,2,16,16,512]{4,3,2,1,0:T(8,128)(2,1)S(1)}, u32[]{:S(2)}, u32[]{:S(2)}) %collective-permute-start) | collective-permute-done | bytes 524320 | tf_op jit(solution)/shard_map/ppermute | solution.py:12
  25.7 11.1 %pad_slice_fusion = (bf16[5,16,16,512]{3,2,1,0:T(8,128)(2,1)}, bf16[5,16,16,512]{3,2,1,0:T(8,128)(2,1)}, bf16[5,16,16,512]{3,2,1,0:T(8,128)(2,1)}, bf16[5,16,16,...) fusion(bf16[7,16,16,512]{3,2,1,0:T(8,128)(2,1)S(1)} %fusion.10), kind=kLoop, calls=%fused_computation.1 | loop fusion | bytes 26738688 | tf_op jit(solution)/shard_map/slice | solution.py:62
  36.8 2.7 pad_slice_fusion.1
  39.5 0.8 fusion.41
  40.4 0.8 fusion.51
  41.2 0.5 copy-done.15
  41.7 0.8 fusion.31
  42.7 0.9 convolution_add_fusion.16
  44.0 0.9 convolution_add_fusion.15
  45.3 0.9 convolution_add_fusion.14
  46.4 0.9 convolution_add_fusion.13
  47.7 0.9 convolution_add_fusion.12
  48.6 0.5 copy-done.10
  49.0 0.9 convolution_add_fusion.11
  49.9 0.5 copy-done.9
  50.3 0.9 convolution_add_fusion.10
  51.7 0.9 convolution_add_fusion.24
  52.5 0.5 copy-done.7
  53.0 0.9 convolution_add_fusion.23
  53.8 0.5 copy-done.6
  54.3 0.9 convolution_add_fusion.22
  55.2 0.8 convolution_add_fusion.21
  56.0 0.5 copy-done.5
  56.5 0.9 convolution_add_fusion.20
  57.3 0.5 copy-done.4
  57.8 0.9 convolution_add_fusion.19
  59.1 0.8 convolution_add_fusion.18
  60.0 0.5 copy-done.2
  60.4 0.9 convolution_add_fusion.17
  61.3 0.5 copy-done.1
  61.7 0.9 convolution_add_fusion.8
  62.6 0.9 convolution_add_fusion.7
  63.5 0.8 convolution_add_fusion.6
  64.3 1.1 convolution_add_fusion.5
  65.4 0.8 convolution_add_fusion.4
  66.2 0.8 convolution_add_fusion.3
  67.1 0.9 convolution_add_fusion.2
  68.4 1.0 fusion.4
  69.7 0.9 fusion.2
  71.0 0.6 fusion.9
  71.7 1.0 copy-done.19
  73.9 0.8 multiply_reduce_fusion
  74.7 1.8 multiply_convert_fusion
  76.6 0.7 all-gather.4.cloned.1.call-update
  77.3 56.9 %all-gather.6.cloned.1.call-done = bf16[1280,3072]{1,0:T(8,128)(2,1)} async-done(((bf16[320,3072]{1,0:T(8,128)(2,1)}), bf16[1280,3072]{1,0:T(8,128)(2,1)}) %all-gather.6.cloned.1.call-update) | async-done | bytes 7864336 | tf_op jit(solution)/shard_map/all_gather | solution.py:89
  134.2 110.5 %all-gather.4.cloned.1.call-done = bf16[3072,1152]{1,0:T(8,128)(2,1)} async-done(((bf16[384,1152]{1,0:T(8,128)(2,1)}), bf16[3072,1152]{1,0:T(8,128)(2,1)}) %all-gather.4.cloned.1.call-update) | async-done | bytes 7077904 | tf_op jit(solution)/shard_map/all_gather | solution.py:96
  244.7 14.7 %convolution_convert_fusion = bf16[1280,1152]{1,0:T(8,128)(2,1)S(1)} fusion(bf16[1280,3072]{1,0:T(8,128)(2,1)} %all-gather.6.cloned.1.call-done, bf16[3072,1152]{1,0:T(8,128)(2,1)} %all-gather.4.cloned.1.call-done), kind=kOutput, calls=%fused_computation.25 | convolution fusion | flops 9061171200 | bytes 17891328 | tf_op jit(solution)/shard_map/dot_general | solution.py:94
  259.4 4.3 %reshape.215 = bf16[4,5,64,3,384]{4,3,2,1,0:T(4,128)(2,1)} reshape(bf16[1280,1152]{1,0:T(8,128)(2,1)S(1)} %convolution_convert_fusion) | data formatting | bytes 5898240 | tf_op jit(solution)/shard_map/reshape | solution.py:99
  263.7 7.5 %copy.48 = bf16[4,5,64,3,384]{4,0,3,1,2:T(4,128)(2,1)} copy(bf16[4,5,64,3,384]{4,3,2,1,0:T(4,128)(2,1)} %reshape.215) | data formatting | bytes 5898240 | tf_op jit(solution)/shard_map/reshape | solution.py:99
  271.2 3.8 all-to-all-start
  275.0 0.6 dynamic-slice
  275.7 0.8 dynamic-update-slice
  276.5 4.9 %all-reduce.1 = s32[4]{0:T(128)S(1)} all-reduce(s32[4]{0:T(128)S(1)} %dynamic-update-slice), channel_id=1, replica_groups=mesh['dp'=4,'ctx'=8] {'dp'}, use_global_device_ids=true, to_apply=%add.1 | all-reduce | flops 4 | bytes 32
  281.5 59.2 %all-to-all-done = bf16[4,5,64,3,384]{4,0,3,1,2:T(4,128)(2,1)S(1)} async-done(((bf16[4,5,64,3,384]{4,0,3,1,2:T(4,128)(2,1)}), bf16[4,5,64,3,384]{4,0,3,1,2:T(4,128)(2,1)S(1)}, u32[]{:S(2)}, u32[]{:S(2)}) %all-to-all-start) | async-done | bytes 2949152 | tf_op jit(solution)/shard_map/all_to_all | solution.py:102
  340.7 0.6 copy.88
  341.6 0.7 fusion.94
  342.3 2.4 fusion.95
  344.7 2.3 fusion.12
  347.1 28.0 %all_to_all.51 = bf16[4,40,8,3,128]{4,2,3,0,1:T(8,128)(2,1)S(1)} all-to-all(bf16[4,40,8,3,128]{4,2,3,0,1:T(8,128)(2,1)S(1)} %copy.55), channel_id=1, replica_groups=mesh['dp'=4,'ctx'=8] {'ctx'}, dimensions={1} | all-to-all | bytes 1966080 | tf_op jit(solution)/shard_map/all_to_all | solution.py:36
  375.5 16.2 %all_to_all.52 = bf16[4,5,64,3,128]{4,2,3,1,0:T(8,128)(2,1)S(1)} all-to-all(bf16[4,5,64,3,128]{4,2,3,1,0:T(8,128)(2,1)S(1)} %bitcast.204), channel_id=1, replica_groups=mesh['dp'=4,'ctx'=8] {'dp'}, dimensions={0} | all-to-all | bytes 1966080 | tf_op jit(solution)/shard_map/all_to_all | solution.py:103
  391.6 0.8 copy.58
  392.5 1.6 reshape.216
  (70 shorter events, 6.2 us)
Async XLA Ops:
  7.2 66.7 %copy-start = (bf16[64,3072]{1,0:T(8,128)(2,1)S(1)}, bf16[64,3072]{1,0:T(8,128)(2,1)}, u32[]{:S(2)}) copy-start(bf16[64,3072]{1,0:T(8,128)(2,1)} %param.13) | copy-start | bytes 1179652
  7.2 127.0 %all-gather.6.cloned.1.call-start = ((), (), s32[]{:S(2)}) async-start(), calls=%async_computation.4 | async-start | bytes 9830400 | tf_op jit(solution)/shard_map/all_gather | solution.py:89
  9.4 16.1 %collective-permute-start = (bf16[1,2,16,16,512]{4,3,2,1,0:T(8,128)(2,1)S(1)}, bf16[1,2,16,16,512]{4,3,2,1,0:T(8,128)(2,1)S(1)}, u32[]{:S(2)}, u32[]{:S(2)}) collective-permute-start(bf16[1,2,16,16,512]{4,3,2,1,0:T(8,128)(2,1)S(1)} %slice.235), channel_id=1, source_target_pairs={{0,1},{1,2},{2,3},{3,4},{4,5},{5,6},{6,7},{8,9},{9,10},{10,11},{11... | collective-permute-start | bytes 1572872 | tf_op jit(solution)/shard_map/ppermute | solution.py:12
  25.5 14.0 %slice-start = ((s8[14155776]{0:T(1024)(128)(4,1)}), s8[4194304]{0:T(1024)(128)(4,1)S(1)}, s32[]{:S(2)}) async-start(s8[14155776]{0:T(1024)(128)(4,1)} %bitcast.171), calls=%async_computation.5 | async-start | bytes 8388608
  25.6 13.9 %slice-start.1 = ((s8[14155776]{0:T(1024)(128)(4,1)}), s8[4194304]{0:T(1024)(128)(4,1)S(1)}, s32[]{:S(2)}) async-start(s8[14155776]{0:T(1024)(128)(4,1)} %bitcast.171), calls=%async_computation.6 | async-start | bytes 8388608
  25.7 13.9 %slice-start.2 = ((s8[14155776]{0:T(1024)(128)(4,1)}), s8[4194304]{0:T(1024)(128)(4,1)S(1)}, s32[]{:S(2)}) async-start(s8[14155776]{0:T(1024)(128)(4,1)} %bitcast.171), calls=%async_computation.7 | async-start | bytes 8388608
  25.7 13.9 %slice-start.3 = ((s8[14155776]{0:T(1024)(128)(4,1)}), s8[1572864]{0:T(1024)(128)(4,1)S(1)}, s32[]{:S(2)}) async-start(s8[14155776]{0:T(1024)(128)(4,1)} %bitcast.171), calls=%async_computation.8 | async-start | bytes 3145728
  40.4 1.3 copy-start.15
  41.2 1.4 copy-start.14
  42.7 1.3 copy-start.13
  44.0 1.3 copy-start.12
  46.4 1.3 copy-start.11
  47.7 1.3 copy-start.10
  49.0 1.3 copy-start.9
  50.3 1.3 copy-start.8
  51.7 1.3 copy-start.7
  53.0 1.3 copy-start.6
  55.2 1.3 copy-start.5
  56.5 1.3 copy-start.4
  57.8 1.3 copy-start.3
  59.1 1.3 copy-start.2
  60.4 1.3 copy-start.1
  67.1 1.3 copy-start.17
  68.4 1.3 copy-start.16
  69.7 1.3 copy-start.18
  71.0 1.7 copy-start.21
  71.6 1.1 copy-start.19
  71.7 2.2 copy-start.20
  73.9 0.8 copy-start.22
  76.5 168.2 %all-gather.4.cloned.1.call-start = ((), (), s32[]{:S(2)}) async-start(), calls=%async_computation.3 | async-start | bytes 7962624 | tf_op jit(solution)/shard_map/all_gather | solution.py:96
  271.2 3.8 copy-start.23
  271.2 69.5 %all-to-all-start = ((bf16[4,5,64,3,384]{4,0,3,1,2:T(4,128)(2,1)}), bf16[4,5,64,3,384]{4,0,3,1,2:T(4,128)(2,1)S(1)}, u32[]{:S(2)}, u32[]{:S(2)}) async-start(bf16[4,5,64,3,384]{4,0,3,1,2:T(4,128)(2,1)} %copy.48), calls=%async_computation | async-start | bytes 5898240 | tf_op jit(solution)/shard_map/all_to_all | solution.py:102
Sparse Core Ops, SparseCore 0:
  76.6 57.4 all-gather.5
  136.3 108.2 all-gather.3
where the time goes:
time: 402 us; the launch traced here: 401 us
  waiting for transfers between devices  238 us (59%)
  blocking collectives  49.1 us (12%)
  matrix products  44 us (11%)
  local copies, waits for them, and re-layouts  41.1 us (10%)
  between operations  15.2 us (4%)
  starting transfers between devices  8.78 us (2%)
  other arithmetic  5.13 us (1%)
    all_gather x1, waiting for transfers between devices, on_device(): lax.all_gather(qkv_weight, 'ctx', axis=0, tiled=True)  111 us
    all_to_all x1, waiting for transfers between devices, on_device(): lax.all_to_all(qkv, 'ctx', split_axis=2, concat_axis=1, tiled=True)  59.2 us
    all_gather x1, waiting for transfers between devices, on_device(): lax.all_gather(normed.reshape(1, -1, width_model), 'dp', axis=0, tiled=True)  56.9 us
    all_to_all x1, blocking collectives, attend(): return lax.all_to_all(out, 'ctx', split_axis=1, concat_axis=2, tiled=True)  28 us
    dot_general x27, matrix products, on_device(): jnp.dot(slab, conv_weight[lag, row, col], preferred_element_type=jnp.floa...  23.4 us
    all_to_all x1, blocking collectives, on_device(): mixed = lax.all_to_all(mixed, 'dp', split_axis=0, concat_axis=3, tiled=True)  16.2 us
    dot_general x1, matrix products, on_device(): jnp.dot(all_rows, lax.all_gather(qkv_weight, 'ctx', axis=0, tiled=True),...  14.7 us
    slice x2, local copies, waits for them, and re-layouts, on_device(): padded[2 - lag:2 - lag + f_dev, row:row + height, col:col + width, :]  13.8 us
  transfers between devices with their start and end apart: 4, of which 4 were waited for; matrix products, arithmetic and copies ran while one was open for 0% of the time, Pallas kernels for 0%

commit v1 on v0

v1 whole, which is shorter than its diff:
```python
import functools

import jax
import jax.numpy as jnp
from jax import lax
from jax.experimental import pallas as pl
from jax.experimental.pallas import tpu as pltpu
from jax.sharding import PartitionSpec as P

HD = 128
VMEM = pl.BlockSpec(memory_space=pltpu.VMEM)
HBM = pl.BlockSpec(memory_space=pltpu.HBM)
SMEM = pl.BlockSpec(memory_space=pltpu.SMEM)


def flip(value, axis, bit):
    count = lax.axis_size(axis)
    return lax.ppermute(value, axis, [(i, i ^ bit) for i in range(count)])


def ring_size(axis):
    count = lax.axis_size(axis)
    return count if count <= 8 and count % 2 == 0 else 0


def gather_ring(block, axis):
    count = ring_size(axis)
    if not count:
        return [lax.all_gather(block, axis, axis=0, tiled=True)]
    cycle = list(range(0, count, 2)) + list(range(count - 1, 0, -2))
    ahead = [(cycle[r], cycle[(r + 1) % count]) for r in range(count)]
    behind = [(b, a) for a, b in ahead]
    pieces = [block]
    up = down = block
    for _ in range(1, count // 2):
        up = lax.ppermute(up, axis, ahead)
        down = lax.ppermute(down, axis, behind)
        pieces += [up, down]
    half = block.shape[0] // 2
    pieces.append(lax.ppermute(up[:half], axis, ahead))
    pieces.append(lax.ppermute(down[half:], axis, behind))
    return pieces


def piece_rows(count, rows):
    if not count:
        return [0]
    me = lax.axis_index("ctx")
    place = jnp.where(lax.rem(me, 2) == 0, me // 2, count - 1 - me // 2)

    def owner(shift):
        spot = lax.rem(place + shift + count, count)
        return jnp.where(spot < count // 2, 2 * spot, 2 * (count - 1 - spot) + 1) * rows

    first = [me * rows]
    for step in range(1, count // 2):
        first += [owner(-step), owner(step)]
    far = owner(count // 2)
    return first + [far, far + rows // 2]


def conv_kernel(
    length_ref, past_ref, frames_ref, weight_ref, latent_weight_ref, section_ref, latent_ref,
    shifted, weights, near, lagged, sems,
):
    f_dev, height, width, channels = frames_ref.shape
    lags, side = past_ref.shape[0] + 1, 3
    taps = weight_ref.shape[0]
    cells = height * width

    def load(tap):
        return pltpu.make_async_copy(weight_ref.at[tap], weights.at[tap], sems.at[tap])

    for tap in range(taps):
        load(tap).start()
    column = lax.rem(lax.broadcasted_iota(jnp.int32, (cells, channels), 0), width)
    edge = jnp.zeros((width, channels), jnp.bfloat16)

    def prepare(source, slot):
        act = jax.nn.silu(source.astype(jnp.float32)).reshape(cells, channels)
        left = jnp.where(column == 0, 0.0, pltpu.roll(act, 1, 0))
        right = jnp.where(column == width - 1, 0.0, pltpu.roll(act, cells - 1, 0))
        for col, value in enumerate((left, act, right)):
            shifted[col, slot, 0] = edge
            shifted[col, slot, height + 1] = edge
            shifted[col, slot, 1 : height + 1] = value.astype(jnp.bfloat16).reshape(
                height, width, channels
            )

    @pl.loop(0, lags - 1)
    def _(slot):
        prepare(past_ref[slot], slot)

    @pl.loop(0, f_dev)
    def _(slot):
        prepare(frames_ref[slot], slot + lags - 1)

    def add(tap, total):
        load(tap).wait()
        lag, row, col = tap // (side * side), lax.rem(tap // side, side), lax.rem(tap, side)
        slab = shifted[col, pl.ds(lags - 1 - lag, f_dev), pl.ds(row, height)]
        total[...] += jnp.dot(
            slab.reshape(f_dev * cells, channels), weights[tap], preferred_element_type=jnp.float32
        )

    near[...] = jnp.zeros_like(near)
    lagged[...] = jnp.zeros_like(lagged)

    @pl.loop(0, side * side)
    def _(tap):
        add(tap, near)

    @pl.loop(side * side, taps)
    def _(tap):
        add(tap, lagged)

    first = lax.axis_index("ctx") * f_dev

    @pl.loop(0, f_dev)
    def _(slot):
        video = jnp.where(first + slot < length_ref[0], 1.0, 0.0)
        rows = pl.ds(pl.multiple_of(slot * cells, cells), cells)
        value = (
            frames_ref[slot].astype(jnp.float32).reshape(cells, channels)
            + near[rows]
            + video * lagged[rows]
        ).astype(jnp.bfloat16)
        section_ref[slot] = value.reshape(height, width, channels)
        latent_ref[rows] = jnp.dot(
            value, latent_weight_ref[...], preferred_element_type=jnp.float32
        ).astype(jnp.bfloat16)


def conv_section(frames, past, length, conv_weight, latent_weight):
    f_dev, height, width, channels = frames.shape
    lags = conv_weight.shape[0]
    taps = conv_weight.shape[0] * conv_weight.shape[1] * conv_weight.shape[2]
    cells = f_dev * height * width
    return pl.pallas_call(
        conv_kernel,
        out_shape=(
            jax.ShapeDtypeStruct(frames.shape, jnp.bfloat16),
            jax.ShapeDtypeStruct((cells, latent_weight.shape[1]), jnp.bfloat16),
        ),
        in_specs=[SMEM, VMEM, VMEM, HBM, VMEM],
        out_specs=(VMEM, VMEM),
        scratch_shapes=[
            pltpu.VMEM((3, f_dev + lags - 1, height + 2, width, channels), jnp.bfloat16),
            pltpu.VMEM((taps, channels, channels), jnp.bfloat16),
            pltpu.VMEM((cells, channels), jnp.float32),
            pltpu.VMEM((cells, channels), jnp.float32),
            pltpu.SemaphoreType.DMA((taps,)),
        ],
        compiler_params=pltpu.CompilerParams(vmem_limit_bytes=40 << 20),
        cost_estimate=pl.CostEstimate(
            flops=2 * cells * taps * channels * channels,
            bytes_accessed=2 * conv_weight.size,
            transcendentals=0,
        ),
        name="conv",
    )(length, past, frames, conv_weight.reshape(taps, channels, channels), latent_weight)


def norm_kernel(bounds, groups, patch_size, patches_ref, embed_ref, gain_ref, *refs):
    parts, (out_ref, held, embedded, sems) = refs[: len(bounds) * groups], refs[len(bounds) * groups :]
    me = lax.axis_index("dp")
    width = embed_ref.shape[1]
    n, f_dev, pos = held.shape[1:4]
    copies = []
    for c, (a, b) in enumerate(bounds):
        for j in range(groups):
            spot = c * groups + j
            copies.append(
                pltpu.make_async_copy(
                    parts[spot], held.at[lax.bitwise_xor(me, j), :, pl.ds(a, b - a)], sems.at[spot]
                )
            )
    for copy in copies:
        copy.start()
    tile = 256

    @pl.loop(0, width // tile)
    def _(i):
        columns = pl.ds(pl.multiple_of(i * tile, tile), tile)
        embedded[:, columns] = jnp.dot(
            patches_ref[:, :patch_size], embed_ref[:, columns], preferred_element_type=jnp.float32
        )

    for copy in copies:
        copy.wait()

    @pl.loop(0, groups * n)
    def _(i):
        group, device = i // n, lax.rem(i, n)

        @pl.loop(0, f_dev)
        def _(slot):
            rows = pl.ds(pl.multiple_of((i * f_dev + slot) * pos, pos), pos)
            value = embedded[rows] + held[group, device, slot].astype(jnp.float32)
            scale = lax.rsqrt(jnp.mean(value * value, axis=-1, keepdims=True) + 1e-06)
            out_ref[group, device, slot] = (value * scale * gain_ref[...]).astype(jnp.bfloat16)


def norm_rows(patches, embed_weight, norm_gain, parts, bounds, groups, n, f_dev, pos):
    width = embed_weight.shape[1]
    rows = groups * n * f_dev * pos
    if pos % 8:
        order = jnp.arange(groups, dtype=jnp.int32) ^ lax.axis_index("dp")
        chunks = [
            jnp.stack(parts[c * groups : (c + 1) * groups])[order] for c in range(len(bounds))
        ]
        held = jnp.concatenate(chunks, axis=2).reshape(rows, width)
        value = jnp.dot(
            patches[:, : embed_weight.shape[0]], embed_weight, preferred_element_type=jnp.float32
        ) + held.astype(jnp.float32)
        scale = lax.rsqrt(jnp.mean(value * value, axis=-1, keepdims=True) + 1e-06)
        return (value * scale * norm_gain).astype(jnp.bfloat16)
    return pl.pallas_call(
        functools.partial(norm_kernel, bounds, groups, embed_weight.shape[0]),
        out_shape=jax.ShapeDtypeStruct((groups, n, f_dev, pos, width), jnp.bfloat16),
        in_specs=[VMEM] * 3 + [HBM] * len(parts),
        out_specs=VMEM,
        scratch_shapes=[
            pltpu.VMEM((groups, n, f_dev, pos, width), jnp.bfloat16),
            pltpu.VMEM((rows, width), jnp.float32),
            pltpu.SemaphoreType.DMA((len(parts),)),
        ],
        compiler_params=pltpu.CompilerParams(vmem_limit_bytes=44 << 20),
        cost_estimate=pl.CostEstimate(
            flops=2 * rows * width * 512, bytes_accessed=4 * rows * width, transcendentals=0
        ),
        name="norm",
    )(patches, embed_weight, norm_gain[None], *parts)


def qkv_kernel(count, normed_ref, *refs):
    *pieces, out_ref, weight, sems = refs
    firsts = piece_rows(count, pieces[0].shape[0])
    copies = [
        pltpu.make_async_copy(
            piece, weight.at[pl.ds(pl.multiple_of(first, 64), piece.shape[0])], sems.at[i]
        )
        for i, (piece, first) in enumerate(zip(pieces, firsts))
    ]
    for copy in copies:
        copy.start()
    for copy in copies:
        copy.wait()
    rows = normed_ref.shape[0]
    tile = rows // 4 if rows % 64 == 0 else rows

    @pl.loop(0, rows // tile)
    def _(i):
        span = pl.ds(pl.multiple_of(i * tile, 16), tile)
        out_ref[span] = jnp.dot(
            normed_ref[span], weight[...], preferred_element_type=jnp.float32
        ).astype(jnp.bfloat16)


def project(normed, pieces, count):
    depth, columns = normed.shape[1], pieces[0].shape[1]
    return pl.pallas_call(
        functools.partial(qkv_kernel, count),
        out_shape=jax.ShapeDtypeStruct((normed.shape[0], columns), jnp.bfloat16),
        in_specs=[VMEM] + [HBM] * len(pieces),
        out_specs=VMEM,
        scratch_shapes=[
            pltpu.VMEM((depth, columns), jnp.bfloat16),
            pltpu.SemaphoreType.DMA((len(pieces),)),
        ],
        compiler_params=pltpu.CompilerParams(vmem_limit_bytes=32 << 20),
        cost_estimate=pl.CostEstimate(
            flops=2 * normed.size * columns,
            bytes_accessed=2 * (normed.size + depth * columns),
            transcendentals=0,
        ),
        name="qkv",
    )(normed, *pieces)


def attend(qkv, lengths):
    query, keys, values = (qkv[..., i * HD : (i + 1) * HD] for i in range(3))
    scores = jnp.einsum(
        "gtphd,gsphd->gphts", query, keys, preferred_element_type=jnp.float32
    ) * HD ** (-0.5)
    frame_ids = jnp.arange(qkv.shape[1], dtype=jnp.int32)
    video = frame_ids[None, :] < lengths[:, None]
    allowed = (
        video[:, :, None] & video[:, None, :] | (frame_ids[:, None] == frame_ids[None, :])[None]
    )
    scores = jnp.where(allowed[:, None, None], scores, -1e30)
    top = jnp.max(scores, axis=-1, keepdims=True)
    expo = jnp.exp(scores - top)
    probs = (expo / jnp.sum(expo, axis=-1, keepdims=True)).astype(jnp.bfloat16)
    return jnp.einsum(
        "gphts,gsphd->gtphd", probs, values, preferred_element_type=jnp.float32
    ).astype(jnp.bfloat16)


def body(
    frames, stream, video_frames, conv_weight, latent_weight, embed_weight, norm_gain, qkv_weight
):
    f_dev, height, width, _ = frames.shape[1:]
    tokens, width_model = stream.shape[2:]
    n, groups = lax.axis_size("ctx"), lax.axis_size("dp")
    pos = tokens // n
    heads = qkv_weight.shape[1] // (3 * HD)

    past = lax.ppermute(frames[0, f_dev - 2 :], "ctx", [(i, i + 1) for i in range(n - 1)])

    bounds = ((0, (f_dev + 1) // 2), ((f_dev + 1) // 2, f_dev))
    parts = []
    for first, end in bounds:
        blocks = stream[0, first:end].reshape(end - first, n, pos, width_model).transpose(1, 0, 2, 3)
        slots = {0: lax.all_to_all(blocks, "ctx", 0, 0)}
        bit = groups // 2
        while bit:
            for j in sorted(slots):
                slots[j ^ bit] = flip(slots[j], "dp", bit)
            bit //= 2
        parts += [slots[j] for j in range(groups)]

    pieces = gather_ring(qkv_weight, "ctx")

    section, latent = conv_section(frames[0], past, video_frames, conv_weight, latent_weight)
    lat = latent.shape[1]
    patches = (
        latent.reshape(f_dev, height // 2, 2, width // 2, 2, lat)
        .transpose(0, 1, 3, 2, 4, 5)
        .reshape(f_dev, n, pos, 4 * lat)
        .transpose(1, 0, 2, 3)
    )
    length = jnp.broadcast_to(video_frames.astype(jnp.bfloat16), (*patches.shape[:-1], 1))
    patches = jnp.concatenate([patches, length], axis=-1)
    patches = jnp.broadcast_to(patches[None], (groups, *patches.shape)).reshape(
        groups * n, f_dev, pos, -1
    )
    patches = lax.all_to_all(patches, ("dp", "ctx"), 0, 0, tiled=True)
    rows = groups * n * f_dev * pos
    patches = patches.reshape(rows, -1)
    lengths = patches[:: rows // groups, -1].astype(jnp.int32)

    normed = norm_rows(
        patches, embed_weight, norm_gain, parts, bounds, groups, n, f_dev, pos
    ).reshape(rows, width_model)
    qkv = project(normed, pieces, ring_size("ctx"))
    out = attend(qkv.reshape(groups, n * f_dev, pos, heads, 3 * HD), lengths)
    out = lax.all_to_all(
        out.reshape(groups * n, f_dev, pos, heads * HD), ("dp", "ctx"), 0, 0, tiled=True
    )
    out = out.reshape(groups, n, f_dev, pos, heads * HD).transpose(2, 1, 3, 0, 4)
    return section[None], out.reshape(1, f_dev, tokens, groups * heads * HD)


def solution(mesh):
    return jax.shard_map(
        body,
        mesh=mesh,
        in_specs=(
            P("dp", "ctx", None, None, None),
            P("dp", "ctx", None, None),
            P("dp"),
            P(),
            P(),
            P(),
            P(),
            P("ctx", "dp"),
        ),
        out_specs=(P("dp", "ctx", None, None, None), P("dp", "ctx", None, None)),
        check_vma=False,
    )
```

time: 402 us -> 253 us (0.63)
  waiting for transfers between devices: 238 us -> 86.8 us
  Pallas kernels: 0 us -> 68.6 us
  matrix products: 44 us -> 6.21 us
  starting transfers between devices: 8.78 us -> 40.2 us
  local copies, waits for them, and re-layouts: 41.1 us -> 20 us
  blocking collectives: 49.1 us -> 28.2 us
  between operations: 15.2 us -> 1.52 us
  other arithmetic: 5.13 us -> 0.29 us
    all_gather x2 -> x0, waiting for transfers between devices: 167 us -> none  [the longest x1 111 us: on_device(): lax.all_gather(qkv_weight, 'ctx', axis=0, tiled=True)]
    pallas_call x0 -> x3, Pallas kernels: none -> 68.6 us  [the longest x1 28 us: conv_section(): pl.pallas_call(conv_kernel, out_shape=(jax.ShapeDtypeStruct(frames.shape,...]
    dot_general x30 -> x0, matrix products: 39.3 us -> none  [the longest x27 23.4 us: on_device(): jnp.dot(slab, conv_weight[lag, row, col], preferred_element_type=jnp.floa...]
    ppermute x1 -> x15, waiting for transfers between devices: 10.3 us -> 48.6 us  [the longest x3 28.5 us: gather_ring(): up = lax.ppermute(up, axis, ahead)]
    all_to_all x1 -> x3, waiting for transfers between devices: 59.2 us -> 38.2 us  [the longest x2 26.5 us: body(): slots = {0: lax.all_to_all(blocks, 'ctx', 0, 0)}]
    ppermute x1 -> x15, starting transfers between devices: 4.93 us -> 24.8 us  [the longest x3 12.5 us: gather_ring(): up = lax.ppermute(up, axis, ahead)]
    all_to_all x2 -> x1, blocking collectives: 44.2 us -> 28.2 us  [body(): lax.all_to_all(out.reshape(groups * n, f_dev, pos, heads * HD), ('dp', 'c...]
    all_to_all x1 -> x3, starting transfers between devices: 3.77 us -> 15.4 us  [the longest x2 10.9 us: body(): slots = {0: lax.all_to_all(blocks, 'ctx', 0, 0)}]
  transfers between devices with their start and end apart: 4 -> 18, of which waited for: 4 -> 4; matrix products, arithmetic and copies ran while one was open for 0% -> 4% of each run, Pallas kernels for 0% -> 22%
where the time goes in v1:
time: 253 us; the launch traced here: 252 us
  waiting for transfers between devices  86.8 us (34%)
  Pallas kernels  68.6 us (27%)
  starting transfers between devices  40.2 us (16%)
  blocking collectives  28.2 us (11%)
  local copies, waits for them, and re-layouts  20 us (8%)
  matrix products  6.21 us (2%)
    ppermute x3, waiting for transfers between devices, gather_ring(): up = lax.ppermute(up, axis, ahead)  28.5 us
    all_to_all x1, blocking collectives, body(): lax.all_to_all(out.reshape(groups * n, f_dev, pos, heads * HD), ('dp', 'c...  28.2 us
    pallas_call x1, Pallas kernels, conv_section(): pl.pallas_call(conv_kernel, out_shape=(jax.ShapeDtypeStruct(frames.shape,...  28 us
    pallas_call x1, Pallas kernels, norm_rows(): pl.pallas_call(functools.partial(norm_kernel, bounds, groups, embed_weigh...  26.9 us
    all_to_all x2, waiting for transfers between devices, body(): slots = {0: lax.all_to_all(blocks, 'ctx', 0, 0)}  26.5 us
    ppermute x1, waiting for transfers between devices, body(): lax.ppermute(frames[0, f_dev - 2:], 'ctx', [(i, i + 1) for i in range(n -...  20.1 us
    pallas_call x1, Pallas kernels, project(): pl.pallas_call(functools.partial(qkv_kernel, count), out_shape=jax.ShapeD...  13.6 us
    ppermute x3, starting transfers between devices, gather_ring(): up = lax.ppermute(up, axis, ahead)  12.5 us
  transfers between devices with their start and end apart: 18, of which 4 were waited for; matrix products, arithmetic and copies ran while one was open for 4% of the time, Pallas kernels for 22%

profile of v1, /device:TPU:0, one launch (start us, length us, event | category | flops | bytes accessed | tf_op | source)
XLA Modules:
  0.0 251.8 jit_solution(16017998202303275746)
XLA Ops:
  0.6 2.4 copy_bitcast_fusion
  3.0 7.3 %all-to-all-start.1 = ((bf16[8,3,8,3072]{3,2,1,0:T(8,128)(2,1)}), bf16[8,3,8,3072]{3,2,1,0:T(8,128)(2,1)S(1)}, u32[]{:S(2)}, u32[]{:S(2)}) async-start(bf16[8,3,8,3072]{3,2,1,0:T(8,128)(2,1)} %copy_bitcast_fusion), calls=%async_computation.1 | async-start | bytes 2359296 | tf_op jit(solution)/shard_map/all_to_all | solution.py:315
  10.3 2.1 copy_bitcast_fusion.1
  12.4 26.5 %all-to-all-done.1.refs_0_ = bf16[8,3,8,3072]{3,2,1,0:T(8,128)(2,1)S(1)} async-done(((bf16[8,3,8,3072]{3,2,1,0:T(8,128)(2,1)}), bf16[8,3,8,3072]{3,2,1,0:T(8,128)(2,1)S(1)}, u32[]{:S(2)}, u32[]{:S(2)}) %all-to-all-start.1) | async-done | bytes 1179680 | tf_op jit(solution)/shard_map/all_to_all | solution.py:315
  38.9 3.6 %all-to-all-start.2 = ((bf16[8,2,8,3072]{3,2,1,0:T(8,128)(2,1)}), bf16[8,2,8,3072]{3,2,1,0:T(8,128)(2,1)S(1)}, u32[]{:S(2)}, u32[]{:S(2)}) async-start(bf16[8,2,8,3072]{3,2,1,0:T(8,128)(2,1)} %copy_bitcast_fusion.1), calls=%async_computation.2 | async-start | bytes 1572864 | tf_op jit(solution)/shard_map/all_to_all | solution.py:315
  42.5 2.0 collective-permute-start.7
  44.5 0.0 collective-permute-start.8
  44.6 1.5 collective-permute-start.2
  46.0 28.5 %collective-permute-done.7.refs_1_ = bf16[384,1152]{1,0:T(8,128)(2,1)} collective-permute-done((bf16[384,1152]{1,0:T(8,128)(2,1)}, bf16[384,1152]{1,0:T(8,128)(2,1)}, u32[]{:S(2)}, u32[]{:S(2)}) %collective-permute-start.7) | collective-permute-done | bytes 884768 | tf_op jit(solution)/shard_map/ppermute | solution.py:36
  74.6 5.7 %collective-permute-start.9 = (bf16[384,1152]{1,0:T(8,128)(2,1)}, bf16[384,1152]{1,0:T(8,128)(2,1)}, u32[]{:S(2)}, u32[]{:S(2)}) collective-permute-start(bf16[384,1152]{1,0:T(8,128)(2,1)} %collective-permute-done.7.refs_1_), channel_id=1, source_target_pairs={{0,2},{2,4},{4,6},{6,7},{7,5},{5,3},{3,1},{1,0},{8,10},{10,12},{12... | collective-permute-start | bytes 2654216 | tf_op jit(solution)/shard_map/ppermute | solution.py:36
  80.3 0.0 collective-permute-done.8.refs_2_
  80.3 0.0 collective-permute-start.10
  80.3 0.0 all-to-all-done.2.refs_4_
  80.3 1.6 collective-permute-start.5
  81.8 1.9 slice_bitcast_fusion.2
  83.7 6.3 %collective-permute-start = (bf16[2,16,16,512]{3,2,1,0:T(8,128)(2,1)}, bf16[2,16,16,512]{3,2,1,0:T(8,128)(2,1)}, u32[]{:S(2)}, u32[]{:S(2)}) collective-permute-start(bf16[2,16,16,512]{3,2,1,0:T(8,128)(2,1)} %slice_bitcast_fusion.2), channel_id=1, source_target_pairs={{0,1},{1,2},{2,3},{3,4},{4,5},{5,6},{6,7},{8,9},{9,10},{10,11},{11... | collective-permute-start | bytes 1572872 | tf_op jit(solution)/shard_map/ppermute | solution.py:309
  90.6 0.0 copy-done.5
  90.6 0.1 copy.25.latent_weight_ref
  90.8 20.1 %collective-permute-done.past_ref = bf16[2,16,16,512]{3,2,1,0:T(8,128)(2,1)} collective-permute-done((bf16[2,16,16,512]{3,2,1,0:T(8,128)(2,1)}, bf16[2,16,16,512]{3,2,1,0:T(8,128)(2,1)}, u32[]{:S(2)}, u32[]{:S(2)}) %collective-permute-start) | collective-permute-done | bytes 524320 | tf_op jit(solution)/shard_map/ppermute | solution.py:309
  110.8 0.0 collective-permute-start.4
  110.8 0.0 collective-permute-done.9.refs_3_
  110.9 4.7 %collective-permute-start.11 = (bf16[384,1152]{1,0:T(8,128)(2,1)}, bf16[384,1152]{1,0:T(8,128)(2,1)}, u32[]{:S(2)}, u32[]{:S(2)}) collective-permute-start(bf16[384,1152]{1,0:T(8,128)(2,1)} %collective-permute-done.9.refs_3_), channel_id=1, source_target_pairs={{0,2},{2,4},{4,6},{6,7},{7,5},{5,3},{3,1},{1,0},{8,10},{10,12},{12... | collective-permute-start | bytes 2654216 | tf_op jit(solution)/shard_map/ppermute | solution.py:36
  115.6 0.0 collective-permute-done.10.refs_4_
  115.6 0.0 collective-permute-start.12
  115.6 0.0 collective-permute-done.5.refs_6_
  115.6 0.3 collective-permute-start.1
  115.9 0.0 collective-permute-done.2.refs_2_
  115.9 0.3 collective-permute-start.3
  116.2 1.3 copy-done.2
  117.5 28.0 %conv.1 = (bf16[5,16,16,512]{3,2,1,0:T(8,128)(2,1)}, bf16[1280,16]{1,0:T(8,128)(2,1)S(1)}) custom-call(s32[1]{0:T(128)S(6)} %copy.67.length_ref, bf16[2,16,16,512]{3,2,1,0:T(8,128)(2,1)} %collective-permute-done.past_ref, bf16[5,16,16,512]{3,2,1,0:T(8,128)(2,1)S(1)} %bitcast.37, bf16[27,512,512]{2,1,0:T(8,128)(2,1)} %bitcast.44, ...), custom_call_target="tpu_custom_call" | custom-call | flops 18119393280 | bytes 14155776 | tf_op jit(solution)/shard_map/conv/pallas_call | solution.py:139
  145.5 0.2 copy.66
  145.7 0.0 copy-start.3
  145.7 0.8 reshape.95
  146.6 0.9 copy.40
  147.5 0.8 broadcast_in_dim.15
  148.3 4.4 %all-to-all-start = ((bf16[32,5,8,65]{3,2,1,0:T(8,128)(2,1)}), bf16[32,5,8,65]{3,2,1,0:T(8,128)(2,1)S(1)}, u32[]{:S(2)}, u32[]{:S(2)}) async-start(bf16[32,5,8,65]{3,2,1,0:T(8,128)(2,1)} %bitcast.41), calls=%async_computation | async-start | bytes 655360 | tf_op jit(solution)/shard_map/all_to_all | solution.py:338
  152.7 0.0 collective-permute-done.11.refs_5_
  152.7 0.3 collective-permute-start.6
  153.0 11.7 %all-to-all-done = bf16[32,5,8,65]{3,2,1,0:T(8,128)(2,1)S(1)} async-done(((bf16[32,5,8,65]{3,2,1,0:T(8,128)(2,1)}), bf16[32,5,8,65]{3,2,1,0:T(8,128)(2,1)S(1)}, u32[]{:S(2)}, u32[]{:S(2)}) %all-to-all-start) | async-done | bytes 166432 | tf_op jit(solution)/shard_map/all_to_all | solution.py:338
  164.7 0.1 slice.33
  164.8 0.1 convert_reduce_fusion
  165.0 0.1 iota_compare_fusion.1
  165.0 1.1 slice.36
  166.1 0.0 collective-permute-done.12.refs_6_
  166.1 1.0 collective-permute-start.13
  167.1 1.0 slice.37
  168.1 0.0 collective-permute-done.4.refs_5_
  168.1 1.2 collective-permute-start.14
  169.3 0.1 and_or_fusion
  169.4 0.0 collective-permute-done.6.refs_7_
  169.4 0.0 collective-permute-done.1.refs_1_
  169.4 0.0 collective-permute-done.3.refs_3_
  169.4 26.9 %norm.1 = bf16[4,8,5,8,3072]{4,3,2,1,0:T(8,128)(2,1)} custom-call(bf16[1280,65]{1,0:T(8,128)(2,1)S(1)} %bitcast.35, bf16[64,3072]{1,0:T(8,128)(2,1)S(1)} %copy-done.1, f32[1,3072]{1,0:T(1,128)S(1)} %bitcast.38, bf16[8,3,8,3072]{3,2,1,0:T(8,128)(2,1)S(1)} %all-to-all-done.1.refs_0_, bf16[8,3,8,3072]{3,2,1,0:T(8,128)(2,1)} %collective-permute-done.1.refs_1_, ...), custom_call_target="tpu_custom_call" | custom-call | flops 4026531840 | bytes 15728640 | tf_op jit(solution)/shard_map/norm/pallas_call | solution.py:218
  196.4 0.0 collective-permute-done.13.refs_7_
  196.4 0.0 collective-permute-done.14.refs_8_
  196.4 3.2 %copy-done = bf16[4,8,5,8,3072]{4,3,2,1,0:T(8,128)(2,1)S(1)} copy-done((bf16[4,8,5,8,3072]{4,3,2,1,0:T(8,128)(2,1)S(1)}, bf16[4,8,5,8,3072]{4,3,2,1,0:T(8,128)(2,1)}, u32[]{:S(2)}) %copy-start) | copy-done | bytes 7864344
  199.6 13.6 %qkv.1 = bf16[1280,1152]{1,0:T(8,128)(2,1)S(1)} custom-call(bf16[1280,3072]{1,0:T(8,128)(2,1)S(1)} %bitcast.32, bf16[384,1152]{1,0:T(8,128)(2,1)} %refs_0_.1, bf16[384,1152]{1,0:T(8,128)(2,1)} %collective-permute-done.7.refs_1_, bf16[384,1152]{1,0:T(8,128)(2,1)} %collective-permute-done.8.refs_2_, bf16[384,1152]{1,0:T(8,128)(2,1)} %collective-permute-done.9.refs_3_, ...), custom_call_target="tpu_custom_call" | custom-call | flops 9059696640 | bytes 14942208 | tf_op jit(solution)/shard_map/qkv/pallas_call | solution.py:262
  213.3 1.8 fusion.25
  215.1 3.9 %fusion.26 = (f32[4,8,3,40]{3,2,1,0:T(4,128)S(1)}, f32[4,8,3,40,40]{3,4,2,1,0:T(8,128)}) fusion(pred[4,40,40]{1,2,0:T(8,128)(4,1)S(1)} %and_or_fusion, bf16[4,40,8,3,128]{4,2,3,1,0:T(8,128)(2,1)} %get-tuple-element.8, bf16[4,40,8,3,128]{4,2,3,1,0:T(8,128)(2,1)} %get-tuple-element.7), kind=kOutput, calls=%fused_computation.28 | convolution fusion | flops 39936040 | bytes 2602240 | tf_op jit(solution)/shard_map/sub | solution.py:293
  219.1 2.3 fusion.2
  221.3 0.1 copy.34
  221.5 28.2 %all_to_all.20 = bf16[32,5,8,384]{3,2,1,0:T(8,128)(2,1)S(1)} all-to-all(bf16[32,5,8,384]{3,2,1,0:T(8,128)(2,1)S(1)} %bitcast.39), channel_id=1, replica_groups=mesh['dp'=4,'ctx'=8] {'dp','ctx'}, dimensions={0} | all-to-all | bytes 1966080 | tf_op jit(solution)/shard_map/all_to_all | solution.py:348
  249.7 0.8 copy.35
  250.5 1.3 reshape.102
  (10 shorter events, 0.0 us)
Async XLA Ops:
  3.0 35.9 %all-to-all-start.1 = ((bf16[8,3,8,3072]{3,2,1,0:T(8,128)(2,1)}), bf16[8,3,8,3072]{3,2,1,0:T(8,128)(2,1)S(1)}, u32[]{:S(2)}, u32[]{:S(2)}) async-start(bf16[8,3,8,3072]{3,2,1,0:T(8,128)(2,1)} %copy_bitcast_fusion), calls=%async_computation.1 | async-start | bytes 2359296 | tf_op jit(solution)/shard_map/all_to_all | solution.py:315
  10.3 80.3 %copy-start.5 = (bf16[512,16]{0,1:T(8,128)(2,1)S(1)}, bf16[512,16]{0,1:T(8,128)(2,1)}, u32[]{:S(2)}) copy-start(bf16[512,16]{0,1:T(8,128)(2,1)} %param.12) | copy-start | bytes 49156
  38.9 41.4 %all-to-all-start.2 = ((bf16[8,2,8,3072]{3,2,1,0:T(8,128)(2,1)}), bf16[8,2,8,3072]{3,2,1,0:T(8,128)(2,1)S(1)}, u32[]{:S(2)}, u32[]{:S(2)}) async-start(bf16[8,2,8,3072]{3,2,1,0:T(8,128)(2,1)} %copy_bitcast_fusion.1), calls=%async_computation.2 | async-start | bytes 1572864 | tf_op jit(solution)/shard_map/all_to_all | solution.py:315
  42.5 32.0 %collective-permute-start.7 = (bf16[384,1152]{1,0:T(8,128)(2,1)}, bf16[384,1152]{1,0:T(8,128)(2,1)}, u32[]{:S(2)}, u32[]{:S(2)}) collective-permute-start(bf16[384,1152]{1,0:T(8,128)(2,1)} %refs_0_.1), channel_id=1, source_target_pairs={{0,2},{2,4},{4,6},{6,7},{7,5},{5,3},{3,1},{1,0},{8,10},{10,12},{12... | collective-permute-start | bytes 2654216 | tf_op jit(solution)/shard_map/ppermute | solution.py:36
  44.5 35.7 %collective-permute-start.8 = (bf16[384,1152]{1,0:T(8,128)(2,1)}, bf16[384,1152]{1,0:T(8,128)(2,1)}, u32[]{:S(2)}, u32[]{:S(2)}) collective-permute-start(bf16[384,1152]{1,0:T(8,128)(2,1)} %refs_0_.1), channel_id=1, source_target_pairs={{2,0},{4,2},{6,4},{7,6},{5,7},{3,5},{1,3},{0,1},{10,8},{12,10},{14... | collective-permute-start | bytes 2654216 | tf_op jit(solution)/shard_map/ppermute | solution.py:37
  44.6 71.3 %collective-permute-start.2 = (bf16[8,3,8,3072]{3,2,1,0:T(8,128)(2,1)S(1)}, bf16[8,3,8,3072]{3,2,1,0:T(8,128)(2,1)S(1)}, u32[]{:S(2)}, u32[]{:S(2)}) collective-permute-start(bf16[8,3,8,3072]{3,2,1,0:T(8,128)(2,1)S(1)} %all-to-all-done.1.refs_0_), channel_id=1, source_target_pairs={{0,16},{8,24},{16,0},{24,8},{1,17},{9,25},{17,1},{25,9},{2,18},{10... | collective-permute-start | bytes 3538952 | tf_op jit(solution)/shard_map/ppermute | solution.py:18
  74.6 36.3 %collective-permute-start.9 = (bf16[384,1152]{1,0:T(8,128)(2,1)}, bf16[384,1152]{1,0:T(8,128)(2,1)}, u32[]{:S(2)}, u32[]{:S(2)}) collective-permute-start(bf16[384,1152]{1,0:T(8,128)(2,1)} %collective-permute-done.7.refs_1_), channel_id=1, source_target_pairs={{0,2},{2,4},{4,6},{6,7},{7,5},{5,3},{3,1},{1,0},{8,10},{10,12},{12... | collective-permute-start | bytes 2654216 | tf_op jit(solution)/shard_map/ppermute | solution.py:36
  80.3 35.3 %collective-permute-start.10 = (bf16[384,1152]{1,0:T(8,128)(2,1)}, bf16[384,1152]{1,0:T(8,128)(2,1)}, u32[]{:S(2)}, u32[]{:S(2)}) collective-permute-start(bf16[384,1152]{1,0:T(8,128)(2,1)} %collective-permute-done.8.refs_2_), channel_id=1, source_target_pairs={{2,0},{4,2},{6,4},{7,6},{5,7},{3,5},{1,3},{0,1},{10,8},{12,10},{14... | collective-permute-start | bytes 2654216 | tf_op jit(solution)/shard_map/ppermute | solution.py:37
  80.3 35.3 %collective-permute-start.5 = (bf16[8,2,8,3072]{3,2,1,0:T(8,128)(2,1)S(1)}, bf16[8,2,8,3072]{3,2,1,0:T(8,128)(2,1)}, u32[]{:S(2)}, u32[]{:S(2)}) collective-permute-start(bf16[8,2,8,3072]{3,2,1,0:T(8,128)(2,1)S(1)} %all-to-all-done.2.refs_4_), channel_id=1, source_target_pairs={{0,16},{8,24},{16,0},{24,8},{1,17},{9,25},{17,1},{25,9},{2,18},{10... | collective-permute-start | bytes 2359304 | tf_op jit(solution)/shard_map/ppermute | solution.py:18
  83.7 27.1 %collective-permute-start = (bf16[2,16,16,512]{3,2,1,0:T(8,128)(2,1)}, bf16[2,16,16,512]{3,2,1,0:T(8,128)(2,1)}, u32[]{:S(2)}, u32[]{:S(2)}) collective-permute-start(bf16[2,16,16,512]{3,2,1,0:T(8,128)(2,1)} %slice_bitcast_fusion.2), channel_id=1, source_target_pairs={{0,1},{1,2},{2,3},{3,4},{4,5},{5,6},{6,7},{8,9},{9,10},{10,11},{11... | collective-permute-start | bytes 1572872 | tf_op jit(solution)/shard_map/ppermute | solution.py:309
  110.8 57.3 %collective-permute-start.4 = (bf16[8,2,8,3072]{3,2,1,0:T(8,128)(2,1)S(1)}, bf16[8,2,8,3072]{3,2,1,0:T(8,128)(2,1)}, u32[]{:S(2)}, u32[]{:S(2)}) collective-permute-start(bf16[8,2,8,3072]{3,2,1,0:T(8,128)(2,1)S(1)} %all-to-all-done.2.refs_4_), channel_id=1, source_target_pairs={{0,8},{8,0},{16,24},{24,16},{1,9},{9,1},{17,25},{25,17},{2,10},{10... | collective-permute-start | bytes 2359304 | tf_op jit(solution)/shard_map/ppermute | solution.py:18
  110.9 41.9 %collective-permute-start.11 = (bf16[384,1152]{1,0:T(8,128)(2,1)}, bf16[384,1152]{1,0:T(8,128)(2,1)}, u32[]{:S(2)}, u32[]{:S(2)}) collective-permute-start(bf16[384,1152]{1,0:T(8,128)(2,1)} %collective-permute-done.9.refs_3_), channel_id=1, source_target_pairs={{0,2},{2,4},{4,6},{6,7},{7,5},{5,3},{3,1},{1,0},{8,10},{10,12},{12... | collective-permute-start | bytes 2654216 | tf_op jit(solution)/shard_map/ppermute | solution.py:36
  115.6 50.5 %collective-permute-start.12 = (bf16[384,1152]{1,0:T(8,128)(2,1)}, bf16[384,1152]{1,0:T(8,128)(2,1)}, u32[]{:S(2)}, u32[]{:S(2)}) collective-permute-start(bf16[384,1152]{1,0:T(8,128)(2,1)} %collective-permute-done.10.refs_4_), channel_id=1, source_target_pairs={{2,0},{4,2},{6,4},{7,6},{5,7},{3,5},{1,3},{0,1},{10,8},{12,10},{14... | collective-permute-start | bytes 2654216 | tf_op jit(solution)/shard_map/ppermute | solution.py:37
  115.6 53.8 %collective-permute-start.1 = (bf16[8,3,8,3072]{3,2,1,0:T(8,128)(2,1)S(1)}, bf16[8,3,8,3072]{3,2,1,0:T(8,128)(2,1)}, u32[]{:S(2)}, u32[]{:S(2)}) collective-permute-start(bf16[8,3,8,3072]{3,2,1,0:T(8,128)(2,1)S(1)} %all-to-all-done.1.refs_0_), channel_id=1, source_target_pairs={{0,8},{8,0},{16,24},{24,16},{1,9},{9,1},{17,25},{25,17},{2,10},{10... | collective-permute-start | bytes 3538952 | tf_op jit(solution)/shard_map/ppermute | solution.py:18
  115.9 53.5 %collective-permute-start.3 = (bf16[8,3,8,3072]{3,2,1,0:T(8,128)(2,1)S(1)}, bf16[8,3,8,3072]{3,2,1,0:T(8,128)(2,1)}, u32[]{:S(2)}, u32[]{:S(2)}) collective-permute-start(bf16[8,3,8,3072]{3,2,1,0:T(8,128)(2,1)S(1)} %collective-permute-done.2.refs_2_), channel_id=1, source_target_pairs={{0,8},{8,0},{16,24},{24,16},{1,9},{9,1},{17,25},{25,17},{2,10},{10... | collective-permute-start | bytes 3538952 | tf_op jit(solution)/shard_map/ppermute | solution.py:18
  116.2 1.3 copy-start.2
  145.7 23.7 %copy-start.3 = (f32[3072]{0:T(1024)S(1)}, f32[3072]{0:T(1024)}, u32[]{:S(2)}) copy-start(f32[3072]{0:T(1024)} %param.14) | copy-start | bytes 36868
  148.3 16.4 %all-to-all-start = ((bf16[32,5,8,65]{3,2,1,0:T(8,128)(2,1)}), bf16[32,5,8,65]{3,2,1,0:T(8,128)(2,1)S(1)}, u32[]{:S(2)}, u32[]{:S(2)}) async-start(bf16[32,5,8,65]{3,2,1,0:T(8,128)(2,1)} %bitcast.41), calls=%async_computation | async-start | bytes 655360 | tf_op jit(solution)/shard_map/all_to_all | solution.py:338
  152.7 16.7 %collective-permute-start.6 = (bf16[8,2,8,3072]{3,2,1,0:T(8,128)(2,1)}, bf16[8,2,8,3072]{3,2,1,0:T(8,128)(2,1)}, u32[]{:S(2)}, u32[]{:S(2)}) collective-permute-start(bf16[8,2,8,3072]{3,2,1,0:T(8,128)(2,1)} %collective-permute-done.5.refs_6_), channel_id=1, source_target_pairs={{0,8},{8,0},{16,24},{24,16},{1,9},{9,1},{17,25},{25,17},{2,10},{10... | collective-permute-start | bytes 2359304 | tf_op jit(solution)/shard_map/ppermute | solution.py:18
  164.8 4.6 %copy-start.1 = (bf16[64,3072]{1,0:T(8,128)(2,1)S(1)}, bf16[64,3072]{1,0:T(8,128)(2,1)}, u32[]{:S(2)}) copy-start(bf16[64,3072]{1,0:T(8,128)(2,1)} %embed_ref.1) | copy-start | bytes 1179652
  166.1 30.3 %collective-permute-start.13 = (bf16[192,1152]{1,0:T(8,128)(2,1)S(1)}, bf16[192,1152]{1,0:T(8,128)(2,1)S(1)}, u32[]{:S(2)}, u32[]{:S(2)}) collective-permute-start(bf16[192,1152]{1,0:T(8,128)(2,1)S(1)} %slice.36), channel_id=1, source_target_pairs={{0,2},{2,4},{4,6},{6,7},{7,5},{5,3},{3,1},{1,0},{8,10},{10,12},{12... | collective-permute-start | bytes 1327112 | tf_op jit(solution)/shard_map/ppermute | solution.py:40
  168.1 28.3 %collective-permute-start.14 = (bf16[192,1152]{1,0:T(8,128)(2,1)S(1)}, bf16[192,1152]{1,0:T(8,128)(2,1)S(1)}, u32[]{:S(2)}, u32[]{:S(2)}) collective-permute-start(bf16[192,1152]{1,0:T(8,128)(2,1)S(1)} %slice.37), channel_id=1, source_target_pairs={{2,0},{4,2},{6,4},{7,6},{5,7},{3,5},{1,3},{0,1},{10,8},{12,10},{14... | collective-permute-start | bytes 1327112 | tf_op jit(solution)/shard_map/ppermute | solution.py:41
  196.4 3.2 %copy-start = (bf16[4,8,5,8,3072]{4,3,2,1,0:T(8,128)(2,1)S(1)}, bf16[4,8,5,8,3072]{4,3,2,1,0:T(8,128)(2,1)}, u32[]{:S(2)}) copy-start(bf16[4,8,5,8,3072]{4,3,2,1,0:T(8,128)(2,1)} %norm.1) | copy-start | bytes 23592964
  215.1 3.9 %copy-start.4 = (bf16[4,40,8,3,128]{4,2,3,1,0:T(8,128)(2,1)S(1)}, bf16[4,40,8,3,128]{4,2,3,1,0:T(8,128)(2,1)}, u32[]{:S(2)}) copy-start(bf16[4,40,8,3,128]{4,2,3,1,0:T(8,128)(2,1)} %get-tuple-element.6) | copy-start | bytes 2949124

commit v2 on v1

--- a/solution.py
+++ b/solution.py
@@ -161,20 +161,15 @@
     )(length, past, frames, conv_weight.reshape(taps, channels, channels), latent_weight)
 
 
-def norm_kernel(bounds, groups, patch_size, patches_ref, embed_ref, gain_ref, *refs):
-    parts, (out_ref, held, embedded, sems) = refs[: len(bounds) * groups], refs[len(bounds) * groups :]
+def norm_kernel(groups, patch_size, patches_ref, embed_ref, gain_ref, *refs):
+    parts, (out_ref, held, embedded, sems) = refs[:groups], refs[groups:]
     me = lax.axis_index("dp")
     width = embed_ref.shape[1]
     n, f_dev, pos = held.shape[1:4]
-    copies = []
-    for c, (a, b) in enumerate(bounds):
-        for j in range(groups):
-            spot = c * groups + j
-            copies.append(
-                pltpu.make_async_copy(
-                    parts[spot], held.at[lax.bitwise_xor(me, j), :, pl.ds(a, b - a)], sems.at[spot]
-                )
-            )
+    copies = [
+        pltpu.make_async_copy(parts[j], held.at[lax.bitwise_xor(me, j)], sems.at[j])
+        for j in range(groups)
+    ]
     for copy in copies:
         copy.start()
     tile = 256
@@ -188,60 +183,66 @@
 
     for copy in copies:
         copy.wait()
+    block = f_dev * pos
 
     @pl.loop(0, groups * n)
     def _(i):
         group, device = i // n, lax.rem(i, n)
-
-        @pl.loop(0, f_dev)
-        def _(slot):
-            rows = pl.ds(pl.multiple_of((i * f_dev + slot) * pos, pos), pos)
-            value = embedded[rows] + held[group, device, slot].astype(jnp.float32)
-            scale = lax.rsqrt(jnp.mean(value * value, axis=-1, keepdims=True) + 1e-06)
-            out_ref[group, device, slot] = (value * scale * gain_ref[...]).astype(jnp.bfloat16)
-
-
-def norm_rows(patches, embed_weight, norm_gain, parts, bounds, groups, n, f_dev, pos):
-    width = embed_weight.shape[1]
+        rows = pl.ds(pl.multiple_of(i * block, pos), block)
+        stream = held[group, device].astype(jnp.float32).reshape(block, width)
+        value = embedded[rows] + stream
+        scale = lax.rsqrt(jnp.mean(value * value, axis=-1, keepdims=True) + 1e-06)
+        value = value * scale * gain_ref[...]
+        out_ref[group, device] = value.reshape(f_dev, pos, width).astype(jnp.bfloat16)
+
+
+def norm_rows(patches, embed_weight, norm_gain, parts):
+    groups, (n, f_dev, pos, width) = len(parts), parts[0].shape
     rows = groups * n * f_dev * pos
     if pos % 8:
         order = jnp.arange(groups, dtype=jnp.int32) ^ lax.axis_index("dp")
-        chunks = [
-            jnp.stack(parts[c * groups : (c + 1) * groups])[order] for c in range(len(bounds))
-        ]
-        held = jnp.concatenate(chunks, axis=2).reshape(rows, width)
+        held = jnp.stack(parts)[order].reshape(rows, width)
         value = jnp.dot(
             patches[:, : embed_weight.shape[0]], embed_weight, preferred_element_type=jnp.float32
         ) + held.astype(jnp.float32)
         scale = lax.rsqrt(jnp.mean(value * value, axis=-1, keepdims=True) + 1e-06)
         return (value * scale * norm_gain).astype(jnp.bfloat16)
     return pl.pallas_call(
-        functools.partial(norm_kernel, bounds, groups, embed_weight.shape[0]),
+        functools.partial(norm_kernel, groups, embed_weight.shape[0]),
         out_shape=jax.ShapeDtypeStruct((groups, n, f_dev, pos, width), jnp.bfloat16),
-        in_specs=[VMEM] * 3 + [HBM] * len(parts),
+        in_specs=[VMEM] * 3 + [HBM] * groups,
         out_specs=VMEM,
         scratch_shapes=[
             pltpu.VMEM((groups, n, f_dev, pos, width), jnp.bfloat16),
             pltpu.VMEM((rows, width), jnp.float32),
-            pltpu.SemaphoreType.DMA((len(parts),)),
+            pltpu.SemaphoreType.DMA((groups,)),
         ],
         compiler_params=pltpu.CompilerParams(vmem_limit_bytes=44 << 20),
         cost_estimate=pl.CostEstimate(
             flops=2 * rows * width * 512, bytes_accessed=4 * rows * width, transcendentals=0
         ),
         name="norm",
-    )(patches, embed_weight, norm_gain[None], *parts)
-
-
-def qkv_kernel(count, normed_ref, *refs):
-    *pieces, out_ref, weight, sems = refs
-    firsts = piece_rows(count, pieces[0].shape[0])
-    copies = [
-        pltpu.make_async_copy(
-            piece, weight.at[pl.ds(pl.multiple_of(first, 64), piece.shape[0])], sems.at[i]
-        )
-        for i, (piece, first) in enumerate(zip(pieces, firsts))
-    ]
+    )(patches, embed_weight, norm_gain[None], *parts).reshape(rows, width)
+
+
+def qkv_kernel(count, spots, has_total, normed_ref, *refs):
+    refs = list(refs)
+    total_ref = refs.pop(0) if has_total else None
+    sems, weight, out_ref = refs.pop(), refs.pop(), refs.pop()
+    depth = weight.shape[1]
+    firsts = piece_rows(count, depth)
+    copies, used = [], 0
+    for i, pieces in enumerate(spots):
+        row = 0
+        for _ in pieces:
+            piece = refs[used]
+            copies.append(
+                pltpu.make_async_copy(
+                    piece, weight.at[i, pl.ds(row, piece.shape[0])], sems.at[used]
+                )
+            )
+            row += piece.shape[0]
+            used += 1
     for copy in copies:
         copy.start()
     for copy in copies:
@@ -252,30 +253,55 @@
     @pl.loop(0, rows // tile)
     def _(i):
         span = pl.ds(pl.multiple_of(i * tile, 16), tile)
-        out_ref[span] = jnp.dot(
-            normed_ref[span], weight[...], preferred_element_type=jnp.float32
-        ).astype(jnp.bfloat16)
-
-
-def project(normed, pieces, count):
-    depth, columns = normed.shape[1], pieces[0].shape[1]
+        total = total_ref[span] if has_total else None
+        for j, pieces in enumerate(spots):
+            first = firsts[pieces[0]]
+            if count:
+                first = pl.multiple_of(first, 128)
+            product = jnp.dot(
+                normed_ref[span, pl.ds(first, depth)], weight[j], preferred_element_type=jnp.float32
+            )
+            total = product if total is None else total + product
+        out_ref[span] = total.astype(out_ref.dtype)
+
+
+def project(normed, pieces, count, spots, total, is_last):
+    depth, columns = pieces[0].shape
+    chosen = [pieces[i] for spot in spots for i in spot]
+    first = [] if total is None else [total]
+    dtype = jnp.bfloat16 if is_last else jnp.float32
     return pl.pallas_call(
-        functools.partial(qkv_kernel, count),
-        out_shape=jax.ShapeDtypeStruct((normed.shape[0], columns), jnp.bfloat16),
-        in_specs=[VMEM] + [HBM] * len(pieces),
+        functools.partial(qkv_kernel, count, spots, total is not None),
+        out_shape=jax.ShapeDtypeStruct((normed.shape[0], columns), dtype),
+        in_specs=[VMEM] * (1 + len(first)) + [HBM] * len(chosen),
         out_specs=VMEM,
         scratch_shapes=[
-            pltpu.VMEM((depth, columns), jnp.bfloat16),
-            pltpu.SemaphoreType.DMA((len(pieces),)),
+            pltpu.VMEM((len(spots), depth, columns), jnp.bfloat16),
+            pltpu.SemaphoreType.DMA((len(chosen),)),
         ],
         compiler_params=pltpu.CompilerParams(vmem_limit_bytes=32 << 20),
         cost_estimate=pl.CostEstimate(
-            flops=2 * normed.size * columns,
-            bytes_accessed=2 * (normed.size + depth * columns),
+            flops=2 * normed.shape[0] * len(spots) * depth * columns,
+            bytes_accessed=2 * normed.size,
             transcendentals=0,
         ),
         name="qkv",
-    )(normed, *pieces)
+    )(normed, *first, *chosen)
+
+
+def project_all(normed, pieces, count):
+    if not count:
+        return project(normed, pieces, count, ((0,),), None, True)
+    last = len(pieces) - 2
+    early = max(1, last - 2)
+    stages = [tuple((i,) for i in range(early))]
+    if early < last:
+        stages.append(tuple((i,) for i in range(early, last)))
+    stages.append(((last, last + 1),))
+    total = None
+    for s, spots in enumerate(stages):
+        total = project(normed, pieces, count, spots, total, s == len(stages) - 1)
+    return total
 
 
 def attend(qkv, lengths):
@@ -308,17 +334,14 @@
 
     past = lax.ppermute(frames[0, f_dev - 2 :], "ctx", [(i, i + 1) for i in range(n - 1)])
 
-    bounds = ((0, (f_dev + 1) // 2), ((f_dev + 1) // 2, f_dev))
-    parts = []
-    for first, end in bounds:
-        blocks = stream[0, first:end].reshape(end - first, n, pos, width_model).transpose(1, 0, 2, 3)
-        slots = {0: lax.all_to_all(blocks, "ctx", 0, 0)}
-        bit = groups // 2
-        while bit:
-            for j in sorted(slots):
-                slots[j ^ bit] = flip(slots[j], "dp", bit)
-            bit //= 2
-        parts += [slots[j] for j in range(groups)]
+    blocks = stream[0].reshape(f_dev, n, pos, width_model).transpose(1, 0, 2, 3)
+    slots = {0: lax.all_to_all(blocks, "ctx", 0, 0)}
+    bit = groups // 2
+    while bit:
+        for j in sorted(slots):
+            slots[j ^ bit] = flip(slots[j], "dp", bit)
+        bit //= 2
+    parts = [slots[j] for j in range(groups)]
 
     pieces = gather_ring(qkv_weight, "ctx")
 
@@ -340,10 +363,8 @@
     patches = patches.reshape(rows, -1)
     lengths = patches[:: rows // groups, -1].astype(jnp.int32)
 
-    normed = norm_rows(
-        patches, embed_weight, norm_gain, parts, bounds, groups, n, f_dev, pos
-    ).reshape(rows, width_model)
-    qkv = project(normed, pieces, ring_size("ctx"))
+    normed = norm_rows(patches, embed_weight, norm_gain, parts)
+    qkv = project_all(normed, pieces, ring_size("ctx"))
     out = attend(qkv.reshape(groups, n * f_dev, pos, heads, 3 * HD), lengths)
     out = lax.all_to_all(
         out.reshape(groups * n, f_dev, pos, heads * HD), ("dp", "ctx"), 0, 0, tiled=True

time: 253 us -> 232 us (0.917)
  blocking collectives: 28.2 us -> 81.2 us
  waiting for transfers between devices: 86.8 us -> 50.6 us
  starting transfers between devices: 40.2 us -> 19.9 us
  Pallas kernels: 68.6 us -> 59 us
  local copies, waits for them, and re-layouts: 20 us -> 14.3 us
    all_to_all x0 -> x1, blocking collectives: none -> 53 us  [body(): slots = {0: lax.all_to_all(blocks, 'ctx', 0, 0)}]
    all_to_all x2 -> x0, waiting for transfers between devices: 26.5 us -> none  [body(): slots = {0: lax.all_to_all(blocks, 'ctx', 0, 0)}]
    ppermute x1, waiting for transfers between devices: 20.1 us -> 8.24 us  [body(): lax.ppermute(frames[0, f_dev - 2:], 'ctx', [(i, i + 1) for i in range(n -...]
    all_to_all x2 -> x0, starting transfers between devices: 10.9 us -> none  [body(): slots = {0: lax.all_to_all(blocks, 'ctx', 0, 0)}]
    ppermute x3, starting transfers between devices: 12.5 us -> 3.62 us  [gather_ring(): up = lax.ppermute(up, axis, ahead)]
    pallas_call x2 -> x4, Pallas kernels: 40.6 us -> 32 us  [the longest x3 19 us: project(): pl.pallas_call(functools.partial(qkv_kernel, count, spots, total is not N...]
    transpose x2 -> x1, local copies, waits for them, and re-layouts: 4.43 us -> 0.13 us  [body(): blocks = stream[0].reshape(f_dev, n, pos, width_model).transpose(1, 0, 2, 3)]
    ppermute x3, starting transfers between devices: 0.03 us -> 4.23 us  [gather_ring(): down = lax.ppermute(down, axis, behind)]
  transfers between devices with their start and end apart: 18 -> 13, of which waited for: 4 -> 5; matrix products, arithmetic and copies ran while one was open for 4% -> 2% of each run, Pallas kernels for 22% -> 24%
where the time goes in v2:
time: 232 us
  blocking collectives  81.2 us (35%)
  Pallas kernels  59 us (25%)
  waiting for transfers between devices  50.6 us (22%)
  starting transfers between devices  19.9 us (9%)
  local copies, waits for them, and re-layouts  14.3 us (6%)
  matrix products  4.63 us (2%)
    all_to_all x1, blocking collectives, body(): slots = {0: lax.all_to_all(blocks, 'ctx', 0, 0)}  53 us
    ppermute x3, waiting for transfers between devices, gather_ring(): up = lax.ppermute(up, axis, ahead)  29 us
    all_to_all x1, blocking collectives, body(): lax.all_to_all(out.reshape(groups * n, f_dev, pos, heads * HD), ('dp', 'c...  28.2 us
    pallas_call x1, Pallas kernels, conv_section(): pl.pallas_call(conv_kernel, out_shape=(jax.ShapeDtypeStruct(frames.shape,...  27 us
    pallas_call x3, Pallas kernels, project(): pl.pallas_call(functools.partial(qkv_kernel, count, spots, total is not N...  19 us
    pallas_call x1, Pallas kernels, norm_rows(): pl.pallas_call(functools.partial(norm_kernel, groups, embed_weight.shape[...  13 us
    all_to_all x1, waiting for transfers between devices, body(): patches = lax.all_to_all(patches, ('dp', 'ctx'), 0, 0, tiled=True)  12 us
    ppermute x1, waiting for transfers between devices, body(): lax.ppermute(frames[0, f_dev - 2:], 'ctx', [(i, i + 1) for i in range(n -...  8.24 us
  transfers between devices with their start and end apart: 13, of which 5 were waited for; matrix products, arithmetic and copies ran while one was open for 2% of the time, Pallas kernels for 24%

profile of v2, /device:TPU:0, one launch (start us, length us, event | category | flops | bytes accessed | tf_op | source)
XLA Modules:
  0.0 231.5 jit_solution(15941498902046622936)
XLA Ops:
  0.6 0.0 copy-start
  0.6 1.5 copy-done
  2.2 0.1 copy_bitcast_fusion
  2.3 0.0 copy-start.6
  2.3 0.0 copy-start.10
  2.3 53.0 %all_to_all.15.refs_0_ = bf16[8,5,8,3072]{3,2,1,0:T(8,128)(2,1)S(1)} all-to-all(bf16[8,5,8,3072]{3,2,1,0:T(8,128)(2,1)S(1)} %copy_bitcast_fusion), channel_id=1, replica_groups=mesh['dp'=4,'ctx'=8] {'ctx'}, dimensions={0} | all-to-all | bytes 3932160 | tf_op jit(solution)/shard_map/all_to_all | solution.py:338
  55.3 1.5 collective-permute-start.2
  56.8 0.0 copy-done.6
  56.8 0.9 collective-permute-start.4
  57.7 1.1 collective-permute-start.5
  58.9 17.6 %collective-permute-done.4.refs_1_ = bf16[384,1152]{1,0:T(8,128)(2,1)S(1)} collective-permute-done((bf16[384,1152]{1,0:T(8,128)(2,1)S(1)}, bf16[384,1152]{1,0:T(8,128)(2,1)S(1)}, u32[]{:S(2)}, u32[]{:S(2)}) %collective-permute-start.4) | collective-permute-done | bytes 884768 | tf_op jit(solution)/shard_map/ppermute | solution.py:36
  76.5 1.4 collective-permute-start.6
  77.9 0.0 collective-permute-done.5.refs_2_
  77.9 0.6 collective-permute-start.7
  78.5 1.9 slice_bitcast_fusion
  80.4 3.7 %collective-permute-start = (bf16[2,16,16,512]{3,2,1,0:T(8,128)(2,1)}, bf16[2,16,16,512]{3,2,1,0:T(8,128)(2,1)S(1)}, u32[]{:S(2)}, u32[]{:S(2)}) collective-permute-start(bf16[2,16,16,512]{3,2,1,0:T(8,128)(2,1)} %slice_bitcast_fusion), channel_id=1, source_target_pairs={{0,1},{1,2},{2,3},{3,4},{4,5},{5,6},{6,7},{8,9},{9,10},{10,11},{11... | collective-permute-start | bytes 1572872 | tf_op jit(solution)/shard_map/ppermute | solution.py:335
  84.7 0.0 copy-done.10
  84.7 0.1 copy.24.latent_weight_ref
  84.9 0.0 copy-done.8
  84.9 11.3 %collective-permute-done.6.refs_3_ = bf16[384,1152]{1,0:T(8,128)(2,1)} collective-permute-done((bf16[384,1152]{1,0:T(8,128)(2,1)S(1)}, bf16[384,1152]{1,0:T(8,128)(2,1)}, u32[]{:S(2)}, u32[]{:S(2)}) %collective-permute-start.6) | collective-permute-done | bytes 884768 | tf_op jit(solution)/shard_map/ppermute | solution.py:36
  96.2 1.3 collective-permute-start.8
  97.5 1.4 collective-permute-done.7.refs_4_
  98.9 2.5 %collective-permute-start.9 = (bf16[384,1152]{1,0:T(8,128)(2,1)}, bf16[384,1152]{1,0:T(8,128)(2,1)}, u32[]{:S(2)}, u32[]{:S(2)}) collective-permute-start(bf16[384,1152]{1,0:T(8,128)(2,1)} %collective-permute-done.7.refs_4_), channel_id=1, source_target_pairs={{2,0},{4,2},{6,4},{7,6},{5,7},{3,5},{1,3},{0,1},{10,8},{12,10},{14... | collective-permute-start | bytes 2654216 | tf_op jit(solution)/shard_map/ppermute | solution.py:37
  101.4 0.0 collective-permute-start.1
  101.4 0.0 collective-permute-done.2.refs_2_
  101.4 0.5 collective-permute-start.3
  101.9 8.2 %collective-permute-done.past_ref = bf16[2,16,16,512]{3,2,1,0:T(8,128)(2,1)S(1)} collective-permute-done((bf16[2,16,16,512]{3,2,1,0:T(8,128)(2,1)}, bf16[2,16,16,512]{3,2,1,0:T(8,128)(2,1)S(1)}, u32[]{:S(2)}, u32[]{:S(2)}) %collective-permute-start) | collective-permute-done | bytes 524320 | tf_op jit(solution)/shard_map/ppermute | solution.py:335
  110.1 1.3 copy-done.4
  111.4 27.0 %conv.1 = (bf16[5,16,16,512]{3,2,1,0:T(8,128)(2,1)}, bf16[1280,16]{1,0:T(8,128)(2,1)S(1)}) custom-call(s32[1]{0:T(128)S(6)} %copy.64.length_ref, bf16[2,16,16,512]{3,2,1,0:T(8,128)(2,1)S(1)} %collective-permute-done.past_ref, bf16[5,16,16,512]{3,2,1,0:T(8,128)(2,1)S(1)} %bitcast.34, bf16[27,512,512]{2,1,0:T(8,128)(2,1)} %bitcast.40, ...), custom_call_target="tpu_custom_call" | custom-call | flops 18119393280 | bytes 14155776 | tf_op jit(solution)/shard_map/conv/pallas_call | solution.py:139
  138.4 0.2 copy.63
  138.6 0.0 copy-start.5
  138.7 0.2 reshape.95
  138.9 0.8 broadcast_in_dim.15
  139.7 4.3 %all-to-all-start = ((bf16[32,5,8,65]{3,2,1,0:T(8,128)(2,1)}), bf16[32,5,8,65]{3,2,1,0:T(8,128)(2,1)S(1)}, u32[]{:S(2)}, u32[]{:S(2)}) async-start(bf16[32,5,8,65]{3,2,1,0:T(8,128)(2,1)} %bitcast.8), calls=%async_computation | async-start | bytes 655360 | tf_op jit(solution)/shard_map/all_to_all | solution.py:361
  144.0 12.0 %all-to-all-done = bf16[32,5,8,65]{3,2,1,0:T(8,128)(2,1)S(1)} async-done(((bf16[32,5,8,65]{3,2,1,0:T(8,128)(2,1)}), bf16[32,5,8,65]{3,2,1,0:T(8,128)(2,1)S(1)}, u32[]{:S(2)}, u32[]{:S(2)}) %all-to-all-start) | async-done | bytes 166432 | tf_op jit(solution)/shard_map/all_to_all | solution.py:361
  156.0 0.1 slice.25
  156.1 0.1 convert_reduce_fusion
  156.2 0.1 iota_compare_fusion.1
  156.3 0.1 and_or_fusion
  156.4 0.0 collective-permute-done.8.refs_1_
  156.5 1.0 collective-permute-start.10
  157.4 0.0 collective-permute-done.9.refs_2_
  157.4 1.8 slice.29
  159.3 1.1 collective-permute-start.11
  160.4 0.0 collective-permute-done.1.refs_1_
  160.4 0.0 collective-permute-done.3.refs_3_
  160.4 0.0 copy-done.5
  160.4 0.0 copy-done.3
  160.4 0.0 copy-start.7
  160.4 0.0 copy-start.9
  160.4 13.0 %norm.1 = bf16[4,8,5,8,3072]{4,3,2,1,0:T(8,128)(2,1)} custom-call(bf16[1280,65]{1,0:T(8,128)(2,1)S(1)} %bitcast.32, bf16[64,3072]{1,0:T(8,128)(2,1)S(1)} %copy-done.3, f32[1,3072]{1,0:T(1,128)S(1)} %bitcast.35, bf16[8,5,8,3072]{3,2,1,0:T(8,128)(2,1)S(1)} %all_to_all.15.refs_0_, bf16[8,5,8,3072]{3,2,1,0:T(8,128)(2,1)} %collective-permute-done.1.refs_1_, ...), custom_call_target="tpu_custom_call" | custom-call | flops 4026531840 | bytes 15728640 | tf_op jit(solution)/shard_map/norm/pallas_call | solution.py:210
  173.5 3.2 %copy-done.2 = bf16[4,8,5,8,3072]{4,3,2,1,0:T(8,128)(2,1)S(1)} copy-done((bf16[4,8,5,8,3072]{4,3,2,1,0:T(8,128)(2,1)S(1)}, bf16[4,8,5,8,3072]{4,3,2,1,0:T(8,128)(2,1)}, u32[]{:S(2)}) %copy-start.2) | copy-done | bytes 7864344
  176.7 10.9 %qkv.3.refs_0_ = f32[1280,1152]{1,0:T(8,128)S(1)} custom-call(bf16[1280,3072]{1,0:T(8,128)(2,1)S(1)} %bitcast.27, bf16[384,1152]{1,0:T(8,128)(2,1)S(1)} %copy-done.7, bf16[384,1152]{1,0:T(8,128)(2,1)S(1)} %copy-done.9, bf16[384,1152]{1,0:T(8,128)(2,1)} %collective-permute-done.5.refs_2_, bf16[384,1152]{1,0:T(8,128)(2,1)} %collective-permute-done.6.refs_3_, ...), custom_call_target="tpu_custom_call" | custom-call | flops 5662310400 | bytes 7864320 | tf_op jit(solution)/shard_map/qkv/pallas_call | solution.py:273
  187.6 5.3 %qkv.4.refs_0_ = f32[1280,1152]{1,0:T(8,128)S(1)} custom-call(bf16[1280,3072]{1,0:T(8,128)(2,1)S(1)} %bitcast.28, f32[1280,1152]{1,0:T(8,128)S(1)} %qkv.3.refs_0_, bf16[384,1152]{1,0:T(8,128)(2,1)S(1)} %collective-permute-done.8.refs_1_, bf16[384,1152]{1,0:T(8,128)(2,1)} %collective-permute-done.9.refs_2_), custom_call_target="tpu_custom_call" | custom-call | flops 2264924160 | bytes 7864320 | tf_op jit(solution)/shard_map/qkv/pallas_call | solution.py:273
  192.9 0.0 collective-permute-done.10.refs_1_
  192.9 0.0 collective-permute-done.11.refs_2_
  192.9 2.8 %qkv.5 = bf16[1280,1152]{1,0:T(8,128)(2,1)S(1)} custom-call(bf16[1280,3072]{1,0:T(8,128)(2,1)S(1)} %bitcast.29, f32[1280,1152]{1,0:T(8,128)S(1)} %qkv.4.refs_0_, bf16[192,1152]{1,0:T(8,128)(2,1)S(1)} %collective-permute-done.10.refs_1_, bf16[192,1152]{1,0:T(8,128)(2,1)S(1)} %collective-permute-done.11.refs_2_), custom_call_target="tpu_custom_call" | custom-call | flops 1132462080 | bytes 7864320 | tf_op jit(solution)/shard_map/qkv/pallas_call | solution.py:273
  195.7 0.7 fusion.25
  196.4 2.4 %fusion.26 = (f32[4,8,3,40]{3,2,1,0:T(4,128)S(1)}, f32[4,8,3,40,40]{3,4,2,1,0:T(8,128)}) fusion(pred[4,40,40]{1,2,0:T(8,128)(4,1)S(1)} %and_or_fusion, bf16[4,40,8,3,128]{4,2,3,1,0:T(8,128)(2,1)S(1)} %get-tuple-element.8, bf16[4,40,8,3,128]{4,2,3,1,0:T(8,128)(2,1)S(1)} %get-tuple-element.7), kind=kOutput, calls=%fused_computation.25 | convolution fusion | flops 39936040 | bytes 2602240 | tf_op jit(solution)/shard_map/sub | solution.py:319
  198.8 2.3 fusion.2
  201.1 0.1 copy.32
  201.2 28.2 %all_to_all.16 = bf16[32,5,8,384]{3,2,1,0:T(8,128)(2,1)S(1)} all-to-all(bf16[32,5,8,384]{3,2,1,0:T(8,128)(2,1)S(1)} %bitcast.36), channel_id=1, replica_groups=mesh['dp'=4,'ctx'=8] {'dp','ctx'}, dimensions={0} | all-to-all | bytes 1966080 | tf_op jit(solution)/shard_map/all_to_all | solution.py:369
  229.5 0.8 copy.33
  230.2 1.3 reshape.102
  (12 shorter events, 0.1 us)
Async XLA Ops:
  0.6 1.6 copy-start
  2.3 54.5 %copy-start.6 = (bf16[384,1152]{1,0:T(8,128)(2,1)S(1)}, bf16[384,1152]{1,0:T(8,128)(2,1)}, u32[]{:S(2)}) copy-start(bf16[384,1152]{1,0:T(8,128)(2,1)} %refs_0_.1) | copy-start | bytes 2654212
  2.3 82.4 %copy-start.10 = (bf16[512,16]{0,1:T(8,128)(2,1)S(1)}, bf16[512,16]{0,1:T(8,128)(2,1)}, u32[]{:S(2)}) copy-start(bf16[512,16]{0,1:T(8,128)(2,1)} %param.12) | copy-start | bytes 49156
  55.3 46.0 %collective-permute-start.2 = (bf16[8,5,8,3072]{3,2,1,0:T(8,128)(2,1)S(1)}, bf16[8,5,8,3072]{3,2,1,0:T(8,128)(2,1)}, u32[]{:S(2)}, u32[]{:S(2)}) collective-permute-start(bf16[8,5,8,3072]{3,2,1,0:T(8,128)(2,1)S(1)} %all_to_all.15.refs_0_), channel_id=1, source_target_pairs={{0,16},{8,24},{16,0},{24,8},{1,17},{9,25},{17,1},{25,9},{2,18},{10... | collective-permute-start | bytes 5898248 | tf_op jit(solution)/shard_map/ppermute | solution.py:18
  56.8 19.7 %collective-permute-start.4 = (bf16[384,1152]{1,0:T(8,128)(2,1)S(1)}, bf16[384,1152]{1,0:T(8,128)(2,1)S(1)}, u32[]{:S(2)}, u32[]{:S(2)}) collective-permute-start(bf16[384,1152]{1,0:T(8,128)(2,1)S(1)} %copy-done.6), channel_id=1, source_target_pairs={{0,2},{2,4},{4,6},{6,7},{7,5},{5,3},{3,1},{1,0},{8,10},{10,12},{12... | collective-permute-start | bytes 2654216 | tf_op jit(solution)/shard_map/ppermute | solution.py:36
  57.7 20.2 %collective-permute-start.5 = (bf16[384,1152]{1,0:T(8,128)(2,1)S(1)}, bf16[384,1152]{1,0:T(8,128)(2,1)}, u32[]{:S(2)}, u32[]{:S(2)}) collective-permute-start(bf16[384,1152]{1,0:T(8,128)(2,1)S(1)} %copy-done.6), channel_id=1, source_target_pairs={{2,0},{4,2},{6,4},{7,6},{5,7},{3,5},{1,3},{0,1},{10,8},{12,10},{14... | collective-permute-start | bytes 2654216 | tf_op jit(solution)/shard_map/ppermute | solution.py:37
  76.5 8.4 %copy-start.8 = (bf16[384,1152]{1,0:T(8,128)(2,1)}, bf16[384,1152]{1,0:T(8,128)(2,1)S(1)}, u32[]{:S(2)}) copy-start(bf16[384,1152]{1,0:T(8,128)(2,1)S(1)} %collective-permute-done.4.refs_1_) | copy-start | bytes 2654212
  76.5 19.7 %collective-permute-start.6 = (bf16[384,1152]{1,0:T(8,128)(2,1)S(1)}, bf16[384,1152]{1,0:T(8,128)(2,1)}, u32[]{:S(2)}, u32[]{:S(2)}) collective-permute-start(bf16[384,1152]{1,0:T(8,128)(2,1)S(1)} %collective-permute-done.4.refs_1_), channel_id=1, source_target_pairs={{0,2},{2,4},{4,6},{6,7},{7,5},{5,3},{3,1},{1,0},{8,10},{10,12},{12... | collective-permute-start | bytes 2654216 | tf_op jit(solution)/shard_map/ppermute | solution.py:36
  77.9 21.0 %collective-permute-start.7 = (bf16[384,1152]{1,0:T(8,128)(2,1)}, bf16[384,1152]{1,0:T(8,128)(2,1)}, u32[]{:S(2)}, u32[]{:S(2)}) collective-permute-start(bf16[384,1152]{1,0:T(8,128)(2,1)} %collective-permute-done.5.refs_2_), channel_id=1, source_target_pairs={{2,0},{4,2},{6,4},{7,6},{5,7},{3,5},{1,3},{0,1},{10,8},{12,10},{14... | collective-permute-start | bytes 2654216 | tf_op jit(solution)/shard_map/ppermute | solution.py:37
  80.4 29.7 %collective-permute-start = (bf16[2,16,16,512]{3,2,1,0:T(8,128)(2,1)}, bf16[2,16,16,512]{3,2,1,0:T(8,128)(2,1)S(1)}, u32[]{:S(2)}, u32[]{:S(2)}) collective-permute-start(bf16[2,16,16,512]{3,2,1,0:T(8,128)(2,1)} %slice_bitcast_fusion), channel_id=1, source_target_pairs={{0,1},{1,2},{2,3},{3,4},{4,5},{5,6},{6,7},{8,9},{9,10},{10,11},{11... | collective-permute-start | bytes 1572872 | tf_op jit(solution)/shard_map/ppermute | solution.py:335
  96.2 60.2 %collective-permute-start.8 = (bf16[384,1152]{1,0:T(8,128)(2,1)}, bf16[384,1152]{1,0:T(8,128)(2,1)S(1)}, u32[]{:S(2)}, u32[]{:S(2)}) collective-permute-start(bf16[384,1152]{1,0:T(8,128)(2,1)} %collective-permute-done.6.refs_3_), channel_id=1, source_target_pairs={{0,2},{2,4},{4,6},{6,7},{7,5},{5,3},{3,1},{1,0},{8,10},{10,12},{12... | collective-permute-start | bytes 2654216 | tf_op jit(solution)/shard_map/ppermute | solution.py:36
  98.9 58.6 %collective-permute-start.9 = (bf16[384,1152]{1,0:T(8,128)(2,1)}, bf16[384,1152]{1,0:T(8,128)(2,1)}, u32[]{:S(2)}, u32[]{:S(2)}) collective-permute-start(bf16[384,1152]{1,0:T(8,128)(2,1)} %collective-permute-done.7.refs_4_), channel_id=1, source_target_pairs={{2,0},{4,2},{6,4},{7,6},{5,7},{3,5},{1,3},{0,1},{10,8},{12,10},{14... | collective-permute-start | bytes 2654216 | tf_op jit(solution)/shard_map/ppermute | solution.py:37
  101.4 59.0 %collective-permute-start.1 = (bf16[8,5,8,3072]{3,2,1,0:T(8,128)(2,1)S(1)}, bf16[8,5,8,3072]{3,2,1,0:T(8,128)(2,1)}, u32[]{:S(2)}, u32[]{:S(2)}) collective-permute-start(bf16[8,5,8,3072]{3,2,1,0:T(8,128)(2,1)S(1)} %all_to_all.15.refs_0_), channel_id=1, source_target_pairs={{0,8},{8,0},{16,24},{24,16},{1,9},{9,1},{17,25},{25,17},{2,10},{10... | collective-permute-start | bytes 5898248 | tf_op jit(solution)/shard_map/ppermute | solution.py:18
  101.4 59.0 %collective-permute-start.3 = (bf16[8,5,8,3072]{3,2,1,0:T(8,128)(2,1)}, bf16[8,5,8,3072]{3,2,1,0:T(8,128)(2,1)}, u32[]{:S(2)}, u32[]{:S(2)}) collective-permute-start(bf16[8,5,8,3072]{3,2,1,0:T(8,128)(2,1)} %collective-permute-done.2.refs_2_), channel_id=1, source_target_pairs={{0,8},{8,0},{16,24},{24,16},{1,9},{9,1},{17,25},{25,17},{2,10},{10... | collective-permute-start | bytes 5898248 | tf_op jit(solution)/shard_map/ppermute | solution.py:18
  110.1 1.3 copy-start.4
  138.6 21.7 %copy-start.5 = (f32[3072]{0:T(1024)S(1)}, f32[3072]{0:T(1024)}, u32[]{:S(2)}) copy-start(f32[3072]{0:T(1024)} %param.14) | copy-start | bytes 36868
  139.7 16.3 %all-to-all-start = ((bf16[32,5,8,65]{3,2,1,0:T(8,128)(2,1)}), bf16[32,5,8,65]{3,2,1,0:T(8,128)(2,1)S(1)}, u32[]{:S(2)}, u32[]{:S(2)}) async-start(bf16[32,5,8,65]{3,2,1,0:T(8,128)(2,1)} %bitcast.8), calls=%async_computation | async-start | bytes 655360 | tf_op jit(solution)/shard_map/all_to_all | solution.py:361
  156.1 4.3 %copy-start.3 = (bf16[64,3072]{1,0:T(8,128)(2,1)S(1)}, bf16[64,3072]{1,0:T(8,128)(2,1)}, u32[]{:S(2)}) copy-start(bf16[64,3072]{1,0:T(8,128)(2,1)} %embed_ref.1) | copy-start | bytes 1179652
  156.5 36.4 %collective-permute-start.10 = (bf16[192,1152]{1,0:T(8,128)(2,1)S(1)}, bf16[192,1152]{1,0:T(8,128)(2,1)S(1)}, u32[]{:S(2)}, u32[]{:S(2)}) collective-permute-start(bf16[192,1152]{1,0:T(8,128)(2,1)S(1)} %slice.28), channel_id=1, source_target_pairs={{0,2},{2,4},{4,6},{6,7},{7,5},{5,3},{3,1},{1,0},{8,10},{10,12},{12... | collective-permute-start | bytes 1327112 | tf_op jit(solution)/shard_map/ppermute | solution.py:40
  159.3 33.6 %collective-permute-start.11 = (bf16[192,1152]{1,0:T(8,128)(2,1)}, bf16[192,1152]{1,0:T(8,128)(2,1)S(1)}, u32[]{:S(2)}, u32[]{:S(2)}) collective-permute-start(bf16[192,1152]{1,0:T(8,128)(2,1)} %slice.29), channel_id=1, source_target_pairs={{2,0},{4,2},{6,4},{7,6},{5,7},{3,5},{1,3},{0,1},{10,8},{12,10},{14... | collective-permute-start | bytes 1327112 | tf_op jit(solution)/shard_map/ppermute | solution.py:41
  160.4 13.1 %copy-start.7 = (bf16[384,1152]{1,0:T(8,128)(2,1)S(1)}, bf16[384,1152]{1,0:T(8,128)(2,1)}, u32[]{:S(2)}) copy-start(bf16[384,1152]{1,0:T(8,128)(2,1)} %refs_0_.1) | copy-start | bytes 2654212
  160.4 13.1 %copy-start.9 = (bf16[384,1152]{1,0:T(8,128)(2,1)S(1)}, bf16[384,1152]{1,0:T(8,128)(2,1)}, u32[]{:S(2)}) copy-start(bf16[384,1152]{1,0:T(8,128)(2,1)} %copy-done.8) | copy-start | bytes 2654212
  173.5 3.2 %copy-start.2 = (bf16[4,8,5,8,3072]{4,3,2,1,0:T(8,128)(2,1)S(1)}, bf16[4,8,5,8,3072]{4,3,2,1,0:T(8,128)(2,1)}, u32[]{:S(2)}) copy-start(bf16[4,8,5,8,3072]{4,3,2,1,0:T(8,128)(2,1)} %norm.1) | copy-start | bytes 23592964
  229.5 2.1 copy-start.1

commit v3 on v2

--- a/solution.py
+++ b/solution.py
@@ -59,60 +59,79 @@
     return first + [far, far + rows // 2]
 
 
-def conv_kernel(
-    length_ref, past_ref, frames_ref, weight_ref, latent_weight_ref, section_ref, latent_ref,
-    shifted, weights, near, lagged, sems,
+def load_taps(weight_ref, weights, sems, first):
+    def load(tap):
+        return pltpu.make_async_copy(weight_ref.at[first + tap], weights.at[tap], sems.at[tap])
+
+    for tap in range(weights.shape[0]):
+        load(tap).start()
+    return load
+
+
+def shift_into(shifted, source, slot):
+    height, width, channels = source.shape
+    cells = height * width
+    column = lax.rem(lax.broadcasted_iota(jnp.int32, (cells, channels), 0), width)
+    edge = jnp.zeros((width, channels), jnp.bfloat16)
+    act = jax.nn.silu(source.astype(jnp.float32)).reshape(cells, channels)
+    left = jnp.where(column == 0, 0.0, pltpu.roll(act, 1, 0))
+    right = jnp.where(column == width - 1, 0.0, pltpu.roll(act, cells - 1, 0))
+    for col, value in enumerate((left, act, right)):
+        shifted[col, slot, 0] = edge
+        shifted[col, slot, height + 1] = edge
+        shifted[col, slot, 1 : height + 1] = value.astype(jnp.bfloat16).reshape(source.shape)
+
+
+def add_tap(total, shifted, weights, load, tap, start, row, col, f_dev, height):
+    load(tap).wait()
+    slab = shifted[col, pl.ds(start, f_dev), pl.ds(row, height)]
+    total[...] += jnp.dot(
+        slab.reshape(total.shape[0], slab.shape[-1]),
+        weights[tap],
+        preferred_element_type=jnp.float32,
+    )
+
+
+def near_kernel(frames_ref, weight_ref, near_ref, shifted, weights, sems):
+    f_dev, height = frames_ref.shape[:2]
+    load = load_taps(weight_ref, weights, sems, 0)
+
+    @pl.loop(0, f_dev)
+    def _(slot):
+        shift_into(shifted, frames_ref[slot], slot)
+
+    near_ref[...] = jnp.zeros_like(near_ref)
+
+    @pl.loop(0, weights.shape[0])
+    def _(tap):
+        add_tap(near_ref, shifted, weights, load, tap, 0, tap // 3, lax.rem(tap, 3), f_dev, height)
+
+
+def lagged_kernel(
+    length_ref, past_ref, frames_ref, weight_ref, latent_weight_ref, near_ref, section_ref,
+    latent_ref, shifted, weights, total, sems,
 ):
     f_dev, height, width, channels = frames_ref.shape
-    lags, side = past_ref.shape[0] + 1, 3
-    taps = weight_ref.shape[0]
-    cells = height * width
-
-    def load(tap):
-        return pltpu.make_async_copy(weight_ref.at[tap], weights.at[tap], sems.at[tap])
-
-    for tap in range(taps):
-        load(tap).start()
-    column = lax.rem(lax.broadcasted_iota(jnp.int32, (cells, channels), 0), width)
-    edge = jnp.zeros((width, channels), jnp.bfloat16)
-
-    def prepare(source, slot):
-        act = jax.nn.silu(source.astype(jnp.float32)).reshape(cells, channels)
-        left = jnp.where(column == 0, 0.0, pltpu.roll(act, 1, 0))
-        right = jnp.where(column == width - 1, 0.0, pltpu.roll(act, cells - 1, 0))
-        for col, value in enumerate((left, act, right)):
-            shifted[col, slot, 0] = edge
-            shifted[col, slot, height + 1] = edge
-            shifted[col, slot, 1 : height + 1] = value.astype(jnp.bfloat16).reshape(
-                height, width, channels
-            )
-
-    @pl.loop(0, lags - 1)
+    lags, cells = past_ref.shape[0], height * width
+    load = load_taps(weight_ref, weights, sems, 9)
+
+    @pl.loop(0, lags)
     def _(slot):
-        prepare(past_ref[slot], slot)
-
-    @pl.loop(0, f_dev)
+        shift_into(shifted, past_ref[slot], slot)
+
+    @pl.loop(0, f_dev - 1)
     def _(slot):
-        prepare(frames_ref[slot], slot + lags - 1)
-
-    def add(tap, total):
-        load(tap).wait()
-        lag, row, col = tap // (side * side), lax.rem(tap // side, side), lax.rem(tap, side)
-        slab = shifted[col, pl.ds(lags - 1 - lag, f_dev), pl.ds(row, height)]
-        total[...] += jnp.dot(
-            slab.reshape(f_dev * cells, channels), weights[tap], preferred_element_type=jnp.float32
+        shift_into(shifted, frames_ref[slot], slot + lags)
+
+    total[...] = jnp.zeros_like(total)
+
+    @pl.loop(0, weights.shape[0])
+    def _(tap):
+        start = lags - 1 - tap // 9
+        add_tap(
+            total, shifted, weights, load, tap, start, lax.rem(tap // 3, 3), lax.rem(tap, 3),
+            f_dev, height,
         )
-
-    near[...] = jnp.zeros_like(near)
-    lagged[...] = jnp.zeros_like(lagged)
-
-    @pl.loop(0, side * side)
-    def _(tap):
-        add(tap, near)
-
-    @pl.loop(side * side, taps)
-    def _(tap):
-        add(tap, lagged)
 
     first = lax.axis_index("ctx") * f_dev
 
@@ -122,8 +141,8 @@
         rows = pl.ds(pl.multiple_of(slot * cells, cells), cells)
         value = (
             frames_ref[slot].astype(jnp.float32).reshape(cells, channels)
-            + near[rows]
-            + video * lagged[rows]
+            + near_ref[rows]
+            + video * total[rows]
         ).astype(jnp.bfloat16)
         section_ref[slot] = value.reshape(height, width, channels)
         latent_ref[rows] = jnp.dot(
@@ -133,43 +152,108 @@
 
 def conv_section(frames, past, length, conv_weight, latent_weight):
     f_dev, height, width, channels = frames.shape
-    lags = conv_weight.shape[0]
-    taps = conv_weight.shape[0] * conv_weight.shape[1] * conv_weight.shape[2]
+    lags = past.shape[0]
     cells = f_dev * height * width
+    weight = conv_weight.reshape(-1, channels, channels)
+
+    def scratch(slots, taps):
+        return [
+            pltpu.VMEM((3, slots, height + 2, width, channels), jnp.bfloat16),
+            pltpu.VMEM((taps, channels, channels), jnp.bfloat16),
+        ]
+
+    def cost(taps):
+        return pl.CostEstimate(
+            flops=2 * cells * taps * channels * channels,
+            bytes_accessed=2 * taps * channels * channels,
+            transcendentals=0,
+        )
+
+    near = pl.pallas_call(
+        near_kernel,
+        out_shape=jax.ShapeDtypeStruct((cells, channels), jnp.float32),
+        in_specs=[VMEM, HBM],
+        out_specs=VMEM,
+        scratch_shapes=[*scratch(f_dev, 9), pltpu.SemaphoreType.DMA((9,))],
+        compiler_params=pltpu.CompilerParams(vmem_limit_bytes=24 << 20),
+        cost_estimate=cost(9),
+        name="near",
+    )(frames, weight)
     return pl.pallas_call(
-        conv_kernel,
+        lagged_kernel,
         out_shape=(
             jax.ShapeDtypeStruct(frames.shape, jnp.bfloat16),
             jax.ShapeDtypeStruct((cells, latent_weight.shape[1]), jnp.bfloat16),
         ),
-        in_specs=[SMEM, VMEM, VMEM, HBM, VMEM],
+        in_specs=[SMEM, VMEM, VMEM, HBM, VMEM, VMEM],
         out_specs=(VMEM, VMEM),
         scratch_shapes=[
-            pltpu.VMEM((3, f_dev + lags - 1, height + 2, width, channels), jnp.bfloat16),
-            pltpu.VMEM((taps, channels, channels), jnp.bfloat16),
+            *scratch(f_dev + lags - 1, 9 * lags),
             pltpu.VMEM((cells, channels), jnp.float32),
-            pltpu.VMEM((cells, channels), jnp.float32),
-            pltpu.SemaphoreType.DMA((taps,)),
+            pltpu.SemaphoreType.DMA((9 * lags,)),
         ],
-        compiler_params=pltpu.CompilerParams(vmem_limit_bytes=40 << 20),
+        compiler_params=pltpu.CompilerParams(vmem_limit_bytes=36 << 20),
+        cost_estimate=cost(9 * lags),
+        name="lagged",
+    )(length, past, frames, weight, latent_weight, near)
+
+
+def deal_kernel(stream_ref, *outs):
+    n = len(outs)
+    me = lax.axis_index("ctx")
+    for k, out in enumerate(outs):
+        out[...] = stream_ref[:, lax.rem(me + k, n)]
+
+
+def deal(blocks):
+    f_dev, n, pos, width = blocks.shape
+    shape = jax.ShapeDtypeStruct((f_dev, pos, width), blocks.dtype)
+    return pl.pallas_call(
+        deal_kernel,
+        out_shape=(shape,) * n,
+        in_specs=[VMEM],
+        out_specs=(VMEM,) * n,
+        compiler_params=pltpu.CompilerParams(vmem_limit_bytes=10 << 20),
         cost_estimate=pl.CostEstimate(
-            flops=2 * cells * taps * channels * channels,
-            bytes_accessed=2 * conv_weight.size,
-            transcendentals=0,
+            flops=blocks.size, bytes_accessed=4 * blocks.size, transcendentals=0
         ),
-        name="conv",
-    )(length, past, frames, conv_weight.reshape(taps, channels, channels), latent_weight)
-
-
-def norm_kernel(groups, patch_size, patches_ref, embed_ref, gain_ref, *refs):
-    parts, (out_ref, held, embedded, sems) = refs[:groups], refs[groups:]
-    me = lax.axis_index("dp")
+        name="deal",
+    )(blocks)
+
+
+def to_owners(blocks):
+    n = blocks.shape[1]
+    if n > 8:
+        return None, [lax.all_to_all(blocks.transpose(1, 0, 2, 3), "ctx", 0, 0)]
+    pieces = deal(blocks)
+    near_first = sorted(range(n), key=lambda k: (min(k, n - k), -k))
+    halves = [near_first[: n // 2], near_first[n // 2 :]]
+    moved = []
+    for turns in halves:
+        rows = [
+            lax.ppermute(pieces[k], "ctx", [(i, (i + k) % n) for i in range(n)])
+            if k
+            else pieces[0]
+            for k in turns
+        ]
+        moved.append(jnp.stack(rows))
+    return halves, moved
+
+
+def norm_kernel(halves, groups, patch_size, patches_ref, embed_ref, gain_ref, *refs):
+    parts, (out_ref, held, embedded, sems) = refs[:-4], refs[-4:]
+    me, me_ctx = lax.axis_index("dp"), lax.axis_index("ctx")
     width = embed_ref.shape[1]
     n, f_dev, pos = held.shape[1:4]
-    copies = [
-        pltpu.make_async_copy(parts[j], held.at[lax.bitwise_xor(me, j)], sems.at[j])
-        for j in range(groups)
-    ]
+    copies = []
+    for spot, part in enumerate(parts):
+        group = lax.bitwise_xor(me, spot % groups)
+        if halves is None:
+            copies.append((part, held.at[group]))
+            continue
+        for i, k in enumerate(halves[spot // groups]):
+            copies.append((part.at[i], held.at[group, lax.rem(me_ctx - k + n, n)]))
+    copies = [pltpu.make_async_copy(a, b, sems.at[i]) for i, (a, b) in enumerate(copies)]
     for copy in copies:
         copy.start()
     tile = 256
@@ -196,8 +280,8 @@
         out_ref[group, device] = value.reshape(f_dev, pos, width).astype(jnp.bfloat16)
 
 
-def norm_rows(patches, embed_weight, norm_gain, parts):
-    groups, (n, f_dev, pos, width) = len(parts), parts[0].shape
+def norm_rows(patches, embed_weight, norm_gain, halves, parts, groups, n):
+    f_dev, pos, width = parts[0].shape[1:]
     rows = groups * n * f_dev * pos
     if pos % 8:
         order = jnp.arange(groups, dtype=jnp.int32) ^ lax.axis_index("dp")
@@ -208,14 +292,14 @@
         scale = lax.rsqrt(jnp.mean(value * value, axis=-1, keepdims=True) + 1e-06)
         return (value * scale * norm_gain).astype(jnp.bfloat16)
     return pl.pallas_call(
-        functools.partial(norm_kernel, groups, embed_weight.shape[0]),
+        functools.partial(norm_kernel, halves, groups, embed_weight.shape[0]),
         out_shape=jax.ShapeDtypeStruct((groups, n, f_dev, pos, width), jnp.bfloat16),
-        in_specs=[VMEM] * 3 + [HBM] * groups,
+        in_specs=[VMEM] * 3 + [HBM] * len(parts),
         out_specs=VMEM,
         scratch_shapes=[
             pltpu.VMEM((groups, n, f_dev, pos, width), jnp.bfloat16),
             pltpu.VMEM((rows, width), jnp.float32),
-            pltpu.SemaphoreType.DMA((groups,)),
+            pltpu.SemaphoreType.DMA((groups * n,)),
         ],
         compiler_params=pltpu.CompilerParams(vmem_limit_bytes=44 << 20),
         cost_estimate=pl.CostEstimate(
@@ -334,14 +418,16 @@
 
     past = lax.ppermute(frames[0, f_dev - 2 :], "ctx", [(i, i + 1) for i in range(n - 1)])
 
-    blocks = stream[0].reshape(f_dev, n, pos, width_model).transpose(1, 0, 2, 3)
-    slots = {0: lax.all_to_all(blocks, "ctx", 0, 0)}
-    bit = groups // 2
-    while bit:
-        for j in sorted(slots):
-            slots[j ^ bit] = flip(slots[j], "dp", bit)
-        bit //= 2
-    parts = [slots[j] for j in range(groups)]
+    halves, moved = to_owners(stream[0].reshape(f_dev, n, pos, width_model))
+    parts = []
+    for value in moved:
+        slots = {0: value}
+        bit = groups // 2
+        while bit:
+            for j in sorted(slots):
+                slots[j ^ bit] = flip(slots[j], "dp", bit)
+            bit //= 2
+        parts += [slots[j] for j in range(groups)]
 
     pieces = gather_ring(qkv_weight, "ctx")
 
@@ -363,7 +449,7 @@
     patches = patches.reshape(rows, -1)
     lengths = patches[:: rows // groups, -1].astype(jnp.int32)
 
-    normed = norm_rows(patches, embed_weight, norm_gain, parts)
+    normed = norm_rows(patches, embed_weight, norm_gain, halves, parts, groups, n)
     qkv = project_all(normed, pieces, ring_size("ctx"))
     out = attend(qkv.reshape(groups, n * f_dev, pos, heads, 3 * HD), lengths)
     out = lax.all_to_all(

time: 232 us -> 218 us (0.940)
  blocking collectives: 81.2 us -> 28.2 us
  starting transfers between devices: 19.9 us -> 47.8 us
  local copies, waits for them, and re-layouts: 14.3 us -> 19.4 us
  Pallas kernels: 59 us -> 63.7 us
    all_to_all x1 -> x0, blocking collectives: 53 us -> none  [body(): slots = {0: lax.all_to_all(blocks, 'ctx', 0, 0)}]
    ppermute x0 -> x7, waiting for transfers between devices: none -> 29.4 us  [to_owners(): lax.ppermute(pieces[k], 'ctx', [(i, (i + k) % n) for i in range(n)])]
    ppermute x3, waiting for transfers between devices: 29 us -> 1.75 us  [gather_ring(): up = lax.ppermute(up, axis, ahead)]
    ppermute x0 -> x7, starting transfers between devices: none -> 11.9 us  [to_owners(): lax.ppermute(pieces[k], 'ctx', [(i, (i + k) % n) for i in range(n)])]
    all_to_all x1, starting transfers between devices: 4.3 us -> 12.9 us  [body(): patches = lax.all_to_all(patches, ('dp', 'ctx'), 0, 0, tiled=True)]
    ppermute x3 -> x6, waiting for transfers between devices: 0.01 us -> 8.45 us  [flip(): return lax.ppermute(value, axis, [(i, i ^ bit) for i in range(count)])]
    ppermute x1, waiting for transfers between devices: 8.24 us -> 0.01 us  [body(): lax.ppermute(frames[0, f_dev - 2:], 'ctx', [(i, i + 1) for i in range(n -...]
    unnamed x24 -> x26, local copies, waits for them, and re-layouts: 6.27 us -> 14.2 us
  transfers between devices with their start and end apart: 13 -> 23, of which waited for: 5 -> 8; matrix products, arithmetic and copies ran while one was open for 2% -> 1% of each run, Pallas kernels for 24% -> 28%
where the time goes in v3:
time: 218 us; the launch traced here: 217 us
  Pallas kernels  63.7 us (29%)
  waiting for transfers between devices  51.7 us (24%)
  starting transfers between devices  47.8 us (22%)
  blocking collectives  28.2 us (13%)
  local copies, waits for them, and re-layouts  19.4 us (9%)
  matrix products  4.63 us (2%)
    ppermute x7, waiting for transfers between devices, to_owners(): lax.ppermute(pieces[k], 'ctx', [(i, (i + k) % n) for i in range(n)])  29.4 us
    all_to_all x1, blocking collectives, body(): lax.all_to_all(out.reshape(groups * n, f_dev, pos, heads * HD), ('dp', 'c...  28.2 us
    pallas_call x1, Pallas kernels, conv_section(): pl.pallas_call(lagged_kernel, out_shape=(jax.ShapeDtypeStruct(frames.shap...  19.2 us
    pallas_call x3, Pallas kernels, project(): pl.pallas_call(functools.partial(qkv_kernel, count, spots, total is not N...  18.2 us
    pallas_call x1, Pallas kernels, norm_rows(): pl.pallas_call(functools.partial(norm_kernel, halves, groups, embed_weigh...  16.8 us
    unnamed x26, local copies, waits for them, and re-layouts  14.2 us
    all_to_all x1, starting transfers between devices, body(): patches = lax.all_to_all(patches, ('dp', 'ctx'), 0, 0, tiled=True)  12.9 us
    all_to_all x1, waiting for transfers between devices, body(): patches = lax.all_to_all(patches, ('dp', 'ctx'), 0, 0, tiled=True)  12 us
  transfers between devices with their start and end apart: 23, of which 8 were waited for; matrix products, arithmetic and copies ran while one was open for 1% of the time, Pallas kernels for 28%

profile of v3, /device:TPU:0, one launch (start us, length us, event | category | flops | bytes accessed | tf_op | source)
XLA Modules:
  0.0 217.5 jit_solution(7443363409730113092)
XLA Ops:
  0.6 1.5 copy-done.1
  2.2 0.1 deal.1
  2.3 5.1 %collective-permute-start.3 = (bf16[5,8,3072]{2,1,0:T(8,128)(2,1)S(1)}, bf16[5,8,3072]{2,1,0:T(8,128)(2,1)S(1)}, u32[]{:S(2)}, u32[]{:S(2)}) collective-permute-start(bf16[5,8,3072]{2,1,0:T(8,128)(2,1)S(1)} %get-tuple-element.17), channel_id=1, source_target_pairs={{0,6},{1,7},{2,0},{3,1},{4,2},{5,3},{6,4},{7,5},{8,14},{9,15},{10,... | collective-permute-start | bytes 737288 | tf_op jit(solution)/shard_map/ppermute | solution.py:234
  7.4 1.5 collective-permute-start.2
  9.0 3.2 %collective-permute-start.1 = (bf16[5,8,3072]{2,1,0:T(8,128)(2,1)S(1)}, bf16[5,8,3072]{2,1,0:T(8,128)(2,1)S(1)}, u32[]{:S(2)}, u32[]{:S(2)}) collective-permute-start(bf16[5,8,3072]{2,1,0:T(8,128)(2,1)S(1)} %get-tuple-element.15), channel_id=1, source_target_pairs={{0,7},{1,0},{2,1},{3,2},{4,3},{5,4},{6,5},{7,6},{8,15},{9,8},{10,9... | collective-permute-start | bytes 737288 | tf_op jit(solution)/shard_map/ppermute | solution.py:234
  12.2 1.1 slice_bitcast_fusion
  13.2 1.3 collective-permute-start
  14.6 0.1 collective-permute-start.10
  14.6 0.0 collective-permute-done.3
  14.7 0.5 collective-permute-start.9
  15.2 5.8 %collective-permute-done.2 = bf16[5,8,3072]{2,1,0:T(8,128)(2,1)S(1)} collective-permute-done((bf16[5,8,3072]{2,1,0:T(8,128)(2,1)S(1)}, bf16[5,8,3072]{2,1,0:T(8,128)(2,1)S(1)}, u32[]{:S(2)}, u32[]{:S(2)}) %collective-permute-start.2) | collective-permute-done | bytes 245792 | tf_op jit(solution)/shard_map/ppermute | solution.py:234
  21.0 0.6 collective-permute-start.8
  21.6 0.9 collective-permute-start.7
  22.5 0.1 pad_maximum_fusion.refs_0_
  22.6 22.3 %collective-permute-done.10 = bf16[5,8,3072]{2,1,0:T(8,128)(2,1)S(1)} collective-permute-done((bf16[5,8,3072]{2,1,0:T(8,128)(2,1)S(1)}, bf16[5,8,3072]{2,1,0:T(8,128)(2,1)S(1)}, u32[]{:S(2)}, u32[]{:S(2)}) %collective-permute-start.10) | collective-permute-done | bytes 245792 | tf_op jit(solution)/shard_map/ppermute | solution.py:234
  44.9 1.3 collective-permute-done.9
  46.2 1.5 collective-permute-start.5
  47.7 0.1 pad_maximum_fusion.1.refs_4_
  47.8 0.6 collective-permute-start.12
  48.4 5.2 %collective-permute-start.14 = (bf16[384,1152]{1,0:T(8,128)(2,1)}, bf16[384,1152]{1,0:T(8,128)(2,1)}, u32[]{:S(2)}, u32[]{:S(2)}) collective-permute-start(bf16[384,1152]{1,0:T(8,128)(2,1)} %refs_0_.1), channel_id=1, source_target_pairs={{0,2},{2,4},{4,6},{6,7},{7,5},{5,3},{3,1},{1,0},{8,10},{10,12},{12... | collective-permute-start | bytes 2654216 | tf_op jit(solution)/shard_map/ppermute | solution.py:36
  53.6 0.8 copy-done.9
  54.4 5.1 %collective-permute-start.15 = (bf16[384,1152]{1,0:T(8,128)(2,1)}, bf16[384,1152]{1,0:T(8,128)(2,1)}, u32[]{:S(2)}, u32[]{:S(2)}) collective-permute-start(bf16[384,1152]{1,0:T(8,128)(2,1)} %refs_0_.1), channel_id=1, source_target_pairs={{2,0},{4,2},{6,4},{7,6},{5,7},{3,5},{1,3},{0,1},{10,8},{12,10},{14... | collective-permute-start | bytes 2654216 | tf_op jit(solution)/shard_map/ppermute | solution.py:37
  60.2 0.1 copy.23.latent_weight_ref
  60.3 0.0 copy-start.5
  60.3 1.3 copy-done.5
  61.6 5.0 %copy-done.8 = bf16[3,3,3,512,512]{4,3,2,1,0:T(8,128)(2,1)S(1)} copy-done((bf16[3,3,3,512,512]{4,3,2,1,0:T(8,128)(2,1)S(1)}, bf16[3,3,3,512,512]{4,3,2,1,0:T(8,128)(2,1)}, u32[]{:S(2)}) %copy-start.8) | copy-done | bytes 14155800
  66.7 9.3 %near.1.near_ref = f32[1280,512]{1,0:T(8,128)S(1)} custom-call(bf16[5,16,16,512]{3,2,1,0:T(8,128)(2,1)S(1)} %bitcast.40, bf16[27,512,512]{2,1,0:T(8,128)(2,1)S(1)} %bitcast.44), custom_call_target="tpu_custom_call" | custom-call | flops 6039797760 | bytes 4718592 | tf_op jit(solution)/shard_map/near/pallas_call | solution.py:172
  76.0 1.6 collective-permute-done.14.refs_1_
  77.6 0.1 collective-permute-done.15.refs_2_
  77.7 3.4 %collective-permute-start.16 = (bf16[384,1152]{1,0:T(8,128)(2,1)}, bf16[384,1152]{1,0:T(8,128)(2,1)}, u32[]{:S(2)}, u32[]{:S(2)}) collective-permute-start(bf16[384,1152]{1,0:T(8,128)(2,1)} %collective-permute-done.14.refs_1_), channel_id=1, source_target_pairs={{0,2},{2,4},{4,6},{6,7},{7,5},{5,3},{3,1},{1,0},{8,10},{10,12},{12... | collective-permute-start | bytes 2654216 | tf_op jit(solution)/shard_map/ppermute | solution.py:36
  81.1 1.2 collective-permute-start.17
  82.3 0.2 collective-permute-start.6
  82.5 8.4 %collective-permute-done.12.refs_6_ = bf16[4,5,8,3072]{3,2,1,0:T(8,128)(2,1)} collective-permute-done((bf16[4,5,8,3072]{3,2,1,0:T(8,128)(2,1)S(1)}, bf16[4,5,8,3072]{3,2,1,0:T(8,128)(2,1)}, u32[]{:S(2)}, u32[]{:S(2)}) %collective-permute-start.12) | collective-permute-done | bytes 983072 | tf_op jit(solution)/shard_map/ppermute | solution.py:18
  91.0 19.2 %lagged.1 = (bf16[5,16,16,512]{3,2,1,0:T(8,128)(2,1)}, bf16[1280,16]{1,0:T(8,128)(2,1)S(1)}) custom-call(s32[1]{0:T(128)S(6)} %copy.61.length_ref, bf16[2,16,16,512]{3,2,1,0:T(8,128)(2,1)S(1)} %copy-done.10, bf16[5,16,16,512]{3,2,1,0:T(8,128)(2,1)S(1)} %bitcast.41, bf16[27,512,512]{2,1,0:T(8,128)(2,1)} %bitcast.43, ...), custom_call_target="tpu_custom_call" | custom-call | flops 12079595520 | bytes 9437184 | tf_op jit(solution)/shard_map/lagged/pallas_call | solution.py:182
  110.2 0.0 copy-start.7
  110.2 0.2 copy.60
  110.5 0.2 reshape.95
  110.7 0.8 broadcast_in_dim.15
  111.5 12.9 %all-to-all-start = ((bf16[32,5,8,65]{3,2,1,0:T(8,128)(2,1)}), bf16[32,5,8,65]{3,2,1,0:T(8,128)(2,1)S(1)}, u32[]{:S(2)}, u32[]{:S(2)}) async-start(bf16[32,5,8,65]{3,2,1,0:T(8,128)(2,1)} %bitcast.8), calls=%async_computation | async-start | bytes 655360 | tf_op jit(solution)/shard_map/all_to_all | solution.py:447
  124.5 12.0 %all-to-all-done = bf16[32,5,8,65]{3,2,1,0:T(8,128)(2,1)S(1)} async-done(((bf16[32,5,8,65]{3,2,1,0:T(8,128)(2,1)}), bf16[32,5,8,65]{3,2,1,0:T(8,128)(2,1)S(1)}, u32[]{:S(2)}, u32[]{:S(2)}) %all-to-all-start) | async-done | bytes 166432 | tf_op jit(solution)/shard_map/all_to_all | solution.py:447
  136.5 0.1 slice.25
  136.6 0.9 collective-permute-start.18
  137.5 1.1 collective-permute-start.19
  138.6 0.1 convert_reduce_fusion
  138.7 0.1 iota_compare_fusion.1
  138.8 0.1 and_or_fusion
  138.9 0.0 copy-start.3
  139.0 1.2 copy-done.3
  140.2 1.0 copy-done.4
  141.2 16.8 %norm.1 = bf16[4,8,5,8,3072]{4,3,2,1,0:T(8,128)(2,1)} custom-call(bf16[1280,65]{1,0:T(8,128)(2,1)S(1)} %bitcast.37, bf16[64,3072]{1,0:T(8,128)(2,1)S(1)} %copy-done.4, f32[1,3072]{1,0:T(1,128)S(1)} %bitcast.42, bf16[4,5,8,3072]{3,2,1,0:T(8,128)(2,1)S(1)} %pad_maximum_fusion.refs_0_, bf16[4,5,8,3072]{3,2,1,0:T(8,128)(2,1)S(1)} %copy-done.3, ...), custom_call_target="tpu_custom_call" | custom-call | flops 4026531840 | bytes 15728640 | tf_op jit(solution)/shard_map/norm/pallas_call | solution.py:294
  158.0 0.1 collective-permute-done.18.refs_1_
  158.2 1.3 collective-permute-start.20
  159.5 1.0 collective-permute-start.21
  160.5 3.2 %copy-done = bf16[4,8,5,8,3072]{4,3,2,1,0:T(8,128)(2,1)S(1)} copy-done((bf16[4,8,5,8,3072]{4,3,2,1,0:T(8,128)(2,1)S(1)}, bf16[4,8,5,8,3072]{4,3,2,1,0:T(8,128)(2,1)}, u32[]{:S(2)}) %copy-start) | copy-done | bytes 7864344
  163.7 11.0 %qkv.3.refs_0_ = f32[1280,1152]{1,0:T(8,128)S(1)} custom-call(bf16[1280,3072]{1,0:T(8,128)(2,1)S(1)} %bitcast.31, bf16[384,1152]{1,0:T(8,128)(2,1)} %refs_0_.1, bf16[384,1152]{1,0:T(8,128)(2,1)} %collective-permute-done.14.refs_1_, bf16[384,1152]{1,0:T(8,128)(2,1)} %collective-permute-done.15.refs_2_, bf16[384,1152]{1,0:T(8,128)(2,1)} %collective-permute-done.16.refs_3_, ...), custom_call_target="tpu_custom_call" | custom-call | flops 5662310400 | bytes 7864320 | tf_op jit(solution)/shard_map/qkv/pallas_call | solution.py:357
  174.8 4.3 %qkv.4.refs_0_ = f32[1280,1152]{1,0:T(8,128)S(1)} custom-call(bf16[1280,3072]{1,0:T(8,128)(2,1)S(1)} %bitcast.32, f32[1280,1152]{1,0:T(8,128)S(1)} %qkv.3.refs_0_, bf16[384,1152]{1,0:T(8,128)(2,1)S(1)} %collective-permute-done.18.refs_1_, bf16[384,1152]{1,0:T(8,128)(2,1)S(1)} %collective-permute-done.19.refs_2_), custom_call_target="tpu_custom_call" | custom-call | flops 2264924160 | bytes 7864320 | tf_op jit(solution)/shard_map/qkv/pallas_call | solution.py:357
  179.1 2.8 %qkv.5 = bf16[1280,1152]{1,0:T(8,128)(2,1)S(1)} custom-call(bf16[1280,3072]{1,0:T(8,128)(2,1)S(1)} %bitcast.33, f32[1280,1152]{1,0:T(8,128)S(1)} %qkv.4.refs_0_, bf16[192,1152]{1,0:T(8,128)(2,1)S(1)} %collective-permute-done.20.refs_1_, bf16[192,1152]{1,0:T(8,128)(2,1)S(1)} %collective-permute-done.21.refs_2_), custom_call_target="tpu_custom_call" | custom-call | flops 1132462080 | bytes 7864320 | tf_op jit(solution)/shard_map/qkv/pallas_call | solution.py:357
  182.0 0.5 fusion.25
  182.5 2.4 %fusion.26 = (f32[4,8,3,40]{3,2,1,0:T(4,128)S(1)}, f32[4,8,3,40,40]{3,4,2,1,0:T(8,128)}) fusion(pred[4,40,40]{1,2,0:T(8,128)(4,1)S(1)} %and_or_fusion, bf16[4,40,8,3,128]{4,2,3,1,0:T(8,128)(2,1)S(1)} %get-tuple-element.24, bf16[4,40,8,3,128]{4,2,3,1,0:T(8,128)(2,1)S(1)} %get-tuple-element.23), kind=kOutput, calls=%fused_computation.26 | convolution fusion | flops 39936040 | bytes 2602240 | tf_op jit(solution)/shard_map/sub | solution.py:403
  184.8 2.3 %fusion.2 = bf16[4,40,8,3,128]{4,1,3,2,0:T(8,128)(2,1)S(1)} fusion(f32[4,8,3,40,40]{3,4,2,1,0:T(8,128)} %get-tuple-element.26, bf16[4,40,8,3,128]{4,2,3,1,0:T(8,128)(2,1)S(1)} %get-tuple-element.22, f32[4,8,3,40]{3,2,1,0:T(4,128)S(1)} %get-tuple-element.25), kind=kOutput, calls=%fused_computation.6 | convolution fusion | flops 40120320 | bytes 2595840 | tf_op jit(solution)/shard_map/gphts,gsphd->gtphd/dot_general | solution.py:405
  187.1 0.1 copy.30
  187.3 28.2 %all_to_all.10 = bf16[32,5,8,384]{3,2,1,0:T(8,128)(2,1)S(1)} all-to-all(bf16[32,5,8,384]{3,2,1,0:T(8,128)(2,1)S(1)} %bitcast.45), channel_id=1, replica_groups=mesh['dp'=4,'ctx'=8] {'dp','ctx'}, dimensions={0} | all-to-all | bytes 1966080 | tf_op jit(solution)/shard_map/all_to_all | solution.py:455
  215.4 0.8 copy.31
  216.2 1.3 reshape.102
  (36 shorter events, 0.2 us)
Async XLA Ops:
  0.6 1.5 copy-start.1
  2.3 12.3 %collective-permute-start.3 = (bf16[5,8,3072]{2,1,0:T(8,128)(2,1)S(1)}, bf16[5,8,3072]{2,1,0:T(8,128)(2,1)S(1)}, u32[]{:S(2)}, u32[]{:S(2)}) collective-permute-start(bf16[5,8,3072]{2,1,0:T(8,128)(2,1)S(1)} %get-tuple-element.17), channel_id=1, source_target_pairs={{0,6},{1,7},{2,0},{3,1},{4,2},{5,3},{6,4},{7,5},{8,14},{9,15},{10,... | collective-permute-start | bytes 737288 | tf_op jit(solution)/shard_map/ppermute | solution.py:234
  7.4 13.6 %collective-permute-start.2 = (bf16[5,8,3072]{2,1,0:T(8,128)(2,1)S(1)}, bf16[5,8,3072]{2,1,0:T(8,128)(2,1)S(1)}, u32[]{:S(2)}, u32[]{:S(2)}) collective-permute-start(bf16[5,8,3072]{2,1,0:T(8,128)(2,1)S(1)} %get-tuple-element.16), channel_id=1, source_target_pairs={{0,1},{1,2},{2,3},{3,4},{4,5},{5,6},{6,7},{7,0},{8,9},{9,10},{10,1... | collective-permute-start | bytes 737288 | tf_op jit(solution)/shard_map/ppermute | solution.py:234
  9.0 12.6 %collective-permute-start.1 = (bf16[5,8,3072]{2,1,0:T(8,128)(2,1)S(1)}, bf16[5,8,3072]{2,1,0:T(8,128)(2,1)S(1)}, u32[]{:S(2)}, u32[]{:S(2)}) collective-permute-start(bf16[5,8,3072]{2,1,0:T(8,128)(2,1)S(1)} %get-tuple-element.15), channel_id=1, source_target_pairs={{0,7},{1,0},{2,1},{3,2},{4,3},{5,4},{6,5},{7,6},{8,15},{9,8},{10,9... | collective-permute-start | bytes 737288 | tf_op jit(solution)/shard_map/ppermute | solution.py:234
  13.2 40.4 %collective-permute-start = (bf16[2,16,16,512]{3,2,1,0:T(8,128)(2,1)S(1)}, bf16[2,16,16,512]{3,2,1,0:T(8,128)(2,1)S(1)}, u32[]{:S(2)}, u32[]{:S(2)}) collective-permute-start(bf16[2,16,16,512]{3,2,1,0:T(8,128)(2,1)S(1)} %slice_bitcast_fusion), channel_id=1, source_target_pairs={{0,1},{1,2},{2,3},{3,4},{4,5},{5,6},{6,7},{8,9},{9,10},{10,11},{11... | collective-permute-start | bytes 1572872 | tf_op jit(solution)/shard_map/ppermute | solution.py:419
  14.6 30.3 %collective-permute-start.10 = (bf16[5,8,3072]{2,1,0:T(8,128)(2,1)S(1)}, bf16[5,8,3072]{2,1,0:T(8,128)(2,1)S(1)}, u32[]{:S(2)}, u32[]{:S(2)}) collective-permute-start(bf16[5,8,3072]{2,1,0:T(8,128)(2,1)S(1)} %get-tuple-element.21), channel_id=1, source_target_pairs={{0,4},{1,5},{2,6},{3,7},{4,0},{5,1},{6,2},{7,3},{8,12},{9,13},{10,... | collective-permute-start | bytes 737288 | tf_op jit(solution)/shard_map/ppermute | solution.py:234
  14.7 31.5 %collective-permute-start.9 = (bf16[5,8,3072]{2,1,0:T(8,128)(2,1)S(1)}, bf16[5,8,3072]{2,1,0:T(8,128)(2,1)S(1)}, u32[]{:S(2)}, u32[]{:S(2)}) collective-permute-start(bf16[5,8,3072]{2,1,0:T(8,128)(2,1)S(1)} %get-tuple-element.20), channel_id=1, source_target_pairs={{0,3},{1,4},{2,5},{3,6},{4,7},{5,0},{6,1},{7,2},{8,11},{9,12},{10,... | collective-permute-start | bytes 737288 | tf_op jit(solution)/shard_map/ppermute | solution.py:234
  21.0 26.7 %collective-permute-start.8 = (bf16[5,8,3072]{2,1,0:T(8,128)(2,1)S(1)}, bf16[5,8,3072]{2,1,0:T(8,128)(2,1)S(1)}, u32[]{:S(2)}, u32[]{:S(2)}) collective-permute-start(bf16[5,8,3072]{2,1,0:T(8,128)(2,1)S(1)} %get-tuple-element.19), channel_id=1, source_target_pairs={{0,5},{1,6},{2,7},{3,0},{4,1},{5,2},{6,3},{7,4},{8,13},{9,14},{10,... | collective-permute-start | bytes 737288 | tf_op jit(solution)/shard_map/ppermute | solution.py:234
  21.6 26.1 %collective-permute-start.7 = (bf16[5,8,3072]{2,1,0:T(8,128)(2,1)S(1)}, bf16[5,8,3072]{2,1,0:T(8,128)(2,1)S(1)}, u32[]{:S(2)}, u32[]{:S(2)}) collective-permute-start(bf16[5,8,3072]{2,1,0:T(8,128)(2,1)S(1)} %get-tuple-element.18), channel_id=1, source_target_pairs={{0,2},{1,3},{2,4},{3,5},{4,6},{5,7},{6,0},{7,1},{8,10},{9,11},{10,... | collective-permute-start | bytes 737288 | tf_op jit(solution)/shard_map/ppermute | solution.py:234
  22.5 37.7 %copy-start.11 = (bf16[512,16]{0,1:T(8,128)(2,1)S(1)}, bf16[512,16]{0,1:T(8,128)(2,1)}, u32[]{:S(2)}) copy-start(bf16[512,16]{0,1:T(8,128)(2,1)} %param.12) | copy-start | bytes 49156
  44.9 36.2 %collective-permute-start.4 = (bf16[4,5,8,3072]{3,2,1,0:T(8,128)(2,1)S(1)}, bf16[4,5,8,3072]{3,2,1,0:T(8,128)(2,1)S(1)}, u32[]{:S(2)}, u32[]{:S(2)}) collective-permute-start(bf16[4,5,8,3072]{3,2,1,0:T(8,128)(2,1)S(1)} %pad_maximum_fusion.refs_0_), channel_id=1, source_target_pairs={{0,8},{8,0},{16,24},{24,16},{1,9},{9,1},{17,25},{25,17},{2,10},{10... | collective-permute-start | bytes 2949128 | tf_op jit(solution)/shard_map/ppermute | solution.py:18
  46.2 36.1 %collective-permute-start.5 = (bf16[4,5,8,3072]{3,2,1,0:T(8,128)(2,1)S(1)}, bf16[4,5,8,3072]{3,2,1,0:T(8,128)(2,1)}, u32[]{:S(2)}, u32[]{:S(2)}) collective-permute-start(bf16[4,5,8,3072]{3,2,1,0:T(8,128)(2,1)S(1)} %pad_maximum_fusion.refs_0_), channel_id=1, source_target_pairs={{0,16},{8,24},{16,0},{24,8},{1,17},{9,25},{17,1},{25,9},{2,18},{10... | collective-permute-start | bytes 2949128 | tf_op jit(solution)/shard_map/ppermute | solution.py:18
  47.8 43.1 %collective-permute-start.12 = (bf16[4,5,8,3072]{3,2,1,0:T(8,128)(2,1)S(1)}, bf16[4,5,8,3072]{3,2,1,0:T(8,128)(2,1)}, u32[]{:S(2)}, u32[]{:S(2)}) collective-permute-start(bf16[4,5,8,3072]{3,2,1,0:T(8,128)(2,1)S(1)} %pad_maximum_fusion.1.refs_4_), channel_id=1, source_target_pairs={{0,16},{8,24},{16,0},{24,8},{1,17},{9,25},{17,1},{25,9},{2,18},{10... | collective-permute-start | bytes 2949128 | tf_op jit(solution)/shard_map/ppermute | solution.py:18
  48.4 29.2 %collective-permute-start.14 = (bf16[384,1152]{1,0:T(8,128)(2,1)}, bf16[384,1152]{1,0:T(8,128)(2,1)}, u32[]{:S(2)}, u32[]{:S(2)}) collective-permute-start(bf16[384,1152]{1,0:T(8,128)(2,1)} %refs_0_.1), channel_id=1, source_target_pairs={{0,2},{2,4},{4,6},{6,7},{7,5},{5,3},{3,1},{1,0},{8,10},{10,12},{12... | collective-permute-start | bytes 2654216 | tf_op jit(solution)/shard_map/ppermute | solution.py:36
  53.6 0.8 copy-start.9
  54.4 23.2 %collective-permute-start.15 = (bf16[384,1152]{1,0:T(8,128)(2,1)}, bf16[384,1152]{1,0:T(8,128)(2,1)}, u32[]{:S(2)}, u32[]{:S(2)}) collective-permute-start(bf16[384,1152]{1,0:T(8,128)(2,1)} %refs_0_.1), channel_id=1, source_target_pairs={{2,0},{4,2},{6,4},{7,6},{5,7},{3,5},{1,3},{0,1},{10,8},{12,10},{14... | collective-permute-start | bytes 2654216 | tf_op jit(solution)/shard_map/ppermute | solution.py:37
  60.3 1.3 copy-start.5
  61.6 5.0 %copy-start.8 = (bf16[3,3,3,512,512]{4,3,2,1,0:T(8,128)(2,1)S(1)}, bf16[3,3,3,512,512]{4,3,2,1,0:T(8,128)(2,1)}, u32[]{:S(2)}) copy-start(bf16[3,3,3,512,512]{4,3,2,1,0:T(8,128)(2,1)} %param.11) | copy-start | bytes 42467332
  66.7 24.3 %copy-start.6 = (bf16[1,5,16,16,512]{4,3,2,1,0:T(8,128)(2,1)S(1)}, bf16[1,5,16,16,512]{4,3,2,1,0:T(8,128)(2,1)}, u32[]{:S(2)}) copy-start(bf16[1,5,16,16,512]{4,3,2,1,0:T(8,128)(2,1)} %param.8) | copy-start | bytes 3932164
  66.7 24.3 %copy-start.10 = (bf16[2,16,16,512]{3,2,1,0:T(8,128)(2,1)S(1)}, bf16[2,16,16,512]{3,2,1,0:T(8,128)(2,1)}, u32[]{:S(2)}) copy-start(bf16[2,16,16,512]{3,2,1,0:T(8,128)(2,1)} %copy-done.9) | copy-start | bytes 1572868
  77.6 61.3 %collective-permute-start.11 = (bf16[4,5,8,3072]{3,2,1,0:T(8,128)(2,1)S(1)}, bf16[4,5,8,3072]{3,2,1,0:T(8,128)(2,1)}, u32[]{:S(2)}, u32[]{:S(2)}) collective-permute-start(bf16[4,5,8,3072]{3,2,1,0:T(8,128)(2,1)S(1)} %pad_maximum_fusion.1.refs_4_), channel_id=1, source_target_pairs={{0,8},{8,0},{16,24},{24,16},{1,9},{9,1},{17,25},{25,17},{2,10},{10... | collective-permute-start | bytes 2949128 | tf_op jit(solution)/shard_map/ppermute | solution.py:18
  77.7 58.9 %collective-permute-start.16 = (bf16[384,1152]{1,0:T(8,128)(2,1)}, bf16[384,1152]{1,0:T(8,128)(2,1)}, u32[]{:S(2)}, u32[]{:S(2)}) collective-permute-start(bf16[384,1152]{1,0:T(8,128)(2,1)} %collective-permute-done.14.refs_1_), channel_id=1, source_target_pairs={{0,2},{2,4},{4,6},{6,7},{7,5},{5,3},{3,1},{1,0},{8,10},{10,12},{12... | collective-permute-start | bytes 2654216 | tf_op jit(solution)/shard_map/ppermute | solution.py:36
  81.1 29.1 %copy-start.2 = (bf16[4,5,8,3072]{3,2,1,0:T(8,128)(2,1)}, bf16[4,5,8,3072]{3,2,1,0:T(8,128)(2,1)S(1)}, u32[]{:S(2)}) copy-start(bf16[4,5,8,3072]{3,2,1,0:T(8,128)(2,1)S(1)} %collective-permute-done.4.refs_1_) | copy-start | bytes 2949124
  81.1 56.4 %collective-permute-start.17 = (bf16[384,1152]{1,0:T(8,128)(2,1)}, bf16[384,1152]{1,0:T(8,128)(2,1)}, u32[]{:S(2)}, u32[]{:S(2)}) collective-permute-start(bf16[384,1152]{1,0:T(8,128)(2,1)} %collective-permute-done.15.refs_2_), channel_id=1, source_target_pairs={{2,0},{4,2},{6,4},{7,6},{5,7},{3,5},{1,3},{0,1},{10,8},{12,10},{14... | collective-permute-start | bytes 2654216 | tf_op jit(solution)/shard_map/ppermute | solution.py:37
  82.3 56.6 %collective-permute-start.6 = (bf16[4,5,8,3072]{3,2,1,0:T(8,128)(2,1)}, bf16[4,5,8,3072]{3,2,1,0:T(8,128)(2,1)}, u32[]{:S(2)}, u32[]{:S(2)}) collective-permute-start(bf16[4,5,8,3072]{3,2,1,0:T(8,128)(2,1)} %collective-permute-done.5.refs_2_), channel_id=1, source_target_pairs={{0,8},{8,0},{16,24},{24,16},{1,9},{9,1},{17,25},{25,17},{2,10},{10... | collective-permute-start | bytes 2949128 | tf_op jit(solution)/shard_map/ppermute | solution.py:18
  91.0 48.0 %collective-permute-start.13 = (bf16[4,5,8,3072]{3,2,1,0:T(8,128)(2,1)}, bf16[4,5,8,3072]{3,2,1,0:T(8,128)(2,1)}, u32[]{:S(2)}, u32[]{:S(2)}) collective-permute-start(bf16[4,5,8,3072]{3,2,1,0:T(8,128)(2,1)} %collective-permute-done.12.refs_6_), channel_id=1, source_target_pairs={{0,8},{8,0},{16,24},{24,16},{1,9},{9,1},{17,25},{25,17},{2,10},{10... | collective-permute-start | bytes 2949128 | tf_op jit(solution)/shard_map/ppermute | solution.py:18
  110.2 28.7 %copy-start.7 = (f32[3072]{0:T(1024)S(1)}, f32[3072]{0:T(1024)}, u32[]{:S(2)}) copy-start(f32[3072]{0:T(1024)} %param.14) | copy-start | bytes 36868
  111.5 25.0 %all-to-all-start = ((bf16[32,5,8,65]{3,2,1,0:T(8,128)(2,1)}), bf16[32,5,8,65]{3,2,1,0:T(8,128)(2,1)S(1)}, u32[]{:S(2)}, u32[]{:S(2)}) async-start(bf16[32,5,8,65]{3,2,1,0:T(8,128)(2,1)} %bitcast.8), calls=%async_computation | async-start | bytes 655360 | tf_op jit(solution)/shard_map/all_to_all | solution.py:447
  136.6 21.5 %collective-permute-start.18 = (bf16[384,1152]{1,0:T(8,128)(2,1)}, bf16[384,1152]{1,0:T(8,128)(2,1)S(1)}, u32[]{:S(2)}, u32[]{:S(2)}) collective-permute-start(bf16[384,1152]{1,0:T(8,128)(2,1)} %collective-permute-done.16.refs_3_), channel_id=1, source_target_pairs={{0,2},{2,4},{4,6},{6,7},{7,5},{5,3},{3,1},{1,0},{8,10},{10,12},{12... | collective-permute-start | bytes 2654216 | tf_op jit(solution)/shard_map/ppermute | solution.py:36
  137.5 22.0 %collective-permute-start.19 = (bf16[384,1152]{1,0:T(8,128)(2,1)}, bf16[384,1152]{1,0:T(8,128)(2,1)S(1)}, u32[]{:S(2)}, u32[]{:S(2)}) collective-permute-start(bf16[384,1152]{1,0:T(8,128)(2,1)} %collective-permute-done.17.refs_4_), channel_id=1, source_target_pairs={{2,0},{4,2},{6,4},{7,6},{5,7},{3,5},{1,3},{0,1},{10,8},{12,10},{14... | collective-permute-start | bytes 2654216 | tf_op jit(solution)/shard_map/ppermute | solution.py:37
  138.9 1.2 copy-start.3
  140.2 1.0 copy-start.4
  158.2 20.9 %collective-permute-start.20 = (bf16[192,1152]{1,0:T(8,128)(2,1)S(1)}, bf16[192,1152]{1,0:T(8,128)(2,1)S(1)}, u32[]{:S(2)}, u32[]{:S(2)}) collective-permute-start(bf16[192,1152]{1,0:T(8,128)(2,1)S(1)} %slice.28), channel_id=1, source_target_pairs={{0,2},{2,4},{4,6},{6,7},{7,5},{5,3},{3,1},{1,0},{8,10},{10,12},{12... | collective-permute-start | bytes 1327112 | tf_op jit(solution)/shard_map/ppermute | solution.py:40
  159.5 19.6 %collective-permute-start.21 = (bf16[192,1152]{1,0:T(8,128)(2,1)S(1)}, bf16[192,1152]{1,0:T(8,128)(2,1)S(1)}, u32[]{:S(2)}, u32[]{:S(2)}) collective-permute-start(bf16[192,1152]{1,0:T(8,128)(2,1)S(1)} %slice.29), channel_id=1, source_target_pairs={{2,0},{4,2},{6,4},{7,6},{5,7},{3,5},{1,3},{0,1},{10,8},{12,10},{14... | collective-permute-start | bytes 1327112 | tf_op jit(solution)/shard_map/ppermute | solution.py:41
  160.5 3.2 %copy-start = (bf16[4,8,5,8,3072]{4,3,2,1,0:T(8,128)(2,1)S(1)}, bf16[4,8,5,8,3072]{4,3,2,1,0:T(8,128)(2,1)}, u32[]{:S(2)}) copy-start(bf16[4,8,5,8,3072]{4,3,2,1,0:T(8,128)(2,1)} %norm.1) | copy-start | bytes 23592964

commit v4 on v3

--- a/solution.py
+++ b/solution.py
@@ -256,28 +256,26 @@
     copies = [pltpu.make_async_copy(a, b, sems.at[i]) for i, (a, b) in enumerate(copies)]
     for copy in copies:
         copy.start()
-    tile = 256
-
-    @pl.loop(0, width // tile)
-    def _(i):
-        columns = pl.ds(pl.multiple_of(i * tile, tile), tile)
-        embedded[:, columns] = jnp.dot(
-            patches_ref[:, :patch_size], embed_ref[:, columns], preferred_element_type=jnp.float32
-        )
-
     for copy in copies:
         copy.wait()
-    block = f_dev * pos
-
-    @pl.loop(0, groups * n)
-    def _(i):
-        group, device = i // n, lax.rem(i, n)
-        rows = pl.ds(pl.multiple_of(i * block, pos), block)
-        stream = held[group, device].astype(jnp.float32).reshape(block, width)
-        value = embedded[rows] + stream
-        scale = lax.rsqrt(jnp.mean(value * value, axis=-1, keepdims=True) + 1e-06)
-        value = value * scale * gain_ref[...]
-        out_ref[group, device] = value.reshape(f_dev, pos, width).astype(jnp.bfloat16)
+    block, batch = f_dev * pos, embedded.shape[0]
+
+    @pl.loop(0, out_ref.shape[0] * n * block // batch)
+    def _(b):
+        rows = pl.ds(pl.multiple_of(b * batch, 16), batch)
+        embedded[...] = jnp.dot(
+            patches_ref[rows, :patch_size], embed_ref[...], preferred_element_type=jnp.float32
+        )
+
+        @pl.loop(0, batch // block)
+        def _(i):
+            spot = b * (batch // block) + i
+            group, device = spot // n, lax.rem(spot, n)
+            stream = held[group, device].astype(jnp.float32).reshape(block, width)
+            value = embedded[pl.ds(pl.multiple_of(i * block, 8), block)] + stream
+            scale = lax.rsqrt(jnp.mean(value * value, axis=-1, keepdims=True) + 1e-06)
+            value = value * scale * gain_ref[...]
+            out_ref[group, device] = value.reshape(f_dev, pos, width).astype(jnp.bfloat16)
 
 
 def norm_rows(patches, embed_weight, norm_gain, halves, parts, groups, n):
@@ -298,10 +296,10 @@
         out_specs=VMEM,
         scratch_shapes=[
             pltpu.VMEM((groups, n, f_dev, pos, width), jnp.bfloat16),
-            pltpu.VMEM((rows, width), jnp.float32),
+            pltpu.VMEM((rows // (2 * groups), width), jnp.float32),
             pltpu.SemaphoreType.DMA((groups * n,)),
         ],
-        compiler_params=pltpu.CompilerParams(vmem_limit_bytes=44 << 20),
+        compiler_params=pltpu.CompilerParams(vmem_limit_bytes=26 << 20),
         cost_estimate=pl.CostEstimate(
             flops=2 * rows * width * 512, bytes_accessed=4 * rows * width, transcendentals=0
         ),

time: 218 us -> 215 us (0.986)
  local copies, waits for them, and re-layouts: 19.4 us -> 15.2 us
  waiting for transfers between devices: 51.7 us -> 54.8 us
    unnamed x26 -> x20, local copies, waits for them, and re-layouts: 14.2 us -> 9.81 us
    ppermute x3, waiting for transfers between devices: 1.75 us -> 4.84 us  [gather_ring(): up = lax.ppermute(up, axis, ahead)]
  transfers between devices with their start and end apart: 23 -> 23, of which waited for: 8 -> 8; matrix products, arithmetic and copies ran while one was open for 1% -> 1% of each run, Pallas kernels for 28% -> 27%
where the time goes in v4:
time: 215 us; the launch traced here: 214 us
  Pallas kernels  61.8 us (29%)
  waiting for transfers between devices  54.8 us (25%)
  starting transfers between devices  47.8 us (22%)
  blocking collectives  28.2 us (13%)
  local copies, waits for them, and re-layouts  15.2 us (7%)
  matrix products  4.65 us (2%)
    ppermute x7, waiting for transfers between devices, to_owners(): lax.ppermute(pieces[k], 'ctx', [(i, (i + k) % n) for i in range(n)])  29.4 us
    all_to_all x1, blocking collectives, body(): lax.all_to_all(out.reshape(groups * n, f_dev, pos, heads * HD), ('dp', 'c...  28.2 us
    pallas_call x1, Pallas kernels, conv_section(): pl.pallas_call(lagged_kernel, out_shape=(jax.ShapeDtypeStruct(frames.shap...  19.2 us
    pallas_call x3, Pallas kernels, project(): pl.pallas_call(functools.partial(qkv_kernel, count, spots, total is not N...  18.2 us
    pallas_call x1, Pallas kernels, norm_rows(): pl.pallas_call(functools.partial(norm_kernel, halves, groups, embed_weigh...  15 us
    all_to_all x1, starting transfers between devices, body(): patches = lax.all_to_all(patches, ('dp', 'ctx'), 0, 0, tiled=True)  12.9 us
    all_to_all x1, waiting for transfers between devices, body(): patches = lax.all_to_all(patches, ('dp', 'ctx'), 0, 0, tiled=True)  12 us
    ppermute x7, starting transfers between devices, to_owners(): lax.ppermute(pieces[k], 'ctx', [(i, (i + k) % n) for i in range(n)])  11.9 us
  transfers between devices with their start and end apart: 23, of which 8 were waited for; matrix products, arithmetic and copies ran while one was open for 1% of the time, Pallas kernels for 27%

profile of v4, /device:TPU:0, one launch (start us, length us, event | category | flops | bytes accessed | tf_op | source)
XLA Modules:
  0.0 214.5 jit_solution(15353504208687265684)
XLA Ops:
  0.6 1.5 copy-done
  2.2 0.1 deal.1
  2.3 5.1 %collective-permute-start.3 = (bf16[5,8,3072]{2,1,0:T(8,128)(2,1)S(1)}, bf16[5,8,3072]{2,1,0:T(8,128)(2,1)S(1)}, u32[]{:S(2)}, u32[]{:S(2)}) collective-permute-start(bf16[5,8,3072]{2,1,0:T(8,128)(2,1)S(1)} %get-tuple-element.17), channel_id=1, source_target_pairs={{0,6},{1,7},{2,0},{3,1},{4,2},{5,3},{6,4},{7,5},{8,14},{9,15},{10,... | collective-permute-start | bytes 737288 | tf_op jit(solution)/shard_map/ppermute | solution.py:234
  7.4 1.5 collective-permute-start.2
  9.0 3.2 %collective-permute-start.1 = (bf16[5,8,3072]{2,1,0:T(8,128)(2,1)S(1)}, bf16[5,8,3072]{2,1,0:T(8,128)(2,1)S(1)}, u32[]{:S(2)}, u32[]{:S(2)}) collective-permute-start(bf16[5,8,3072]{2,1,0:T(8,128)(2,1)S(1)} %get-tuple-element.15), channel_id=1, source_target_pairs={{0,7},{1,0},{2,1},{3,2},{4,3},{5,4},{6,5},{7,6},{8,15},{9,8},{10,9... | collective-permute-start | bytes 737288 | tf_op jit(solution)/shard_map/ppermute | solution.py:234
  12.2 1.1 slice_bitcast_fusion
  13.2 1.3 collective-permute-start
  14.6 0.1 collective-permute-start.10
  14.6 0.0 collective-permute-done.3
  14.7 0.5 collective-permute-start.9
  15.2 5.8 %collective-permute-done.2 = bf16[5,8,3072]{2,1,0:T(8,128)(2,1)S(1)} collective-permute-done((bf16[5,8,3072]{2,1,0:T(8,128)(2,1)S(1)}, bf16[5,8,3072]{2,1,0:T(8,128)(2,1)S(1)}, u32[]{:S(2)}, u32[]{:S(2)}) %collective-permute-start.2) | collective-permute-done | bytes 245792 | tf_op jit(solution)/shard_map/ppermute | solution.py:234
  21.0 0.6 collective-permute-start.8
  21.6 0.0 collective-permute-done.1
  21.6 0.9 collective-permute-start.7
  22.5 0.1 pad_maximum_fusion.refs_0_
  22.6 22.3 %collective-permute-done.10 = bf16[5,8,3072]{2,1,0:T(8,128)(2,1)S(1)} collective-permute-done((bf16[5,8,3072]{2,1,0:T(8,128)(2,1)S(1)}, bf16[5,8,3072]{2,1,0:T(8,128)(2,1)S(1)}, u32[]{:S(2)}, u32[]{:S(2)}) %collective-permute-start.10) | collective-permute-done | bytes 245792 | tf_op jit(solution)/shard_map/ppermute | solution.py:234
  44.9 0.0 collective-permute-start.4
  44.9 1.3 collective-permute-done.9
  46.2 1.5 collective-permute-start.5
  47.7 0.1 pad_maximum_fusion.1.refs_4_
  47.8 0.6 collective-permute-start.12
  48.4 5.2 %collective-permute-start.14 = (bf16[384,1152]{1,0:T(8,128)(2,1)}, bf16[384,1152]{1,0:T(8,128)(2,1)}, u32[]{:S(2)}, u32[]{:S(2)}) collective-permute-start(bf16[384,1152]{1,0:T(8,128)(2,1)} %refs_0_.1), channel_id=1, source_target_pairs={{0,2},{2,4},{4,6},{6,7},{7,5},{5,3},{3,1},{1,0},{8,10},{10,12},{12... | collective-permute-start | bytes 2654216 | tf_op jit(solution)/shard_map/ppermute | solution.py:36
  53.6 0.8 copy-done.6
  54.4 5.1 %collective-permute-start.15 = (bf16[384,1152]{1,0:T(8,128)(2,1)}, bf16[384,1152]{1,0:T(8,128)(2,1)}, u32[]{:S(2)}, u32[]{:S(2)}) collective-permute-start(bf16[384,1152]{1,0:T(8,128)(2,1)} %refs_0_.1), channel_id=1, source_target_pairs={{2,0},{4,2},{6,4},{7,6},{5,7},{3,5},{1,3},{0,1},{10,8},{12,10},{14... | collective-permute-start | bytes 2654216 | tf_op jit(solution)/shard_map/ppermute | solution.py:37
  60.2 0.1 copy.23.latent_weight_ref
  60.3 0.0 copy-start.2
  60.3 1.3 copy-done.2
  61.6 5.0 %copy-done.5 = bf16[3,3,3,512,512]{4,3,2,1,0:T(8,128)(2,1)S(1)} copy-done((bf16[3,3,3,512,512]{4,3,2,1,0:T(8,128)(2,1)S(1)}, bf16[3,3,3,512,512]{4,3,2,1,0:T(8,128)(2,1)}, u32[]{:S(2)}) %copy-start.5) | copy-done | bytes 14155800
  66.7 9.3 %near.1.near_ref = f32[1280,512]{1,0:T(8,128)S(1)} custom-call(bf16[5,16,16,512]{3,2,1,0:T(8,128)(2,1)S(1)} %bitcast.40, bf16[27,512,512]{2,1,0:T(8,128)(2,1)S(1)} %bitcast.44), custom_call_target="tpu_custom_call" | custom-call | flops 6039797760 | bytes 4718592 | tf_op jit(solution)/shard_map/near/pallas_call | solution.py:172
  76.0 1.6 collective-permute-done.14.refs_1_
  77.6 0.1 collective-permute-done.15.refs_2_
  77.7 3.4 %collective-permute-start.16 = (bf16[384,1152]{1,0:T(8,128)(2,1)}, bf16[384,1152]{1,0:T(8,128)(2,1)}, u32[]{:S(2)}, u32[]{:S(2)}) collective-permute-start(bf16[384,1152]{1,0:T(8,128)(2,1)} %collective-permute-done.14.refs_1_), channel_id=1, source_target_pairs={{0,2},{2,4},{4,6},{6,7},{7,5},{5,3},{3,1},{1,0},{8,10},{10,12},{12... | collective-permute-start | bytes 2654216 | tf_op jit(solution)/shard_map/ppermute | solution.py:36
  81.1 1.2 collective-permute-start.17
  82.3 0.2 collective-permute-start.6
  82.5 8.4 %collective-permute-done.12.refs_6_ = bf16[4,5,8,3072]{3,2,1,0:T(8,128)(2,1)} collective-permute-done((bf16[4,5,8,3072]{3,2,1,0:T(8,128)(2,1)S(1)}, bf16[4,5,8,3072]{3,2,1,0:T(8,128)(2,1)}, u32[]{:S(2)}, u32[]{:S(2)}) %collective-permute-start.12) | collective-permute-done | bytes 983072 | tf_op jit(solution)/shard_map/ppermute | solution.py:18
  91.0 19.2 %lagged.1 = (bf16[5,16,16,512]{3,2,1,0:T(8,128)(2,1)}, bf16[1280,16]{1,0:T(8,128)(2,1)S(1)}) custom-call(s32[1]{0:T(128)S(6)} %copy.61.length_ref, bf16[2,16,16,512]{3,2,1,0:T(8,128)(2,1)S(1)} %copy-done.7, bf16[5,16,16,512]{3,2,1,0:T(8,128)(2,1)S(1)} %bitcast.41, bf16[27,512,512]{2,1,0:T(8,128)(2,1)} %bitcast.43, ...), custom_call_target="tpu_custom_call" | custom-call | flops 12079595520 | bytes 9437184 | tf_op jit(solution)/shard_map/lagged/pallas_call | solution.py:182
  110.2 0.0 copy-start.4
  110.2 0.2 copy.60
  110.5 0.2 reshape.95
  110.7 0.8 broadcast_in_dim.15
  111.5 12.9 %all-to-all-start = ((bf16[32,5,8,65]{3,2,1,0:T(8,128)(2,1)}), bf16[32,5,8,65]{3,2,1,0:T(8,128)(2,1)S(1)}, u32[]{:S(2)}, u32[]{:S(2)}) async-start(bf16[32,5,8,65]{3,2,1,0:T(8,128)(2,1)} %bitcast.47), calls=%async_computation | async-start | bytes 655360 | tf_op jit(solution)/shard_map/all_to_all | solution.py:445
  124.5 12.0 %all-to-all-done = bf16[32,5,8,65]{3,2,1,0:T(8,128)(2,1)S(1)} async-done(((bf16[32,5,8,65]{3,2,1,0:T(8,128)(2,1)}), bf16[32,5,8,65]{3,2,1,0:T(8,128)(2,1)S(1)}, u32[]{:S(2)}, u32[]{:S(2)}) %all-to-all-start) | async-done | bytes 166432 | tf_op jit(solution)/shard_map/all_to_all | solution.py:445
  136.5 0.1 slice.25
  136.6 0.9 collective-permute-start.18
  137.5 1.1 collective-permute-start.19
  138.6 0.1 convert_reduce_fusion
  138.7 0.1 iota_compare_fusion.1
  138.8 0.1 and_or_fusion
  138.9 0.0 copy-start.1
  139.0 1.0 copy-done.1
  139.9 15.0 %norm.1 = bf16[4,8,5,8,3072]{4,3,2,1,0:T(8,128)(2,1)S(1)} custom-call(bf16[1280,65]{1,0:T(8,128)(2,1)S(1)} %bitcast.37, bf16[64,3072]{1,0:T(8,128)(2,1)S(1)} %copy-done.1, f32[1,3072]{1,0:T(1,128)S(1)} %bitcast.42, bf16[4,5,8,3072]{3,2,1,0:T(8,128)(2,1)S(1)} %pad_maximum_fusion.refs_0_, bf16[4,5,8,3072]{3,2,1,0:T(8,128)(2,1)S(1)} %collective-permute-done.4.refs_1_, ...), custom_call_target="tpu_custom_call" | custom-call | flops 4026531840 | bytes 15728640 | tf_op jit(solution)/shard_map/norm/pallas_call | solution.py:292
  154.9 3.2 %collective-permute-done.18.refs_1_ = bf16[384,1152]{1,0:T(8,128)(2,1)S(1)} collective-permute-done((bf16[384,1152]{1,0:T(8,128)(2,1)}, bf16[384,1152]{1,0:T(8,128)(2,1)S(1)}, u32[]{:S(2)}, u32[]{:S(2)}) %collective-permute-start.18) | collective-permute-done | bytes 884768 | tf_op jit(solution)/shard_map/ppermute | solution.py:36
  158.1 1.3 collective-permute-start.20
  159.5 1.0 collective-permute-start.21
  160.5 11.0 %qkv.3.refs_0_ = f32[1280,1152]{1,0:T(8,128)S(1)} custom-call(bf16[1280,3072]{1,0:T(8,128)(2,1)S(1)} %bitcast.31, bf16[384,1152]{1,0:T(8,128)(2,1)} %refs_0_.1, bf16[384,1152]{1,0:T(8,128)(2,1)} %collective-permute-done.14.refs_1_, bf16[384,1152]{1,0:T(8,128)(2,1)} %collective-permute-done.15.refs_2_, bf16[384,1152]{1,0:T(8,128)(2,1)} %collective-permute-done.16.refs_3_, ...), custom_call_target="tpu_custom_call" | custom-call | flops 5662310400 | bytes 7864320 | tf_op jit(solution)/shard_map/qkv/pallas_call | solution.py:355
  171.5 4.3 %qkv.4.refs_0_ = f32[1280,1152]{1,0:T(8,128)S(1)} custom-call(bf16[1280,3072]{1,0:T(8,128)(2,1)S(1)} %bitcast.32, f32[1280,1152]{1,0:T(8,128)S(1)} %qkv.3.refs_0_, bf16[384,1152]{1,0:T(8,128)(2,1)S(1)} %collective-permute-done.18.refs_1_, bf16[384,1152]{1,0:T(8,128)(2,1)S(1)} %collective-permute-done.19.refs_2_), custom_call_target="tpu_custom_call" | custom-call | flops 2264924160 | bytes 7864320 | tf_op jit(solution)/shard_map/qkv/pallas_call | solution.py:355
  175.9 2.8 %qkv.5 = bf16[1280,1152]{1,0:T(8,128)(2,1)S(1)} custom-call(bf16[1280,3072]{1,0:T(8,128)(2,1)S(1)} %bitcast.33, f32[1280,1152]{1,0:T(8,128)S(1)} %qkv.4.refs_0_, bf16[192,1152]{1,0:T(8,128)(2,1)S(1)} %collective-permute-done.20.refs_1_, bf16[192,1152]{1,0:T(8,128)(2,1)S(1)} %collective-permute-done.21.refs_2_), custom_call_target="tpu_custom_call" | custom-call | flops 1132462080 | bytes 7864320 | tf_op jit(solution)/shard_map/qkv/pallas_call | solution.py:355
  178.7 0.7 fusion.25
  179.4 2.4 %fusion.26 = (f32[4,8,3,40]{3,2,1,0:T(4,128)S(1)}, f32[4,8,3,40,40]{3,4,2,1,0:T(8,128)}) fusion(pred[4,40,40]{1,2,0:T(8,128)(4,1)S(1)} %and_or_fusion, bf16[4,40,8,3,128]{4,2,3,1,0:T(8,128)(2,1)S(1)} %get-tuple-element.24, bf16[4,40,8,3,128]{4,2,3,1,0:T(8,128)(2,1)S(1)} %get-tuple-element.23), kind=kOutput, calls=%fused_computation.26 | convolution fusion | flops 39936040 | bytes 2602240 | tf_op jit(solution)/shard_map/sub | solution.py:401
  181.8 2.3 %fusion.2 = bf16[4,40,8,3,128]{4,1,3,2,0:T(8,128)(2,1)S(1)} fusion(f32[4,8,3,40,40]{3,4,2,1,0:T(8,128)} %get-tuple-element.26, bf16[4,40,8,3,128]{4,2,3,1,0:T(8,128)(2,1)S(1)} %get-tuple-element.22, f32[4,8,3,40]{3,2,1,0:T(4,128)S(1)} %get-tuple-element.25), kind=kOutput, calls=%fused_computation.6 | convolution fusion | flops 40120320 | bytes 2595840 | tf_op jit(solution)/shard_map/gphts,gsphd->gtphd/dot_general | solution.py:403
  184.1 0.1 copy.30
  184.2 28.2 %all_to_all.10 = bf16[32,5,8,384]{3,2,1,0:T(8,128)(2,1)S(1)} all-to-all(bf16[32,5,8,384]{3,2,1,0:T(8,128)(2,1)S(1)} %bitcast.45), channel_id=1, replica_groups=mesh['dp'=4,'ctx'=8] {'dp','ctx'}, dimensions={0} | all-to-all | bytes 1966080 | tf_op jit(solution)/shard_map/all_to_all | solution.py:453
  212.4 0.8 copy.31
  213.2 1.3 reshape.102
  (30 shorter events, 0.2 us)
Async XLA Ops:
  0.6 1.5 copy-start
  2.3 12.3 %collective-permute-start.3 = (bf16[5,8,3072]{2,1,0:T(8,128)(2,1)S(1)}, bf16[5,8,3072]{2,1,0:T(8,128)(2,1)S(1)}, u32[]{:S(2)}, u32[]{:S(2)}) collective-permute-start(bf16[5,8,3072]{2,1,0:T(8,128)(2,1)S(1)} %get-tuple-element.17), channel_id=1, source_target_pairs={{0,6},{1,7},{2,0},{3,1},{4,2},{5,3},{6,4},{7,5},{8,14},{9,15},{10,... | collective-permute-start | bytes 737288 | tf_op jit(solution)/shard_map/ppermute | solution.py:234
  7.4 13.6 %collective-permute-start.2 = (bf16[5,8,3072]{2,1,0:T(8,128)(2,1)S(1)}, bf16[5,8,3072]{2,1,0:T(8,128)(2,1)S(1)}, u32[]{:S(2)}, u32[]{:S(2)}) collective-permute-start(bf16[5,8,3072]{2,1,0:T(8,128)(2,1)S(1)} %get-tuple-element.16), channel_id=1, source_target_pairs={{0,1},{1,2},{2,3},{3,4},{4,5},{5,6},{6,7},{7,0},{8,9},{9,10},{10,1... | collective-permute-start | bytes 737288 | tf_op jit(solution)/shard_map/ppermute | solution.py:234
  9.0 12.6 %collective-permute-start.1 = (bf16[5,8,3072]{2,1,0:T(8,128)(2,1)S(1)}, bf16[5,8,3072]{2,1,0:T(8,128)(2,1)S(1)}, u32[]{:S(2)}, u32[]{:S(2)}) collective-permute-start(bf16[5,8,3072]{2,1,0:T(8,128)(2,1)S(1)} %get-tuple-element.15), channel_id=1, source_target_pairs={{0,7},{1,0},{2,1},{3,2},{4,3},{5,4},{6,5},{7,6},{8,15},{9,8},{10,9... | collective-permute-start | bytes 737288 | tf_op jit(solution)/shard_map/ppermute | solution.py:234
  13.2 40.4 %collective-permute-start = (bf16[2,16,16,512]{3,2,1,0:T(8,128)(2,1)S(1)}, bf16[2,16,16,512]{3,2,1,0:T(8,128)(2,1)S(1)}, u32[]{:S(2)}, u32[]{:S(2)}) collective-permute-start(bf16[2,16,16,512]{3,2,1,0:T(8,128)(2,1)S(1)} %slice_bitcast_fusion), channel_id=1, source_target_pairs={{0,1},{1,2},{2,3},{3,4},{4,5},{5,6},{6,7},{8,9},{9,10},{10,11},{11... | collective-permute-start | bytes 1572872 | tf_op jit(solution)/shard_map/ppermute | solution.py:417
  14.6 30.3 %collective-permute-start.10 = (bf16[5,8,3072]{2,1,0:T(8,128)(2,1)S(1)}, bf16[5,8,3072]{2,1,0:T(8,128)(2,1)S(1)}, u32[]{:S(2)}, u32[]{:S(2)}) collective-permute-start(bf16[5,8,3072]{2,1,0:T(8,128)(2,1)S(1)} %get-tuple-element.21), channel_id=1, source_target_pairs={{0,4},{1,5},{2,6},{3,7},{4,0},{5,1},{6,2},{7,3},{8,12},{9,13},{10,... | collective-permute-start | bytes 737288 | tf_op jit(solution)/shard_map/ppermute | solution.py:234
  14.7 31.5 %collective-permute-start.9 = (bf16[5,8,3072]{2,1,0:T(8,128)(2,1)S(1)}, bf16[5,8,3072]{2,1,0:T(8,128)(2,1)S(1)}, u32[]{:S(2)}, u32[]{:S(2)}) collective-permute-start(bf16[5,8,3072]{2,1,0:T(8,128)(2,1)S(1)} %get-tuple-element.20), channel_id=1, source_target_pairs={{0,3},{1,4},{2,5},{3,6},{4,7},{5,0},{6,1},{7,2},{8,11},{9,12},{10,... | collective-permute-start | bytes 737288 | tf_op jit(solution)/shard_map/ppermute | solution.py:234
  21.0 26.7 %collective-permute-start.8 = (bf16[5,8,3072]{2,1,0:T(8,128)(2,1)S(1)}, bf16[5,8,3072]{2,1,0:T(8,128)(2,1)S(1)}, u32[]{:S(2)}, u32[]{:S(2)}) collective-permute-start(bf16[5,8,3072]{2,1,0:T(8,128)(2,1)S(1)} %get-tuple-element.19), channel_id=1, source_target_pairs={{0,5},{1,6},{2,7},{3,0},{4,1},{5,2},{6,3},{7,4},{8,13},{9,14},{10,... | collective-permute-start | bytes 737288 | tf_op jit(solution)/shard_map/ppermute | solution.py:234
  21.6 26.1 %collective-permute-start.7 = (bf16[5,8,3072]{2,1,0:T(8,128)(2,1)S(1)}, bf16[5,8,3072]{2,1,0:T(8,128)(2,1)S(1)}, u32[]{:S(2)}, u32[]{:S(2)}) collective-permute-start(bf16[5,8,3072]{2,1,0:T(8,128)(2,1)S(1)} %get-tuple-element.18), channel_id=1, source_target_pairs={{0,2},{1,3},{2,4},{3,5},{4,6},{5,7},{6,0},{7,1},{8,10},{9,11},{10,... | collective-permute-start | bytes 737288 | tf_op jit(solution)/shard_map/ppermute | solution.py:234
  22.5 37.7 %copy-start.8 = (bf16[512,16]{0,1:T(8,128)(2,1)S(1)}, bf16[512,16]{0,1:T(8,128)(2,1)}, u32[]{:S(2)}) copy-start(bf16[512,16]{0,1:T(8,128)(2,1)} %param.12) | copy-start | bytes 49156
  44.9 36.2 %collective-permute-start.4 = (bf16[4,5,8,3072]{3,2,1,0:T(8,128)(2,1)S(1)}, bf16[4,5,8,3072]{3,2,1,0:T(8,128)(2,1)S(1)}, u32[]{:S(2)}, u32[]{:S(2)}) collective-permute-start(bf16[4,5,8,3072]{3,2,1,0:T(8,128)(2,1)S(1)} %pad_maximum_fusion.refs_0_), channel_id=1, source_target_pairs={{0,8},{8,0},{16,24},{24,16},{1,9},{9,1},{17,25},{25,17},{2,10},{10... | collective-permute-start | bytes 2949128 | tf_op jit(solution)/shard_map/ppermute | solution.py:18
  46.2 36.1 %collective-permute-start.5 = (bf16[4,5,8,3072]{3,2,1,0:T(8,128)(2,1)S(1)}, bf16[4,5,8,3072]{3,2,1,0:T(8,128)(2,1)}, u32[]{:S(2)}, u32[]{:S(2)}) collective-permute-start(bf16[4,5,8,3072]{3,2,1,0:T(8,128)(2,1)S(1)} %pad_maximum_fusion.refs_0_), channel_id=1, source_target_pairs={{0,16},{8,24},{16,0},{24,8},{1,17},{9,25},{17,1},{25,9},{2,18},{10... | collective-permute-start | bytes 2949128 | tf_op jit(solution)/shard_map/ppermute | solution.py:18
  47.8 43.1 %collective-permute-start.12 = (bf16[4,5,8,3072]{3,2,1,0:T(8,128)(2,1)S(1)}, bf16[4,5,8,3072]{3,2,1,0:T(8,128)(2,1)}, u32[]{:S(2)}, u32[]{:S(2)}) collective-permute-start(bf16[4,5,8,3072]{3,2,1,0:T(8,128)(2,1)S(1)} %pad_maximum_fusion.1.refs_4_), channel_id=1, source_target_pairs={{0,16},{8,24},{16,0},{24,8},{1,17},{9,25},{17,1},{25,9},{2,18},{10... | collective-permute-start | bytes 2949128 | tf_op jit(solution)/shard_map/ppermute | solution.py:18
  48.4 29.2 %collective-permute-start.14 = (bf16[384,1152]{1,0:T(8,128)(2,1)}, bf16[384,1152]{1,0:T(8,128)(2,1)}, u32[]{:S(2)}, u32[]{:S(2)}) collective-permute-start(bf16[384,1152]{1,0:T(8,128)(2,1)} %refs_0_.1), channel_id=1, source_target_pairs={{0,2},{2,4},{4,6},{6,7},{7,5},{5,3},{3,1},{1,0},{8,10},{10,12},{12... | collective-permute-start | bytes 2654216 | tf_op jit(solution)/shard_map/ppermute | solution.py:36
  53.6 0.8 copy-start.6
  54.4 23.2 %collective-permute-start.15 = (bf16[384,1152]{1,0:T(8,128)(2,1)}, bf16[384,1152]{1,0:T(8,128)(2,1)}, u32[]{:S(2)}, u32[]{:S(2)}) collective-permute-start(bf16[384,1152]{1,0:T(8,128)(2,1)} %refs_0_.1), channel_id=1, source_target_pairs={{2,0},{4,2},{6,4},{7,6},{5,7},{3,5},{1,3},{0,1},{10,8},{12,10},{14... | collective-permute-start | bytes 2654216 | tf_op jit(solution)/shard_map/ppermute | solution.py:37
  60.3 1.3 copy-start.2
  61.6 5.0 %copy-start.5 = (bf16[3,3,3,512,512]{4,3,2,1,0:T(8,128)(2,1)S(1)}, bf16[3,3,3,512,512]{4,3,2,1,0:T(8,128)(2,1)}, u32[]{:S(2)}) copy-start(bf16[3,3,3,512,512]{4,3,2,1,0:T(8,128)(2,1)} %param.11) | copy-start | bytes 42467332
  66.7 24.3 %copy-start.3 = (bf16[1,5,16,16,512]{4,3,2,1,0:T(8,128)(2,1)S(1)}, bf16[1,5,16,16,512]{4,3,2,1,0:T(8,128)(2,1)}, u32[]{:S(2)}) copy-start(bf16[1,5,16,16,512]{4,3,2,1,0:T(8,128)(2,1)} %param.8) | copy-start | bytes 3932164
  66.7 24.3 %copy-start.7 = (bf16[2,16,16,512]{3,2,1,0:T(8,128)(2,1)S(1)}, bf16[2,16,16,512]{3,2,1,0:T(8,128)(2,1)}, u32[]{:S(2)}) copy-start(bf16[2,16,16,512]{3,2,1,0:T(8,128)(2,1)} %copy-done.6) | copy-start | bytes 1572868
  77.6 61.3 %collective-permute-start.11 = (bf16[4,5,8,3072]{3,2,1,0:T(8,128)(2,1)S(1)}, bf16[4,5,8,3072]{3,2,1,0:T(8,128)(2,1)}, u32[]{:S(2)}, u32[]{:S(2)}) collective-permute-start(bf16[4,5,8,3072]{3,2,1,0:T(8,128)(2,1)S(1)} %pad_maximum_fusion.1.refs_4_), channel_id=1, source_target_pairs={{0,8},{8,0},{16,24},{24,16},{1,9},{9,1},{17,25},{25,17},{2,10},{10... | collective-permute-start | bytes 2949128 | tf_op jit(solution)/shard_map/ppermute | solution.py:18
  77.7 58.9 %collective-permute-start.16 = (bf16[384,1152]{1,0:T(8,128)(2,1)}, bf16[384,1152]{1,0:T(8,128)(2,1)}, u32[]{:S(2)}, u32[]{:S(2)}) collective-permute-start(bf16[384,1152]{1,0:T(8,128)(2,1)} %collective-permute-done.14.refs_1_), channel_id=1, source_target_pairs={{0,2},{2,4},{4,6},{6,7},{7,5},{5,3},{3,1},{1,0},{8,10},{10,12},{12... | collective-permute-start | bytes 2654216 | tf_op jit(solution)/shard_map/ppermute | solution.py:36
  81.1 56.4 %collective-permute-start.17 = (bf16[384,1152]{1,0:T(8,128)(2,1)}, bf16[384,1152]{1,0:T(8,128)(2,1)}, u32[]{:S(2)}, u32[]{:S(2)}) collective-permute-start(bf16[384,1152]{1,0:T(8,128)(2,1)} %collective-permute-done.15.refs_2_), channel_id=1, source_target_pairs={{2,0},{4,2},{6,4},{7,6},{5,7},{3,5},{1,3},{0,1},{10,8},{12,10},{14... | collective-permute-start | bytes 2654216 | tf_op jit(solution)/shard_map/ppermute | solution.py:37
  82.3 56.6 %collective-permute-start.6 = (bf16[4,5,8,3072]{3,2,1,0:T(8,128)(2,1)}, bf16[4,5,8,3072]{3,2,1,0:T(8,128)(2,1)}, u32[]{:S(2)}, u32[]{:S(2)}) collective-permute-start(bf16[4,5,8,3072]{3,2,1,0:T(8,128)(2,1)} %collective-permute-done.5.refs_2_), channel_id=1, source_target_pairs={{0,8},{8,0},{16,24},{24,16},{1,9},{9,1},{17,25},{25,17},{2,10},{10... | collective-permute-start | bytes 2949128 | tf_op jit(solution)/shard_map/ppermute | solution.py:18
  91.0 48.0 %collective-permute-start.13 = (bf16[4,5,8,3072]{3,2,1,0:T(8,128)(2,1)}, bf16[4,5,8,3072]{3,2,1,0:T(8,128)(2,1)}, u32[]{:S(2)}, u32[]{:S(2)}) collective-permute-start(bf16[4,5,8,3072]{3,2,1,0:T(8,128)(2,1)} %collective-permute-done.12.refs_6_), channel_id=1, source_target_pairs={{0,8},{8,0},{16,24},{24,16},{1,9},{9,1},{17,25},{25,17},{2,10},{10... | collective-permute-start | bytes 2949128 | tf_op jit(solution)/shard_map/ppermute | solution.py:18
  110.2 28.7 %copy-start.4 = (f32[3072]{0:T(1024)S(1)}, f32[3072]{0:T(1024)}, u32[]{:S(2)}) copy-start(f32[3072]{0:T(1024)} %param.14) | copy-start | bytes 36868
  111.5 25.0 %all-to-all-start = ((bf16[32,5,8,65]{3,2,1,0:T(8,128)(2,1)}), bf16[32,5,8,65]{3,2,1,0:T(8,128)(2,1)S(1)}, u32[]{:S(2)}, u32[]{:S(2)}) async-start(bf16[32,5,8,65]{3,2,1,0:T(8,128)(2,1)} %bitcast.47), calls=%async_computation | async-start | bytes 655360 | tf_op jit(solution)/shard_map/all_to_all | solution.py:445
  136.6 21.5 %collective-permute-start.18 = (bf16[384,1152]{1,0:T(8,128)(2,1)}, bf16[384,1152]{1,0:T(8,128)(2,1)S(1)}, u32[]{:S(2)}, u32[]{:S(2)}) collective-permute-start(bf16[384,1152]{1,0:T(8,128)(2,1)} %collective-permute-done.16.refs_3_), channel_id=1, source_target_pairs={{0,2},{2,4},{4,6},{6,7},{7,5},{5,3},{3,1},{1,0},{8,10},{10,12},{12... | collective-permute-start | bytes 2654216 | tf_op jit(solution)/shard_map/ppermute | solution.py:36
  137.5 22.0 %collective-permute-start.19 = (bf16[384,1152]{1,0:T(8,128)(2,1)}, bf16[384,1152]{1,0:T(8,128)(2,1)S(1)}, u32[]{:S(2)}, u32[]{:S(2)}) collective-permute-start(bf16[384,1152]{1,0:T(8,128)(2,1)} %collective-permute-done.17.refs_4_), channel_id=1, source_target_pairs={{2,0},{4,2},{6,4},{7,6},{5,7},{3,5},{1,3},{0,1},{10,8},{12,10},{14... | collective-permute-start | bytes 2654216 | tf_op jit(solution)/shard_map/ppermute | solution.py:37
  138.9 1.0 copy-start.1
  158.1 17.7 %collective-permute-start.20 = (bf16[192,1152]{1,0:T(8,128)(2,1)S(1)}, bf16[192,1152]{1,0:T(8,128)(2,1)S(1)}, u32[]{:S(2)}, u32[]{:S(2)}) collective-permute-start(bf16[192,1152]{1,0:T(8,128)(2,1)S(1)} %slice.28), channel_id=1, source_target_pairs={{0,2},{2,4},{4,6},{6,7},{7,5},{5,3},{3,1},{1,0},{8,10},{10,12},{12... | collective-permute-start | bytes 1327112 | tf_op jit(solution)/shard_map/ppermute | solution.py:40
  159.5 16.4 %collective-permute-start.21 = (bf16[192,1152]{1,0:T(8,128)(2,1)S(1)}, bf16[192,1152]{1,0:T(8,128)(2,1)S(1)}, u32[]{:S(2)}, u32[]{:S(2)}) collective-permute-start(bf16[192,1152]{1,0:T(8,128)(2,1)S(1)} %slice.29), channel_id=1, source_target_pairs={{2,0},{4,2},{6,4},{7,6},{5,7},{3,5},{1,3},{0,1},{10,8},{12,10},{14... | collective-permute-start | bytes 1327112 | tf_op jit(solution)/shard_map/ppermute | solution.py:41

commit v5 on v4

--- a/solution.py
+++ b/solution.py
@@ -30,15 +30,17 @@
     cycle = list(range(0, count, 2)) + list(range(count - 1, 0, -2))
     ahead = [(cycle[r], cycle[(r + 1) % count]) for r in range(count)]
     behind = [(b, a) for a, b in ahead]
+    half = block.shape[0] // 2
     pieces = [block]
-    up = down = block
+    ups = downs = (block[:half], block[half:])
     for _ in range(1, count // 2):
-        up = lax.ppermute(up, axis, ahead)
-        down = lax.ppermute(down, axis, behind)
-        pieces += [up, down]
-    half = block.shape[0] // 2
-    pieces.append(lax.ppermute(up[:half], axis, ahead))
-    pieces.append(lax.ppermute(down[half:], axis, behind))
+        moved = []
+        for up, down in zip(ups, downs):
+            moved.append((lax.ppermute(up, axis, ahead), lax.ppermute(down, axis, behind)))
+        ups, downs = zip(*moved)
+        pieces += [*ups, *downs]
+    pieces.append(lax.ppermute(ups[0], axis, ahead))
+    pieces.append(lax.ppermute(downs[1], axis, behind))
     return pieces
 
 
@@ -54,9 +56,8 @@
 
     first = [me * rows]
     for step in range(1, count // 2):
-        first += [owner(-step), owner(step)]
-    far = owner(count // 2)
-    return first + [far, far + rows // 2]
+        first += [owner(-step)] * 2 + [owner(step)] * 2
+    return first + [owner(count // 2)] * 2
 
 
 def load_taps(weight_ref, weights, sems, first):
@@ -375,10 +376,10 @@
     if not count:
         return project(normed, pieces, count, ((0,),), None, True)
     last = len(pieces) - 2
-    early = max(1, last - 2)
-    stages = [tuple((i,) for i in range(early))]
+    early = max(1, last - 4)
+    stages = [((0,), *((i, i + 1) for i in range(1, early, 2)))]
     if early < last:
-        stages.append(tuple((i,) for i in range(early, last)))
+        stages.append(tuple((i, i + 1) for i in range(early, last, 2)))
     stages.append(((last, last + 1),))
     total = None
     for s, spots in enumerate(stages):

time: 215 us -> 233 us (1.084)
  starting transfers between devices: 47.8 us -> 61.5 us
  local copies, waits for them, and re-layouts: 15.2 us -> 17.9 us
    ppermute x8 -> x14, starting transfers between devices: 19.3 us -> 29.6 us  [the longest x6 16.4 us: gather_ring(): lax.ppermute(up, axis, ahead)]
    ppermute x6, waiting for transfers between devices: 8.46 us -> 0.02 us  [flip(): return lax.ppermute(value, axis, [(i, i ^ bit) for i in range(count)])]
    ppermute x8 -> x14, waiting for transfers between devices: 4.91 us -> 10.9 us  [the longest x6 10.9 us: gather_ring(): lax.ppermute(up, axis, ahead)]
    ppermute x1, waiting for transfers between devices: 0.01 us -> 4.72 us  [body(): lax.ppermute(frames[0, f_dev - 2:], 'ctx', [(i, i + 1) for i in range(n -...]
    ppermute x7, waiting for transfers between devices: 29.4 us -> 25.9 us  [to_owners(): lax.ppermute(pieces[k], 'ctx', [(i, (i + k) % n) for i in range(n)])]
    ppermute x7, starting transfers between devices: 11.9 us -> 15.2 us  [to_owners(): lax.ppermute(pieces[k], 'ctx', [(i, (i + k) % n) for i in range(n)])]
    all_to_all x1, starting transfers between devices: 12.9 us -> 9.91 us  [body(): patches = lax.all_to_all(patches, ('dp', 'ctx'), 0, 0, tiled=True)]
    unnamed x20 -> x40, local copies, waits for them, and re-layouts: 9.81 us -> 9.07 us
  transfers between devices with their start and end apart: 23 -> 29, of which waited for: 8 -> 7; matrix products, arithmetic and copies ran while one was open for 1% -> 3% of each run, Pallas kernels for 27% -> 26%
where the time goes in v5:
time: 233 us
  Pallas kernels  64 us (27%)
  starting transfers between devices  61.5 us (26%)
  waiting for transfers between devices  53.6 us (23%)
  blocking collectives  28.7 us (12%)
  local copies, waits for them, and re-layouts  17.9 us (8%)
  matrix products  4.66 us (2%)
    all_to_all x1, blocking collectives, body(): lax.all_to_all(out.reshape(groups * n, f_dev, pos, heads * HD), ('dp', 'c...  28.7 us
    ppermute x7, waiting for transfers between devices, to_owners(): lax.ppermute(pieces[k], 'ctx', [(i, (i + k) % n) for i in range(n)])  25.9 us
    pallas_call x1, Pallas kernels, conv_section(): pl.pallas_call(lagged_kernel, out_shape=(jax.ShapeDtypeStruct(frames.shap...  20.3 us
    pallas_call x3, Pallas kernels, project(): pl.pallas_call(functools.partial(qkv_kernel, count, spots, total is not N...  19.2 us
    ppermute x6, starting transfers between devices, gather_ring(): lax.ppermute(up, axis, ahead)  16.4 us
    ppermute x7, starting transfers between devices, to_owners(): lax.ppermute(pieces[k], 'ctx', [(i, (i + k) % n) for i in range(n)])  15.2 us
    pallas_call x1, Pallas kernels, norm_rows(): pl.pallas_call(functools.partial(norm_kernel, halves, groups, embed_weigh...  15.1 us
    all_to_all x1, waiting for transfers between devices, body(): patches = lax.all_to_all(patches, ('dp', 'ctx'), 0, 0, tiled=True)  12 us
  transfers between devices with their start and end apart: 29, of which 7 were waited for; matrix products, arithmetic and copies ran while one was open for 3% of the time, Pallas kernels for 26%

profile of v5, /device:TPU:0, one launch (start us, length us, event | category | flops | bytes accessed | tf_op | source)
XLA Modules:
  0.0 232.6 jit_solution(9450504288485751791)
XLA Ops:
  0.6 1.5 copy-done
  2.2 0.1 deal.1
  2.3 5.1 %collective-permute-start.3 = (bf16[5,8,3072]{2,1,0:T(8,128)(2,1)S(1)}, bf16[5,8,3072]{2,1,0:T(8,128)(2,1)S(1)}, u32[]{:S(2)}, u32[]{:S(2)}) collective-permute-start(bf16[5,8,3072]{2,1,0:T(8,128)(2,1)S(1)} %get-tuple-element.17), channel_id=1, source_target_pairs={{0,6},{1,7},{2,0},{3,1},{4,2},{5,3},{6,4},{7,5},{8,14},{9,15},{10,... | collective-permute-start | bytes 737288 | tf_op jit(solution)/shard_map/ppermute | solution.py:235
  7.4 1.5 collective-permute-start.2
  9.0 3.2 %collective-permute-start.1 = (bf16[5,8,3072]{2,1,0:T(8,128)(2,1)S(1)}, bf16[5,8,3072]{2,1,0:T(8,128)(2,1)S(1)}, u32[]{:S(2)}, u32[]{:S(2)}) collective-permute-start(bf16[5,8,3072]{2,1,0:T(8,128)(2,1)S(1)} %get-tuple-element.15), channel_id=1, source_target_pairs={{0,7},{1,0},{2,1},{3,2},{4,3},{5,4},{6,5},{7,6},{8,15},{9,8},{10,9... | collective-permute-start | bytes 737288 | tf_op jit(solution)/shard_map/ppermute | solution.py:235
  12.2 0.6 collective-permute-start.9
  12.7 1.0 fusion.26
  13.7 1.9 slice_bitcast_fusion
  15.6 3.3 %collective-permute-start.8 = (bf16[5,8,3072]{2,1,0:T(8,128)(2,1)S(1)}, bf16[5,8,3072]{2,1,0:T(8,128)(2,1)S(1)}, u32[]{:S(2)}, u32[]{:S(2)}) collective-permute-start(bf16[5,8,3072]{2,1,0:T(8,128)(2,1)S(1)} %get-tuple-element.19), channel_id=1, source_target_pairs={{0,5},{1,6},{2,7},{3,0},{4,1},{5,2},{6,3},{7,4},{8,13},{9,14},{10,... | collective-permute-start | bytes 737288 | tf_op jit(solution)/shard_map/ppermute | solution.py:235
  18.8 2.2 collective-permute-done.2
  21.0 1.5 collective-permute-start.7
  22.5 5.6 %collective-permute-done.1 = bf16[5,8,3072]{2,1,0:T(8,128)(2,1)S(1)} collective-permute-done((bf16[5,8,3072]{2,1,0:T(8,128)(2,1)S(1)}, bf16[5,8,3072]{2,1,0:T(8,128)(2,1)S(1)}, u32[]{:S(2)}, u32[]{:S(2)}) %collective-permute-start.1) | collective-permute-done | bytes 245792 | tf_op jit(solution)/shard_map/ppermute | solution.py:235
  28.1 18.1 %collective-permute-done.10 = bf16[5,8,3072]{2,1,0:T(8,128)(2,1)S(1)} collective-permute-done((bf16[5,8,3072]{2,1,0:T(8,128)(2,1)S(1)}, bf16[5,8,3072]{2,1,0:T(8,128)(2,1)S(1)}, u32[]{:S(2)}, u32[]{:S(2)}) %collective-permute-start.10) | collective-permute-done | bytes 245792 | tf_op jit(solution)/shard_map/ppermute | solution.py:235
  46.2 0.1 pad_maximum_fusion.refs_0_
  46.4 2.1 collective-permute-start.16
  48.4 4.5 %collective-permute-start.17 = (bf16[192,1152]{1,0:T(8,128)(2,1)}, bf16[192,1152]{1,0:T(8,128)(2,1)}, u32[]{:S(2)}, u32[]{:S(2)}) collective-permute-start(bf16[192,1152]{1,0:T(8,128)(2,1)} %get-tuple-element.25), channel_id=1, source_target_pairs={{2,0},{4,2},{6,4},{7,6},{5,7},{3,5},{1,3},{0,1},{10,8},{12,10},{14... | collective-permute-start | bytes 1327112 | tf_op jit(solution)/shard_map/ppermute | solution.py:39
  53.0 2.7 %collective-permute-start = (bf16[2,16,16,512]{3,2,1,0:T(8,128)(2,1)}, bf16[2,16,16,512]{3,2,1,0:T(8,128)(2,1)}, u32[]{:S(2)}, u32[]{:S(2)}) collective-permute-start(bf16[2,16,16,512]{3,2,1,0:T(8,128)(2,1)} %slice_bitcast_fusion), channel_id=1, source_target_pairs={{0,1},{1,2},{2,3},{3,4},{4,5},{5,6},{6,7},{8,9},{9,10},{10,11},{11... | collective-permute-start | bytes 1572872 | tf_op jit(solution)/shard_map/ppermute | solution.py:418
  55.7 0.1 pad_maximum_fusion.1.refs_4_
  55.8 1.6 collective-permute-start.5
  57.4 0.8 collective-permute-done.15.refs_2_
  58.2 1.5 collective-permute-start.12
  60.3 0.1 copy.23.latent_weight_ref
  60.5 12.0 %collective-permute-start.18 = (bf16[192,1152]{1,0:T(8,128)(2,1)S(1)}, bf16[192,1152]{1,0:T(8,128)(2,1)S(1)}, u32[]{:S(2)}, u32[]{:S(2)}) collective-permute-start(bf16[192,1152]{1,0:T(8,128)(2,1)S(1)} %collective-permute-done.14.refs_1_), channel_id=1, source_target_pairs={{0,2},{2,4},{4,6},{6,7},{7,5},{5,3},{3,1},{1,0},{8,10},{10,12},{12... | collective-permute-start | bytes 1327112 | tf_op jit(solution)/shard_map/ppermute | solution.py:39
  72.5 2.4 %collective-permute-start.19 = (bf16[192,1152]{1,0:T(8,128)(2,1)}, bf16[192,1152]{1,0:T(8,128)(2,1)S(1)}, u32[]{:S(2)}, u32[]{:S(2)}) collective-permute-start(bf16[192,1152]{1,0:T(8,128)(2,1)} %copy-done.10), channel_id=1, source_target_pairs={{0,2},{2,4},{4,6},{6,7},{7,5},{5,3},{3,1},{1,0},{8,10},{10,12},{12... | collective-permute-start | bytes 1327112 | tf_op jit(solution)/shard_map/ppermute | solution.py:39
  74.9 4.7 %collective-permute-done.past_ref = bf16[2,16,16,512]{3,2,1,0:T(8,128)(2,1)} collective-permute-done((bf16[2,16,16,512]{3,2,1,0:T(8,128)(2,1)}, bf16[2,16,16,512]{3,2,1,0:T(8,128)(2,1)}, u32[]{:S(2)}, u32[]{:S(2)}) %collective-permute-start) | collective-permute-done | bytes 524320 | tf_op jit(solution)/shard_map/ppermute | solution.py:418
  79.6 2.5 %collective-permute-start.20 = (bf16[192,1152]{1,0:T(8,128)(2,1)}, bf16[192,1152]{1,0:T(8,128)(2,1)S(1)}, u32[]{:S(2)}, u32[]{:S(2)}) collective-permute-start(bf16[192,1152]{1,0:T(8,128)(2,1)} %collective-permute-done.16.refs_3_), channel_id=1, source_target_pairs={{2,0},{4,2},{6,4},{7,6},{5,7},{3,5},{1,3},{0,1},{10,8},{12,10},{14... | collective-permute-start | bytes 1327112 | tf_op jit(solution)/shard_map/ppermute | solution.py:39
  82.1 1.3 copy-done.4
  83.4 5.0 %copy-done.7 = bf16[3,3,3,512,512]{4,3,2,1,0:T(8,128)(2,1)S(1)} copy-done((bf16[3,3,3,512,512]{4,3,2,1,0:T(8,128)(2,1)S(1)}, bf16[3,3,3,512,512]{4,3,2,1,0:T(8,128)(2,1)}, u32[]{:S(2)}) %copy-start.7) | copy-done | bytes 14155800
  88.5 9.3 %near.1.near_ref = f32[1280,512]{1,0:T(8,128)S(1)} custom-call(bf16[5,16,16,512]{3,2,1,0:T(8,128)(2,1)S(1)} %bitcast.40, bf16[27,512,512]{2,1,0:T(8,128)(2,1)S(1)} %bitcast.44), custom_call_target="tpu_custom_call" | custom-call | flops 6039797760 | bytes 4718592 | tf_op jit(solution)/shard_map/near/pallas_call | solution.py:173
  97.8 0.0 copy-start.12
  97.8 0.1 collective-permute-start.4
  97.9 0.5 collective-permute-start.11
  98.4 0.2 collective-permute-start.6
  98.6 0.4 collective-permute-start.13
  99.0 20.3 %lagged.1 = (bf16[5,16,16,512]{3,2,1,0:T(8,128)(2,1)}, bf16[1280,16]{1,0:T(8,128)(2,1)S(1)}) custom-call(s32[1]{0:T(128)S(6)} %copy.61.length_ref, bf16[2,16,16,512]{3,2,1,0:T(8,128)(2,1)} %collective-permute-done.past_ref, bf16[5,16,16,512]{3,2,1,0:T(8,128)(2,1)S(1)} %bitcast.41, bf16[27,512,512]{2,1,0:T(8,128)(2,1)} %bitcast.43, ...), custom_call_target="tpu_custom_call" | custom-call | flops 12079595520 | bytes 9437184 | tf_op jit(solution)/shard_map/lagged/pallas_call | solution.py:183
  119.3 0.0 copy-start.6
  119.3 1.0 copy.60
  120.3 1.2 reshape.95
  121.5 0.8 broadcast_in_dim.15
  122.3 9.9 %all-to-all-start = ((bf16[32,5,8,65]{3,2,1,0:T(8,128)(2,1)}), bf16[32,5,8,65]{3,2,1,0:T(8,128)(2,1)S(1)}, u32[]{:S(2)}, u32[]{:S(2)}) async-start(bf16[32,5,8,65]{3,2,1,0:T(8,128)(2,1)} %bitcast.47), calls=%async_computation | async-start | bytes 655360 | tf_op jit(solution)/shard_map/all_to_all | solution.py:446
  132.2 12.0 %all-to-all-done = bf16[32,5,8,65]{3,2,1,0:T(8,128)(2,1)S(1)} async-done(((bf16[32,5,8,65]{3,2,1,0:T(8,128)(2,1)}), bf16[32,5,8,65]{3,2,1,0:T(8,128)(2,1)S(1)}, u32[]{:S(2)}, u32[]{:S(2)}) %all-to-all-start) | async-done | bytes 166432 | tf_op jit(solution)/shard_map/all_to_all | solution.py:446
  144.2 0.1 slice.25
  144.4 0.1 convert_reduce_fusion
  144.5 1.0 collective-permute-start.22
  145.5 1.1 collective-permute-start.25
  146.6 0.1 iota_compare_fusion.1
  146.6 0.1 and_or_fusion
  146.8 1.0 collective-permute-start.23
  147.7 10.1 %collective-permute-done.22.refs_1_ = bf16[192,1152]{1,0:T(8,128)(2,1)S(1)} collective-permute-done((bf16[192,1152]{1,0:T(8,128)(2,1)}, bf16[192,1152]{1,0:T(8,128)(2,1)S(1)}, u32[]{:S(2)}, u32[]{:S(2)}) %collective-permute-start.22) | collective-permute-done | bytes 442400 | tf_op jit(solution)/shard_map/ppermute | solution.py:39
  157.8 1.0 collective-permute-start.24
  158.8 1.0 collective-permute-start.26
  159.8 1.0 collective-permute-start.27
  160.8 1.0 copy-done.3
  161.8 15.1 %norm.1 = bf16[4,8,5,8,3072]{4,3,2,1,0:T(8,128)(2,1)S(1)} custom-call(bf16[1280,65]{1,0:T(8,128)(2,1)S(1)} %bitcast.37, bf16[64,3072]{1,0:T(8,128)(2,1)S(1)} %copy-done.3, f32[1,3072]{1,0:T(1,128)S(1)} %bitcast.42, bf16[4,5,8,3072]{3,2,1,0:T(8,128)(2,1)S(1)} %pad_maximum_fusion.refs_0_, bf16[4,5,8,3072]{3,2,1,0:T(8,128)(2,1)} %collective-permute-done.4.refs_1_, ...), custom_call_target="tpu_custom_call" | custom-call | flops 4026531840 | bytes 15728640 | tf_op jit(solution)/shard_map/norm/pallas_call | solution.py:293
  177.0 11.4 %qkv.3.refs_0_ = f32[1280,1152]{1,0:T(8,128)S(1)} custom-call(bf16[1280,3072]{1,0:T(8,128)(2,1)S(1)} %bitcast.31, bf16[384,1152]{1,0:T(8,128)(2,1)S(1)} %copy-done.2, bf16[192,1152]{1,0:T(8,128)(2,1)S(1)} %copy-done.9, bf16[192,1152]{1,0:T(8,128)(2,1)S(1)} %copy-done.11, bf16[192,1152]{1,0:T(8,128)(2,1)} %collective-permute-done.16.refs_3_, ...), custom_call_target="tpu_custom_call" | custom-call | flops 5662310400 | bytes 7864320 | tf_op jit(solution)/shard_map/qkv/pallas_call | solution.py:356
  188.4 5.0 %qkv.4.refs_0_ = f32[1280,1152]{1,0:T(8,128)S(1)} custom-call(bf16[1280,3072]{1,0:T(8,128)(2,1)S(1)} %bitcast.32, f32[1280,1152]{1,0:T(8,128)S(1)} %qkv.3.refs_0_, bf16[192,1152]{1,0:T(8,128)(2,1)S(1)} %collective-permute-done.22.refs_1_, bf16[192,1152]{1,0:T(8,128)(2,1)S(1)} %collective-permute-done.23.refs_2_, ...), custom_call_target="tpu_custom_call" | custom-call | flops 2264924160 | bytes 7864320 | tf_op jit(solution)/shard_map/qkv/pallas_call | solution.py:356
  193.4 2.8 %qkv.5 = bf16[1280,1152]{1,0:T(8,128)(2,1)S(1)} custom-call(bf16[1280,3072]{1,0:T(8,128)(2,1)S(1)} %bitcast.33, f32[1280,1152]{1,0:T(8,128)S(1)} %qkv.4.refs_0_, bf16[192,1152]{1,0:T(8,128)(2,1)S(1)} %collective-permute-done.26.refs_1_, bf16[192,1152]{1,0:T(8,128)(2,1)S(1)} %collective-permute-done.27.refs_2_), custom_call_target="tpu_custom_call" | custom-call | flops 1132462080 | bytes 7864320 | tf_op jit(solution)/shard_map/qkv/pallas_call | solution.py:356
  196.3 0.7 fusion.25
  197.0 2.4 %fusion.27 = (f32[4,8,3,40]{3,2,1,0:T(4,128)S(1)}, f32[4,8,3,40,40]{3,4,2,1,0:T(8,128)}) fusion(pred[4,40,40]{1,2,0:T(8,128)(4,1)S(1)} %and_or_fusion, bf16[4,40,8,3,128]{4,2,3,1,0:T(8,128)(2,1)S(1)} %get-tuple-element.24, bf16[4,40,8,3,128]{4,2,3,1,0:T(8,128)(2,1)S(1)} %get-tuple-element.23), kind=kOutput, calls=%fused_computation.27 | convolution fusion | flops 39936040 | bytes 2602240 | tf_op jit(solution)/shard_map/sub | solution.py:402
  199.4 2.3 fusion.2
  201.6 0.1 copy.30
  201.8 28.7 %all_to_all.10 = bf16[32,5,8,384]{3,2,1,0:T(8,128)(2,1)S(1)} all-to-all(bf16[32,5,8,384]{3,2,1,0:T(8,128)(2,1)S(1)} %bitcast.45), channel_id=1, replica_groups=mesh['dp'=4,'ctx'=8] {'dp','ctx'}, dimensions={0} | all-to-all | bytes 1966080 | tf_op jit(solution)/shard_map/all_to_all | solution.py:454
  230.5 0.8 copy.31
  231.3 1.3 reshape.102
  (61 shorter events, 0.2 us)
Async XLA Ops:
  0.6 1.5 copy-start
  2.2 10.6 %copy-start.1 = (bf16[384,1152]{1,0:T(8,128)(2,1)S(1)}, bf16[384,1152]{1,0:T(8,128)(2,1)}, u32[]{:S(2)}) copy-start(bf16[384,1152]{1,0:T(8,128)(2,1)} %refs_0_.1) | copy-start | bytes 2654212
  2.3 13.3 %collective-permute-start.3 = (bf16[5,8,3072]{2,1,0:T(8,128)(2,1)S(1)}, bf16[5,8,3072]{2,1,0:T(8,128)(2,1)S(1)}, u32[]{:S(2)}, u32[]{:S(2)}) collective-permute-start(bf16[5,8,3072]{2,1,0:T(8,128)(2,1)S(1)} %get-tuple-element.17), channel_id=1, source_target_pairs={{0,6},{1,7},{2,0},{3,1},{4,2},{5,3},{6,4},{7,5},{8,14},{9,15},{10,... | collective-permute-start | bytes 737288 | tf_op jit(solution)/shard_map/ppermute | solution.py:235
  7.4 13.6 %collective-permute-start.2 = (bf16[5,8,3072]{2,1,0:T(8,128)(2,1)S(1)}, bf16[5,8,3072]{2,1,0:T(8,128)(2,1)S(1)}, u32[]{:S(2)}, u32[]{:S(2)}) collective-permute-start(bf16[5,8,3072]{2,1,0:T(8,128)(2,1)S(1)} %get-tuple-element.16), channel_id=1, source_target_pairs={{0,1},{1,2},{2,3},{3,4},{4,5},{5,6},{6,7},{7,0},{8,9},{9,10},{10,1... | collective-permute-start | bytes 737288 | tf_op jit(solution)/shard_map/ppermute | solution.py:235
  9.0 19.1 %collective-permute-start.1 = (bf16[5,8,3072]{2,1,0:T(8,128)(2,1)S(1)}, bf16[5,8,3072]{2,1,0:T(8,128)(2,1)S(1)}, u32[]{:S(2)}, u32[]{:S(2)}) collective-permute-start(bf16[5,8,3072]{2,1,0:T(8,128)(2,1)S(1)} %get-tuple-element.15), channel_id=1, source_target_pairs={{0,7},{1,0},{2,1},{3,2},{4,3},{5,4},{6,5},{7,6},{8,15},{9,8},{10,9... | collective-permute-start | bytes 737288 | tf_op jit(solution)/shard_map/ppermute | solution.py:235
  12.2 34.1 %collective-permute-start.10 = (bf16[5,8,3072]{2,1,0:T(8,128)(2,1)S(1)}, bf16[5,8,3072]{2,1,0:T(8,128)(2,1)S(1)}, u32[]{:S(2)}, u32[]{:S(2)}) collective-permute-start(bf16[5,8,3072]{2,1,0:T(8,128)(2,1)S(1)} %get-tuple-element.21), channel_id=1, source_target_pairs={{0,4},{1,5},{2,6},{3,7},{4,0},{5,1},{6,2},{7,3},{8,12},{9,13},{10,... | collective-permute-start | bytes 737288 | tf_op jit(solution)/shard_map/ppermute | solution.py:235
  12.2 34.2 %collective-permute-start.9 = (bf16[5,8,3072]{2,1,0:T(8,128)(2,1)S(1)}, bf16[5,8,3072]{2,1,0:T(8,128)(2,1)S(1)}, u32[]{:S(2)}, u32[]{:S(2)}) collective-permute-start(bf16[5,8,3072]{2,1,0:T(8,128)(2,1)S(1)} %get-tuple-element.20), channel_id=1, source_target_pairs={{0,3},{1,4},{2,5},{3,6},{4,7},{5,0},{6,1},{7,2},{8,11},{9,12},{10,... | collective-permute-start | bytes 737288 | tf_op jit(solution)/shard_map/ppermute | solution.py:235
  15.6 32.9 %collective-permute-start.8 = (bf16[5,8,3072]{2,1,0:T(8,128)(2,1)S(1)}, bf16[5,8,3072]{2,1,0:T(8,128)(2,1)S(1)}, u32[]{:S(2)}, u32[]{:S(2)}) collective-permute-start(bf16[5,8,3072]{2,1,0:T(8,128)(2,1)S(1)} %get-tuple-element.19), channel_id=1, source_target_pairs={{0,5},{1,6},{2,7},{3,0},{4,1},{5,2},{6,3},{7,4},{8,13},{9,14},{10,... | collective-permute-start | bytes 737288 | tf_op jit(solution)/shard_map/ppermute | solution.py:235
  21.0 32.0 %collective-permute-start.7 = (bf16[5,8,3072]{2,1,0:T(8,128)(2,1)S(1)}, bf16[5,8,3072]{2,1,0:T(8,128)(2,1)S(1)}, u32[]{:S(2)}, u32[]{:S(2)}) collective-permute-start(bf16[5,8,3072]{2,1,0:T(8,128)(2,1)S(1)} %get-tuple-element.18), channel_id=1, source_target_pairs={{0,2},{1,3},{2,4},{3,5},{4,6},{5,7},{6,0},{7,1},{8,10},{9,11},{10,... | collective-permute-start | bytes 737288 | tf_op jit(solution)/shard_map/ppermute | solution.py:235
  28.1 27.7 %collective-permute-start.14 = (bf16[192,1152]{1,0:T(8,128)(2,1)}, bf16[192,1152]{1,0:T(8,128)(2,1)S(1)}, u32[]{:S(2)}, u32[]{:S(2)}) collective-permute-start(bf16[192,1152]{1,0:T(8,128)(2,1)} %get-tuple-element.26), channel_id=1, source_target_pairs={{0,2},{2,4},{4,6},{6,7},{7,5},{5,3},{3,1},{1,0},{8,10},{10,12},{12... | collective-permute-start | bytes 1327112 | tf_op jit(solution)/shard_map/ppermute | solution.py:39
  46.2 12.0 %collective-permute-start.15 = (bf16[192,1152]{1,0:T(8,128)(2,1)}, bf16[192,1152]{1,0:T(8,128)(2,1)S(1)}, u32[]{:S(2)}, u32[]{:S(2)}) collective-permute-start(bf16[192,1152]{1,0:T(8,128)(2,1)} %get-tuple-element.25), channel_id=1, source_target_pairs={{0,2},{2,4},{4,6},{6,7},{7,5},{5,3},{3,1},{1,0},{8,10},{10,12},{12... | collective-permute-start | bytes 1327112 | tf_op jit(solution)/shard_map/ppermute | solution.py:39
  46.2 14.1 %copy-start.18 = (bf16[512,16]{0,1:T(8,128)(2,1)S(1)}, bf16[512,16]{0,1:T(8,128)(2,1)}, u32[]{:S(2)}) copy-start(bf16[512,16]{0,1:T(8,128)(2,1)} %param.12) | copy-start | bytes 49156
  46.4 14.1 %collective-permute-start.16 = (bf16[192,1152]{1,0:T(8,128)(2,1)}, bf16[192,1152]{1,0:T(8,128)(2,1)}, u32[]{:S(2)}, u32[]{:S(2)}) collective-permute-start(bf16[192,1152]{1,0:T(8,128)(2,1)} %get-tuple-element.26), channel_id=1, source_target_pairs={{2,0},{4,2},{6,4},{7,6},{5,7},{3,5},{1,3},{0,1},{10,8},{12,10},{14... | collective-permute-start | bytes 1327112 | tf_op jit(solution)/shard_map/ppermute | solution.py:39
  48.4 24.1 %collective-permute-start.17 = (bf16[192,1152]{1,0:T(8,128)(2,1)}, bf16[192,1152]{1,0:T(8,128)(2,1)}, u32[]{:S(2)}, u32[]{:S(2)}) collective-permute-start(bf16[192,1152]{1,0:T(8,128)(2,1)} %get-tuple-element.25), channel_id=1, source_target_pairs={{2,0},{4,2},{6,4},{7,6},{5,7},{3,5},{1,3},{0,1},{10,8},{12,10},{14... | collective-permute-start | bytes 1327112 | tf_op jit(solution)/shard_map/ppermute | solution.py:39
  53.0 26.7 %collective-permute-start = (bf16[2,16,16,512]{3,2,1,0:T(8,128)(2,1)}, bf16[2,16,16,512]{3,2,1,0:T(8,128)(2,1)}, u32[]{:S(2)}, u32[]{:S(2)}) collective-permute-start(bf16[2,16,16,512]{3,2,1,0:T(8,128)(2,1)} %slice_bitcast_fusion), channel_id=1, source_target_pairs={{0,1},{1,2},{2,3},{3,4},{4,5},{5,6},{6,7},{8,9},{9,10},{10,11},{11... | collective-permute-start | bytes 1572872 | tf_op jit(solution)/shard_map/ppermute | solution.py:418
  55.8 41.9 %copy-start.8 = (bf16[192,1152]{1,0:T(8,128)(2,1)}, bf16[192,1152]{1,0:T(8,128)(2,1)S(1)}, u32[]{:S(2)}) copy-start(bf16[192,1152]{1,0:T(8,128)(2,1)S(1)} %collective-permute-done.14.refs_1_) | copy-start | bytes 1327108
  55.8 42.6 %collective-permute-start.5 = (bf16[4,5,8,3072]{3,2,1,0:T(8,128)(2,1)S(1)}, bf16[4,5,8,3072]{3,2,1,0:T(8,128)(2,1)S(1)}, u32[]{:S(2)}, u32[]{:S(2)}) collective-permute-start(bf16[4,5,8,3072]{3,2,1,0:T(8,128)(2,1)S(1)} %pad_maximum_fusion.refs_0_), channel_id=1, source_target_pairs={{0,16},{8,24},{16,0},{24,8},{1,17},{9,25},{17,1},{25,9},{2,18},{10... | collective-permute-start | bytes 2949128 | tf_op jit(solution)/shard_map/ppermute | solution.py:18
  58.2 1.5 copy-start.10
  58.2 40.4 %collective-permute-start.12 = (bf16[4,5,8,3072]{3,2,1,0:T(8,128)(2,1)S(1)}, bf16[4,5,8,3072]{3,2,1,0:T(8,128)(2,1)}, u32[]{:S(2)}, u32[]{:S(2)}) collective-permute-start(bf16[4,5,8,3072]{3,2,1,0:T(8,128)(2,1)S(1)} %pad_maximum_fusion.1.refs_4_), channel_id=1, source_target_pairs={{0,16},{8,24},{16,0},{24,8},{1,17},{9,25},{17,1},{25,9},{2,18},{10... | collective-permute-start | bytes 2949128 | tf_op jit(solution)/shard_map/ppermute | solution.py:18
  60.5 37.3 %collective-permute-start.18 = (bf16[192,1152]{1,0:T(8,128)(2,1)S(1)}, bf16[192,1152]{1,0:T(8,128)(2,1)S(1)}, u32[]{:S(2)}, u32[]{:S(2)}) collective-permute-start(bf16[192,1152]{1,0:T(8,128)(2,1)S(1)} %collective-permute-done.14.refs_1_), channel_id=1, source_target_pairs={{0,2},{2,4},{4,6},{6,7},{7,5},{5,3},{3,1},{1,0},{8,10},{10,12},{12... | collective-permute-start | bytes 1327112 | tf_op jit(solution)/shard_map/ppermute | solution.py:39
  72.5 25.3 %collective-permute-start.19 = (bf16[192,1152]{1,0:T(8,128)(2,1)}, bf16[192,1152]{1,0:T(8,128)(2,1)S(1)}, u32[]{:S(2)}, u32[]{:S(2)}) collective-permute-start(bf16[192,1152]{1,0:T(8,128)(2,1)} %copy-done.10), channel_id=1, source_target_pairs={{0,2},{2,4},{4,6},{6,7},{7,5},{5,3},{3,1},{1,0},{8,10},{10,12},{12... | collective-permute-start | bytes 1327112 | tf_op jit(solution)/shard_map/ppermute | solution.py:39
  79.6 18.7 %collective-permute-start.20 = (bf16[192,1152]{1,0:T(8,128)(2,1)}, bf16[192,1152]{1,0:T(8,128)(2,1)S(1)}, u32[]{:S(2)}, u32[]{:S(2)}) collective-permute-start(bf16[192,1152]{1,0:T(8,128)(2,1)} %collective-permute-done.16.refs_3_), channel_id=1, source_target_pairs={{2,0},{4,2},{6,4},{7,6},{5,7},{3,5},{1,3},{0,1},{10,8},{12,10},{14... | collective-permute-start | bytes 1327112 | tf_op jit(solution)/shard_map/ppermute | solution.py:39
  82.1 1.3 copy-start.4
  83.4 5.0 %copy-start.7 = (bf16[3,3,3,512,512]{4,3,2,1,0:T(8,128)(2,1)S(1)}, bf16[3,3,3,512,512]{4,3,2,1,0:T(8,128)(2,1)}, u32[]{:S(2)}) copy-start(bf16[3,3,3,512,512]{4,3,2,1,0:T(8,128)(2,1)} %param.11) | copy-start | bytes 42467332
  88.5 10.5 %copy-start.5 = (bf16[1,5,16,16,512]{4,3,2,1,0:T(8,128)(2,1)S(1)}, bf16[1,5,16,16,512]{4,3,2,1,0:T(8,128)(2,1)}, u32[]{:S(2)}) copy-start(bf16[1,5,16,16,512]{4,3,2,1,0:T(8,128)(2,1)} %param.8) | copy-start | bytes 3932164
  97.8 21.5 %copy-start.12 = (bf16[192,1152]{1,0:T(8,128)(2,1)}, bf16[192,1152]{1,0:T(8,128)(2,1)S(1)}, u32[]{:S(2)}) copy-start(bf16[192,1152]{1,0:T(8,128)(2,1)S(1)} %collective-permute-done.18.refs_5_) | copy-start | bytes 1327108
  97.8 47.7 %collective-permute-start.4 = (bf16[4,5,8,3072]{3,2,1,0:T(8,128)(2,1)S(1)}, bf16[4,5,8,3072]{3,2,1,0:T(8,128)(2,1)}, u32[]{:S(2)}, u32[]{:S(2)}) collective-permute-start(bf16[4,5,8,3072]{3,2,1,0:T(8,128)(2,1)S(1)} %pad_maximum_fusion.refs_0_), channel_id=1, source_target_pairs={{0,8},{8,0},{16,24},{24,16},{1,9},{9,1},{17,25},{25,17},{2,10},{10... | collective-permute-start | bytes 2949128 | tf_op jit(solution)/shard_map/ppermute | solution.py:18
  97.9 21.4 %copy-start.14 = (bf16[192,1152]{1,0:T(8,128)(2,1)}, bf16[192,1152]{1,0:T(8,128)(2,1)S(1)}, u32[]{:S(2)}) copy-start(bf16[192,1152]{1,0:T(8,128)(2,1)S(1)} %collective-permute-done.19.refs_6_) | copy-start | bytes 1327108
  97.9 48.9 %collective-permute-start.11 = (bf16[4,5,8,3072]{3,2,1,0:T(8,128)(2,1)S(1)}, bf16[4,5,8,3072]{3,2,1,0:T(8,128)(2,1)}, u32[]{:S(2)}, u32[]{:S(2)}) collective-permute-start(bf16[4,5,8,3072]{3,2,1,0:T(8,128)(2,1)S(1)} %pad_maximum_fusion.1.refs_4_), channel_id=1, source_target_pairs={{0,8},{8,0},{16,24},{24,16},{1,9},{9,1},{17,25},{25,17},{2,10},{10... | collective-permute-start | bytes 2949128 | tf_op jit(solution)/shard_map/ppermute | solution.py:18
  98.4 20.9 %copy-start.16 = (bf16[192,1152]{1,0:T(8,128)(2,1)}, bf16[192,1152]{1,0:T(8,128)(2,1)S(1)}, u32[]{:S(2)}) copy-start(bf16[192,1152]{1,0:T(8,128)(2,1)S(1)} %collective-permute-done.20.refs_7_) | copy-start | bytes 1327108
  98.4 46.1 %collective-permute-start.21 = (bf16[192,1152]{1,0:T(8,128)(2,1)}, bf16[192,1152]{1,0:T(8,128)(2,1)}, u32[]{:S(2)}, u32[]{:S(2)}) collective-permute-start(bf16[192,1152]{1,0:T(8,128)(2,1)} %collective-permute-done.17.refs_4_), channel_id=1, source_target_pairs={{2,0},{4,2},{6,4},{7,6},{5,7},{3,5},{1,3},{0,1},{10,8},{12,10},{14... | collective-permute-start | bytes 1327112 | tf_op jit(solution)/shard_map/ppermute | solution.py:39
  98.4 61.4 %collective-permute-start.6 = (bf16[4,5,8,3072]{3,2,1,0:T(8,128)(2,1)S(1)}, bf16[4,5,8,3072]{3,2,1,0:T(8,128)(2,1)}, u32[]{:S(2)}, u32[]{:S(2)}) collective-permute-start(bf16[4,5,8,3072]{3,2,1,0:T(8,128)(2,1)S(1)} %collective-permute-done.5.refs_2_), channel_id=1, source_target_pairs={{0,8},{8,0},{16,24},{24,16},{1,9},{9,1},{17,25},{25,17},{2,10},{10... | collective-permute-start | bytes 2949128 | tf_op jit(solution)/shard_map/ppermute | solution.py:18
  98.6 62.3 %collective-permute-start.13 = (bf16[4,5,8,3072]{3,2,1,0:T(8,128)(2,1)}, bf16[4,5,8,3072]{3,2,1,0:T(8,128)(2,1)}, u32[]{:S(2)}, u32[]{:S(2)}) collective-permute-start(bf16[4,5,8,3072]{3,2,1,0:T(8,128)(2,1)} %collective-permute-done.12.refs_6_), channel_id=1, source_target_pairs={{0,8},{8,0},{16,24},{24,16},{1,9},{9,1},{17,25},{25,17},{2,10},{10... | collective-permute-start | bytes 2949128 | tf_op jit(solution)/shard_map/ppermute | solution.py:18
  119.3 41.6 %copy-start.6 = (f32[3072]{0:T(1024)S(1)}, f32[3072]{0:T(1024)}, u32[]{:S(2)}) copy-start(f32[3072]{0:T(1024)} %param.14) | copy-start | bytes 36868
  122.3 21.9 %all-to-all-start = ((bf16[32,5,8,65]{3,2,1,0:T(8,128)(2,1)}), bf16[32,5,8,65]{3,2,1,0:T(8,128)(2,1)S(1)}, u32[]{:S(2)}, u32[]{:S(2)}) async-start(bf16[32,5,8,65]{3,2,1,0:T(8,128)(2,1)} %bitcast.47), calls=%async_computation | async-start | bytes 655360 | tf_op jit(solution)/shard_map/all_to_all | solution.py:446
  144.5 13.3 %collective-permute-start.22 = (bf16[192,1152]{1,0:T(8,128)(2,1)}, bf16[192,1152]{1,0:T(8,128)(2,1)S(1)}, u32[]{:S(2)}, u32[]{:S(2)}) collective-permute-start(bf16[192,1152]{1,0:T(8,128)(2,1)} %copy-done.12), channel_id=1, source_target_pairs={{0,2},{2,4},{4,6},{6,7},{7,5},{5,3},{3,1},{1,0},{8,10},{10,12},{12... | collective-permute-start | bytes 1327112 | tf_op jit(solution)/shard_map/ppermute | solution.py:39
  145.5 13.3 %collective-permute-start.25 = (bf16[192,1152]{1,0:T(8,128)(2,1)}, bf16[192,1152]{1,0:T(8,128)(2,1)S(1)}, u32[]{:S(2)}, u32[]{:S(2)}) collective-permute-start(bf16[192,1152]{1,0:T(8,128)(2,1)} %collective-permute-done.21.refs_8_), channel_id=1, source_target_pairs={{2,0},{4,2},{6,4},{7,6},{5,7},{3,5},{1,3},{0,1},{10,8},{12,10},{14... | collective-permute-start | bytes 1327112 | tf_op jit(solution)/shard_map/ppermute | solution.py:39
  146.8 41.7 %collective-permute-start.23 = (bf16[192,1152]{1,0:T(8,128)(2,1)}, bf16[192,1152]{1,0:T(8,128)(2,1)S(1)}, u32[]{:S(2)}, u32[]{:S(2)}) collective-permute-start(bf16[192,1152]{1,0:T(8,128)(2,1)} %copy-done.14), channel_id=1, source_target_pairs={{0,2},{2,4},{4,6},{6,7},{7,5},{5,3},{3,1},{1,0},{8,10},{10,12},{12... | collective-permute-start | bytes 1327112 | tf_op jit(solution)/shard_map/ppermute | solution.py:39
  157.8 30.7 %collective-permute-start.24 = (bf16[192,1152]{1,0:T(8,128)(2,1)}, bf16[192,1152]{1,0:T(8,128)(2,1)S(1)}, u32[]{:S(2)}, u32[]{:S(2)}) collective-permute-start(bf16[192,1152]{1,0:T(8,128)(2,1)} %copy-done.16), channel_id=1, source_target_pairs={{2,0},{4,2},{6,4},{7,6},{5,7},{3,5},{1,3},{0,1},{10,8},{12,10},{14... | collective-permute-start | bytes 1327112 | tf_op jit(solution)/shard_map/ppermute | solution.py:39
  158.8 34.6 %collective-permute-start.26 = (bf16[192,1152]{1,0:T(8,128)(2,1)S(1)}, bf16[192,1152]{1,0:T(8,128)(2,1)S(1)}, u32[]{:S(2)}, u32[]{:S(2)}) collective-permute-start(bf16[192,1152]{1,0:T(8,128)(2,1)S(1)} %collective-permute-done.22.refs_1_), channel_id=1, source_target_pairs={{0,2},{2,4},{4,6},{6,7},{7,5},{5,3},{3,1},{1,0},{8,10},{10,12},{12... | collective-permute-start | bytes 1327112 | tf_op jit(solution)/shard_map/ppermute | solution.py:42
  159.8 33.6 %collective-permute-start.27 = (bf16[192,1152]{1,0:T(8,128)(2,1)S(1)}, bf16[192,1152]{1,0:T(8,128)(2,1)S(1)}, u32[]{:S(2)}, u32[]{:S(2)}) collective-permute-start(bf16[192,1152]{1,0:T(8,128)(2,1)S(1)} %collective-permute-done.25.refs_4_), channel_id=1, source_target_pairs={{2,0},{4,2},{6,4},{7,6},{5,7},{3,5},{1,3},{0,1},{10,8},{12,10},{14... | collective-permute-start | bytes 1327112 | tf_op jit(solution)/shard_map/ppermute | solution.py:43
  160.8 1.0 copy-start.3
  161.8 15.2 %copy-start.2 = (bf16[384,1152]{1,0:T(8,128)(2,1)S(1)}, bf16[384,1152]{1,0:T(8,128)(2,1)}, u32[]{:S(2)}) copy-start(bf16[384,1152]{1,0:T(8,128)(2,1)} %refs_0_.1) | copy-start | bytes 2654212
  161.8 15.2 %copy-start.9 = (bf16[192,1152]{1,0:T(8,128)(2,1)S(1)}, bf16[192,1152]{1,0:T(8,128)(2,1)}, u32[]{:S(2)}) copy-start(bf16[192,1152]{1,0:T(8,128)(2,1)} %copy-done.8) | copy-start | bytes 1327108
  161.8 15.2 %copy-start.11 = (bf16[192,1152]{1,0:T(8,128)(2,1)S(1)}, bf16[192,1152]{1,0:T(8,128)(2,1)}, u32[]{:S(2)}) copy-start(bf16[192,1152]{1,0:T(8,128)(2,1)} %copy-done.10) | copy-start | bytes 1327108
  161.8 15.2 %copy-start.13 = (bf16[192,1152]{1,0:T(8,128)(2,1)S(1)}, bf16[192,1152]{1,0:T(8,128)(2,1)}, u32[]{:S(2)}) copy-start(bf16[192,1152]{1,0:T(8,128)(2,1)} %copy-done.12) | copy-start | bytes 1327108
  161.8 15.2 %copy-start.15 = (bf16[192,1152]{1,0:T(8,128)(2,1)S(1)}, bf16[192,1152]{1,0:T(8,128)(2,1)}, u32[]{:S(2)}) copy-start(bf16[192,1152]{1,0:T(8,128)(2,1)} %copy-done.14) | copy-start | bytes 1327108
  161.8 15.2 %copy-start.17 = (bf16[192,1152]{1,0:T(8,128)(2,1)S(1)}, bf16[192,1152]{1,0:T(8,128)(2,1)}, u32[]{:S(2)}) copy-start(bf16[192,1152]{1,0:T(8,128)(2,1)} %copy-done.16) | copy-start | bytes 1327108

commit v6 on v4

--- a/solution.py
+++ b/solution.py
@@ -249,33 +249,40 @@
     for spot, part in enumerate(parts):
         group = lax.bitwise_xor(me, spot % groups)
         if halves is None:
-            copies.append((part, held.at[group]))
+            copies.append((spot % groups, part, held.at[group]))
             continue
         for i, k in enumerate(halves[spot // groups]):
-            copies.append((part.at[i], held.at[group, lax.rem(me_ctx - k + n, n)]))
-    copies = [pltpu.make_async_copy(a, b, sems.at[i]) for i, (a, b) in enumerate(copies)]
-    for copy in copies:
+            place = held.at[group, lax.rem(me_ctx - k + n, n)]
+            copies.append((spot % groups, part.at[i], place))
+    copies.sort(key=lambda entry: entry[0])
+    copies = [
+        (slot, pltpu.make_async_copy(a, b, sems.at[i])) for i, (slot, a, b) in enumerate(copies)
+    ]
+    for _, copy in copies:
         copy.start()
-    for copy in copies:
-        copy.wait()
     block, batch = f_dev * pos, embedded.shape[0]
-
-    @pl.loop(0, out_ref.shape[0] * n * block // batch)
-    def _(b):
-        rows = pl.ds(pl.multiple_of(b * batch, 16), batch)
-        embedded[...] = jnp.dot(
-            patches_ref[rows, :patch_size], embed_ref[...], preferred_element_type=jnp.float32
-        )
-
-        @pl.loop(0, batch // block)
-        def _(i):
-            spot = b * (batch // block) + i
-            group, device = spot // n, lax.rem(spot, n)
-            stream = held[group, device].astype(jnp.float32).reshape(block, width)
-            value = embedded[pl.ds(pl.multiple_of(i * block, 8), block)] + stream
-            scale = lax.rsqrt(jnp.mean(value * value, axis=-1, keepdims=True) + 1e-06)
-            value = value * scale * gain_ref[...]
-            out_ref[group, device] = value.reshape(f_dev, pos, width).astype(jnp.bfloat16)
+    batches = n * block // batch
+    for slot in range(groups):
+        group = lax.bitwise_xor(me, slot)
+        for owner, copy in copies:
+            if owner == slot:
+                copy.wait()
+
+        @pl.loop(0, batches)
+        def _(b, group=group):
+            rows = pl.ds(pl.multiple_of((group * batches + b) * batch, 16), batch)
+            embedded[...] = jnp.dot(
+                patches_ref[rows, :patch_size], embed_ref[...], preferred_element_type=jnp.float32
+            )
+
+            @pl.loop(0, batch // block)
+            def _(i):
+                device = b * (batch // block) + i
+                stream = held[group, device].astype(jnp.float32).reshape(block, width)
+                value = embedded[pl.ds(pl.multiple_of(i * block, 8), block)] + stream
+                scale = lax.rsqrt(jnp.mean(value * value, axis=-1, keepdims=True) + 1e-06)
+                value = value * scale * gain_ref[...]
+                out_ref[group, device] = value.reshape(f_dev, pos, width).astype(jnp.bfloat16)
 
 
 def norm_rows(patches, embed_weight, norm_gain, halves, parts, groups, n):
@@ -311,16 +318,16 @@
     refs = list(refs)
     total_ref = refs.pop(0) if has_total else None
     sems, weight, out_ref = refs.pop(), refs.pop(), refs.pop()
-    depth = weight.shape[1]
+    depth = weight.shape[0] // len(spots)
     firsts = piece_rows(count, depth)
     copies, used = [], 0
     for i, pieces in enumerate(spots):
-        row = 0
+        row = i * depth
         for _ in pieces:
             piece = refs[used]
             copies.append(
                 pltpu.make_async_copy(
-                    piece, weight.at[i, pl.ds(row, piece.shape[0])], sems.at[used]
+                    piece, weight.at[pl.ds(row, piece.shape[0])], sems.at[used]
                 )
             )
             row += piece.shape[0]
@@ -335,15 +342,17 @@
     @pl.loop(0, rows // tile)
     def _(i):
         span = pl.ds(pl.multiple_of(i * tile, 16), tile)
-        total = total_ref[span] if has_total else None
-        for j, pieces in enumerate(spots):
+        blocks = []
+        for pieces in spots:
             first = firsts[pieces[0]]
             if count:
                 first = pl.multiple_of(first, 128)
-            product = jnp.dot(
-                normed_ref[span, pl.ds(first, depth)], weight[j], preferred_element_type=jnp.float32
-            )
-            total = product if total is None else total + product
+            blocks.append(normed_ref[span, pl.ds(first, depth)])
+        total = jnp.dot(
+            jnp.concatenate(blocks, axis=1), weight[...], preferred_element_type=jnp.float32
+        )
+        if has_total:
+            total = total_ref[span] + total
         out_ref[span] = total.astype(out_ref.dtype)
 
 
@@ -358,7 +367,7 @@
         in_specs=[VMEM] * (1 + len(first)) + [HBM] * len(chosen),
         out_specs=VMEM,
         scratch_shapes=[
-            pltpu.VMEM((len(spots), depth, columns), jnp.bfloat16),
+            pltpu.VMEM((len(spots) * depth, columns), jnp.bfloat16),
             pltpu.SemaphoreType.DMA((len(chosen),)),
         ],
         compiler_params=pltpu.CompilerParams(vmem_limit_bytes=32 << 20),

time: 215 us -> 213 us (level)
  Pallas kernels: 61.8 us -> 58 us
  transfers between devices with their start and end apart: 23 -> 23, of which waited for: 8 -> 8; matrix products, arithmetic and copies ran while one was open for 1% -> 1% of each run, Pallas kernels for 27% -> 26%
where the time goes in v6:
time: 213 us
  Pallas kernels  58 us (27%)
  waiting for transfers between devices  56.7 us (27%)
  starting transfers between devices  47.8 us (22%)
  blocking collectives  28.3 us (13%)
  local copies, waits for them, and re-layouts  15.2 us (7%)
  matrix products  4.65 us (2%)
    ppermute x7, waiting for transfers between devices, to_owners(): lax.ppermute(pieces[k], 'ctx', [(i, (i + k) % n) for i in range(n)])  29.4 us
    all_to_all x1, blocking collectives, body(): lax.all_to_all(out.reshape(groups * n, f_dev, pos, heads * HD), ('dp', 'c...  28.3 us
    pallas_call x1, Pallas kernels, conv_section(): pl.pallas_call(lagged_kernel, out_shape=(jax.ShapeDtypeStruct(frames.shap...  19.2 us
    pallas_call x3, Pallas kernels, project(): pl.pallas_call(functools.partial(qkv_kernel, count, spots, total is not N...  16.3 us
    pallas_call x1, Pallas kernels, norm_rows(): pl.pallas_call(functools.partial(norm_kernel, halves, groups, embed_weigh...  13.1 us
    all_to_all x1, starting transfers between devices, body(): patches = lax.all_to_all(patches, ('dp', 'ctx'), 0, 0, tiled=True)  12.9 us
    all_to_all x1, waiting for transfers between devices, body(): patches = lax.all_to_all(patches, ('dp', 'ctx'), 0, 0, tiled=True)  12 us
    ppermute x7, starting transfers between devices, to_owners(): lax.ppermute(pieces[k], 'ctx', [(i, (i + k) % n) for i in range(n)])  11.9 us
  transfers between devices with their start and end apart: 23, of which 8 were waited for; matrix products, arithmetic and copies ran while one was open for 1% of the time, Pallas kernels for 26%

profile of v6, /device:TPU:0, one launch (start us, length us, event | category | flops | bytes accessed | tf_op | source)
XLA Modules:
  0.0 212.7 jit_solution(8993603883706671887)
XLA Ops:
  0.6 1.5 copy-done
  2.2 0.1 deal.1
  2.3 5.1 %collective-permute-start.3 = (bf16[5,8,3072]{2,1,0:T(8,128)(2,1)S(1)}, bf16[5,8,3072]{2,1,0:T(8,128)(2,1)S(1)}, u32[]{:S(2)}, u32[]{:S(2)}) collective-permute-start(bf16[5,8,3072]{2,1,0:T(8,128)(2,1)S(1)} %get-tuple-element.17), channel_id=1, source_target_pairs={{0,6},{1,7},{2,0},{3,1},{4,2},{5,3},{6,4},{7,5},{8,14},{9,15},{10,... | collective-permute-start | bytes 737288 | tf_op jit(solution)/shard_map/ppermute | solution.py:234
  7.4 1.5 collective-permute-start.2
  9.0 3.2 %collective-permute-start.1 = (bf16[5,8,3072]{2,1,0:T(8,128)(2,1)S(1)}, bf16[5,8,3072]{2,1,0:T(8,128)(2,1)S(1)}, u32[]{:S(2)}, u32[]{:S(2)}) collective-permute-start(bf16[5,8,3072]{2,1,0:T(8,128)(2,1)S(1)} %get-tuple-element.15), channel_id=1, source_target_pairs={{0,7},{1,0},{2,1},{3,2},{4,3},{5,4},{6,5},{7,6},{8,15},{9,8},{10,9... | collective-permute-start | bytes 737288 | tf_op jit(solution)/shard_map/ppermute | solution.py:234
  12.2 1.1 slice_bitcast_fusion
  13.2 1.3 collective-permute-start
  14.6 0.1 collective-permute-start.10
  14.6 0.0 collective-permute-done.3
  14.7 0.5 collective-permute-start.9
  15.2 5.8 %collective-permute-done.2 = bf16[5,8,3072]{2,1,0:T(8,128)(2,1)S(1)} collective-permute-done((bf16[5,8,3072]{2,1,0:T(8,128)(2,1)S(1)}, bf16[5,8,3072]{2,1,0:T(8,128)(2,1)S(1)}, u32[]{:S(2)}, u32[]{:S(2)}) %collective-permute-start.2) | collective-permute-done | bytes 245792 | tf_op jit(solution)/shard_map/ppermute | solution.py:234
  21.0 0.6 collective-permute-start.8
  21.6 0.0 collective-permute-done.1
  21.6 0.9 collective-permute-start.7
  22.5 0.1 pad_maximum_fusion.refs_0_
  22.6 22.3 %collective-permute-done.10 = bf16[5,8,3072]{2,1,0:T(8,128)(2,1)S(1)} collective-permute-done((bf16[5,8,3072]{2,1,0:T(8,128)(2,1)S(1)}, bf16[5,8,3072]{2,1,0:T(8,128)(2,1)S(1)}, u32[]{:S(2)}, u32[]{:S(2)}) %collective-permute-start.10) | collective-permute-done | bytes 245792 | tf_op jit(solution)/shard_map/ppermute | solution.py:234
  44.9 0.0 collective-permute-start.4
  44.9 1.3 collective-permute-done.9
  46.2 1.5 collective-permute-start.5
  47.7 0.1 pad_maximum_fusion.1.refs_4_
  47.8 0.6 collective-permute-start.12
  48.4 5.2 %collective-permute-start.14 = (bf16[384,1152]{1,0:T(8,128)(2,1)}, bf16[384,1152]{1,0:T(8,128)(2,1)}, u32[]{:S(2)}, u32[]{:S(2)}) collective-permute-start(bf16[384,1152]{1,0:T(8,128)(2,1)} %refs_0_.1), channel_id=1, source_target_pairs={{0,2},{2,4},{4,6},{6,7},{7,5},{5,3},{3,1},{1,0},{8,10},{10,12},{12... | collective-permute-start | bytes 2654216 | tf_op jit(solution)/shard_map/ppermute | solution.py:36
  53.6 0.8 copy-done.6
  54.4 5.1 %collective-permute-start.15 = (bf16[384,1152]{1,0:T(8,128)(2,1)}, bf16[384,1152]{1,0:T(8,128)(2,1)}, u32[]{:S(2)}, u32[]{:S(2)}) collective-permute-start(bf16[384,1152]{1,0:T(8,128)(2,1)} %refs_0_.1), channel_id=1, source_target_pairs={{2,0},{4,2},{6,4},{7,6},{5,7},{3,5},{1,3},{0,1},{10,8},{12,10},{14... | collective-permute-start | bytes 2654216 | tf_op jit(solution)/shard_map/ppermute | solution.py:37
  60.2 0.1 copy.23.latent_weight_ref
  60.3 0.0 copy-start.2
  60.3 1.3 copy-done.2
  61.6 5.0 %copy-done.5 = bf16[3,3,3,512,512]{4,3,2,1,0:T(8,128)(2,1)S(1)} copy-done((bf16[3,3,3,512,512]{4,3,2,1,0:T(8,128)(2,1)S(1)}, bf16[3,3,3,512,512]{4,3,2,1,0:T(8,128)(2,1)}, u32[]{:S(2)}) %copy-start.5) | copy-done | bytes 14155800
  66.7 9.3 %near.1.near_ref = f32[1280,512]{1,0:T(8,128)S(1)} custom-call(bf16[5,16,16,512]{3,2,1,0:T(8,128)(2,1)S(1)} %bitcast.40, bf16[27,512,512]{2,1,0:T(8,128)(2,1)S(1)} %bitcast.44), custom_call_target="tpu_custom_call" | custom-call | flops 6039797760 | bytes 4718592 | tf_op jit(solution)/shard_map/near/pallas_call | solution.py:172
  76.0 1.6 collective-permute-done.14.refs_1_
  77.6 0.1 collective-permute-done.15.refs_2_
  77.7 3.4 %collective-permute-start.16 = (bf16[384,1152]{1,0:T(8,128)(2,1)}, bf16[384,1152]{1,0:T(8,128)(2,1)}, u32[]{:S(2)}, u32[]{:S(2)}) collective-permute-start(bf16[384,1152]{1,0:T(8,128)(2,1)} %collective-permute-done.14.refs_1_), channel_id=1, source_target_pairs={{0,2},{2,4},{4,6},{6,7},{7,5},{5,3},{3,1},{1,0},{8,10},{10,12},{12... | collective-permute-start | bytes 2654216 | tf_op jit(solution)/shard_map/ppermute | solution.py:36
  81.1 1.2 collective-permute-start.17
  82.3 0.2 collective-permute-start.6
  82.5 8.4 %collective-permute-done.12.refs_6_ = bf16[4,5,8,3072]{3,2,1,0:T(8,128)(2,1)} collective-permute-done((bf16[4,5,8,3072]{3,2,1,0:T(8,128)(2,1)S(1)}, bf16[4,5,8,3072]{3,2,1,0:T(8,128)(2,1)}, u32[]{:S(2)}, u32[]{:S(2)}) %collective-permute-start.12) | collective-permute-done | bytes 983072 | tf_op jit(solution)/shard_map/ppermute | solution.py:18
  91.0 19.2 %lagged.1 = (bf16[5,16,16,512]{3,2,1,0:T(8,128)(2,1)}, bf16[1280,16]{1,0:T(8,128)(2,1)S(1)}) custom-call(s32[1]{0:T(128)S(6)} %copy.61.length_ref, bf16[2,16,16,512]{3,2,1,0:T(8,128)(2,1)S(1)} %copy-done.7, bf16[5,16,16,512]{3,2,1,0:T(8,128)(2,1)S(1)} %bitcast.41, bf16[27,512,512]{2,1,0:T(8,128)(2,1)} %bitcast.43, ...), custom_call_target="tpu_custom_call" | custom-call | flops 12079595520 | bytes 9437184 | tf_op jit(solution)/shard_map/lagged/pallas_call | solution.py:182
  110.2 0.0 copy-start.4
  110.2 0.2 copy.60
  110.5 0.2 reshape.95
  110.7 0.8 broadcast_in_dim.15
  111.5 12.9 %all-to-all-start = ((bf16[32,5,8,65]{3,2,1,0:T(8,128)(2,1)}), bf16[32,5,8,65]{3,2,1,0:T(8,128)(2,1)S(1)}, u32[]{:S(2)}, u32[]{:S(2)}) async-start(bf16[32,5,8,65]{3,2,1,0:T(8,128)(2,1)} %bitcast.47), calls=%async_computation | async-start | bytes 655360 | tf_op jit(solution)/shard_map/all_to_all | solution.py:454
  124.5 12.0 %all-to-all-done = bf16[32,5,8,65]{3,2,1,0:T(8,128)(2,1)S(1)} async-done(((bf16[32,5,8,65]{3,2,1,0:T(8,128)(2,1)}), bf16[32,5,8,65]{3,2,1,0:T(8,128)(2,1)S(1)}, u32[]{:S(2)}, u32[]{:S(2)}) %all-to-all-start) | async-done | bytes 166432 | tf_op jit(solution)/shard_map/all_to_all | solution.py:454
  136.5 0.1 slice.25
  136.6 0.9 collective-permute-start.18
  137.5 1.1 collective-permute-start.19
  138.6 0.1 convert_reduce_fusion
  138.7 0.1 iota_compare_fusion.1
  138.8 0.1 and_or_fusion
  138.9 0.0 copy-start.1
  139.0 1.0 copy-done.1
  139.9 13.1 %norm.1 = bf16[4,8,5,8,3072]{4,3,2,1,0:T(8,128)(2,1)S(1)} custom-call(bf16[1280,65]{1,0:T(8,128)(2,1)S(1)} %bitcast.37, bf16[64,3072]{1,0:T(8,128)(2,1)S(1)} %copy-done.1, f32[1,3072]{1,0:T(1,128)S(1)} %bitcast.42, bf16[4,5,8,3072]{3,2,1,0:T(8,128)(2,1)S(1)} %pad_maximum_fusion.refs_0_, bf16[4,5,8,3072]{3,2,1,0:T(8,128)(2,1)S(1)} %collective-permute-done.4.refs_1_, ...), custom_call_target="tpu_custom_call" | custom-call | flops 4026531840 | bytes 15728640 | tf_op jit(solution)/shard_map/norm/pallas_call | solution.py:299
  153.0 5.1 %collective-permute-done.18.refs_1_ = bf16[384,1152]{1,0:T(8,128)(2,1)S(1)} collective-permute-done((bf16[384,1152]{1,0:T(8,128)(2,1)}, bf16[384,1152]{1,0:T(8,128)(2,1)S(1)}, u32[]{:S(2)}, u32[]{:S(2)}) %collective-permute-start.18) | collective-permute-done | bytes 884768 | tf_op jit(solution)/shard_map/ppermute | solution.py:36
  158.1 1.3 collective-permute-start.20
  159.5 1.0 collective-permute-start.21
  160.5 9.8 %qkv.3.refs_0_ = f32[1280,1152]{1,0:T(8,128)S(1)} custom-call(bf16[1280,3072]{1,0:T(8,128)(2,1)S(1)} %bitcast.31, bf16[384,1152]{1,0:T(8,128)(2,1)} %refs_0_.1, bf16[384,1152]{1,0:T(8,128)(2,1)} %collective-permute-done.14.refs_1_, bf16[384,1152]{1,0:T(8,128)(2,1)} %collective-permute-done.15.refs_2_, bf16[384,1152]{1,0:T(8,128)(2,1)} %collective-permute-done.16.refs_3_, ...), custom_call_target="tpu_custom_call" | custom-call | flops 5662310400 | bytes 7864320 | tf_op jit(solution)/shard_map/qkv/pallas_call | solution.py:364
  170.3 3.7 %qkv.4.refs_0_ = f32[1280,1152]{1,0:T(8,128)S(1)} custom-call(bf16[1280,3072]{1,0:T(8,128)(2,1)S(1)} %bitcast.32, f32[1280,1152]{1,0:T(8,128)S(1)} %qkv.3.refs_0_, bf16[384,1152]{1,0:T(8,128)(2,1)S(1)} %collective-permute-done.18.refs_1_, bf16[384,1152]{1,0:T(8,128)(2,1)S(1)} %collective-permute-done.19.refs_2_), custom_call_target="tpu_custom_call" | custom-call | flops 2264924160 | bytes 7864320 | tf_op jit(solution)/shard_map/qkv/pallas_call | solution.py:364
  174.0 2.8 %qkv.5 = bf16[1280,1152]{1,0:T(8,128)(2,1)S(1)} custom-call(bf16[1280,3072]{1,0:T(8,128)(2,1)S(1)} %bitcast.33, f32[1280,1152]{1,0:T(8,128)S(1)} %qkv.4.refs_0_, bf16[192,1152]{1,0:T(8,128)(2,1)S(1)} %collective-permute-done.20.refs_1_, bf16[192,1152]{1,0:T(8,128)(2,1)S(1)} %collective-permute-done.21.refs_2_), custom_call_target="tpu_custom_call" | custom-call | flops 1132462080 | bytes 7864320 | tf_op jit(solution)/shard_map/qkv/pallas_call | solution.py:364
  176.9 0.7 fusion.25
  177.5 2.4 %fusion.26 = (f32[4,8,3,40]{3,2,1,0:T(4,128)S(1)}, f32[4,8,3,40,40]{3,4,2,1,0:T(8,128)}) fusion(pred[4,40,40]{1,2,0:T(8,128)(4,1)S(1)} %and_or_fusion, bf16[4,40,8,3,128]{4,2,3,1,0:T(8,128)(2,1)S(1)} %get-tuple-element.24, bf16[4,40,8,3,128]{4,2,3,1,0:T(8,128)(2,1)S(1)} %get-tuple-element.23), kind=kOutput, calls=%fused_computation.26 | convolution fusion | flops 39936040 | bytes 2602240 | tf_op jit(solution)/shard_map/sub | solution.py:410
  179.9 2.3 %fusion.2 = bf16[4,40,8,3,128]{4,1,3,2,0:T(8,128)(2,1)S(1)} fusion(f32[4,8,3,40,40]{3,4,2,1,0:T(8,128)} %get-tuple-element.26, bf16[4,40,8,3,128]{4,2,3,1,0:T(8,128)(2,1)S(1)} %get-tuple-element.22, f32[4,8,3,40]{3,2,1,0:T(4,128)S(1)} %get-tuple-element.25), kind=kOutput, calls=%fused_computation.6 | convolution fusion | flops 40120320 | bytes 2595840 | tf_op jit(solution)/shard_map/gphts,gsphd->gtphd/dot_general | solution.py:412
  182.2 0.1 copy.30
  182.3 28.3 %all_to_all.10 = bf16[32,5,8,384]{3,2,1,0:T(8,128)(2,1)S(1)} all-to-all(bf16[32,5,8,384]{3,2,1,0:T(8,128)(2,1)S(1)} %bitcast.45), channel_id=1, replica_groups=mesh['dp'=4,'ctx'=8] {'dp','ctx'}, dimensions={0} | all-to-all | bytes 1966080 | tf_op jit(solution)/shard_map/all_to_all | solution.py:462
  210.6 0.8 copy.31
  211.4 1.3 reshape.102
  (30 shorter events, 0.2 us)
Async XLA Ops:
  0.6 1.5 copy-start
  2.3 12.3 %collective-permute-start.3 = (bf16[5,8,3072]{2,1,0:T(8,128)(2,1)S(1)}, bf16[5,8,3072]{2,1,0:T(8,128)(2,1)S(1)}, u32[]{:S(2)}, u32[]{:S(2)}) collective-permute-start(bf16[5,8,3072]{2,1,0:T(8,128)(2,1)S(1)} %get-tuple-element.17), channel_id=1, source_target_pairs={{0,6},{1,7},{2,0},{3,1},{4,2},{5,3},{6,4},{7,5},{8,14},{9,15},{10,... | collective-permute-start | bytes 737288 | tf_op jit(solution)/shard_map/ppermute | solution.py:234
  7.4 13.6 %collective-permute-start.2 = (bf16[5,8,3072]{2,1,0:T(8,128)(2,1)S(1)}, bf16[5,8,3072]{2,1,0:T(8,128)(2,1)S(1)}, u32[]{:S(2)}, u32[]{:S(2)}) collective-permute-start(bf16[5,8,3072]{2,1,0:T(8,128)(2,1)S(1)} %get-tuple-element.16), channel_id=1, source_target_pairs={{0,1},{1,2},{2,3},{3,4},{4,5},{5,6},{6,7},{7,0},{8,9},{9,10},{10,1... | collective-permute-start | bytes 737288 | tf_op jit(solution)/shard_map/ppermute | solution.py:234
  9.0 12.6 %collective-permute-start.1 = (bf16[5,8,3072]{2,1,0:T(8,128)(2,1)S(1)}, bf16[5,8,3072]{2,1,0:T(8,128)(2,1)S(1)}, u32[]{:S(2)}, u32[]{:S(2)}) collective-permute-start(bf16[5,8,3072]{2,1,0:T(8,128)(2,1)S(1)} %get-tuple-element.15), channel_id=1, source_target_pairs={{0,7},{1,0},{2,1},{3,2},{4,3},{5,4},{6,5},{7,6},{8,15},{9,8},{10,9... | collective-permute-start | bytes 737288 | tf_op jit(solution)/shard_map/ppermute | solution.py:234
  13.2 40.4 %collective-permute-start = (bf16[2,16,16,512]{3,2,1,0:T(8,128)(2,1)S(1)}, bf16[2,16,16,512]{3,2,1,0:T(8,128)(2,1)S(1)}, u32[]{:S(2)}, u32[]{:S(2)}) collective-permute-start(bf16[2,16,16,512]{3,2,1,0:T(8,128)(2,1)S(1)} %slice_bitcast_fusion), channel_id=1, source_target_pairs={{0,1},{1,2},{2,3},{3,4},{4,5},{5,6},{6,7},{8,9},{9,10},{10,11},{11... | collective-permute-start | bytes 1572872 | tf_op jit(solution)/shard_map/ppermute | solution.py:426
  14.6 30.3 %collective-permute-start.10 = (bf16[5,8,3072]{2,1,0:T(8,128)(2,1)S(1)}, bf16[5,8,3072]{2,1,0:T(8,128)(2,1)S(1)}, u32[]{:S(2)}, u32[]{:S(2)}) collective-permute-start(bf16[5,8,3072]{2,1,0:T(8,128)(2,1)S(1)} %get-tuple-element.21), channel_id=1, source_target_pairs={{0,4},{1,5},{2,6},{3,7},{4,0},{5,1},{6,2},{7,3},{8,12},{9,13},{10,... | collective-permute-start | bytes 737288 | tf_op jit(solution)/shard_map/ppermute | solution.py:234
  14.7 31.5 %collective-permute-start.9 = (bf16[5,8,3072]{2,1,0:T(8,128)(2,1)S(1)}, bf16[5,8,3072]{2,1,0:T(8,128)(2,1)S(1)}, u32[]{:S(2)}, u32[]{:S(2)}) collective-permute-start(bf16[5,8,3072]{2,1,0:T(8,128)(2,1)S(1)} %get-tuple-element.20), channel_id=1, source_target_pairs={{0,3},{1,4},{2,5},{3,6},{4,7},{5,0},{6,1},{7,2},{8,11},{9,12},{10,... | collective-permute-start | bytes 737288 | tf_op jit(solution)/shard_map/ppermute | solution.py:234
  21.0 26.7 %collective-permute-start.8 = (bf16[5,8,3072]{2,1,0:T(8,128)(2,1)S(1)}, bf16[5,8,3072]{2,1,0:T(8,128)(2,1)S(1)}, u32[]{:S(2)}, u32[]{:S(2)}) collective-permute-start(bf16[5,8,3072]{2,1,0:T(8,128)(2,1)S(1)} %get-tuple-element.19), channel_id=1, source_target_pairs={{0,5},{1,6},{2,7},{3,0},{4,1},{5,2},{6,3},{7,4},{8,13},{9,14},{10,... | collective-permute-start | bytes 737288 | tf_op jit(solution)/shard_map/ppermute | solution.py:234
  21.6 26.1 %collective-permute-start.7 = (bf16[5,8,3072]{2,1,0:T(8,128)(2,1)S(1)}, bf16[5,8,3072]{2,1,0:T(8,128)(2,1)S(1)}, u32[]{:S(2)}, u32[]{:S(2)}) collective-permute-start(bf16[5,8,3072]{2,1,0:T(8,128)(2,1)S(1)} %get-tuple-element.18), channel_id=1, source_target_pairs={{0,2},{1,3},{2,4},{3,5},{4,6},{5,7},{6,0},{7,1},{8,10},{9,11},{10,... | collective-permute-start | bytes 737288 | tf_op jit(solution)/shard_map/ppermute | solution.py:234
  22.5 37.7 %copy-start.8 = (bf16[512,16]{0,1:T(8,128)(2,1)S(1)}, bf16[512,16]{0,1:T(8,128)(2,1)}, u32[]{:S(2)}) copy-start(bf16[512,16]{0,1:T(8,128)(2,1)} %param.12) | copy-start | bytes 49156
  44.9 36.2 %collective-permute-start.4 = (bf16[4,5,8,3072]{3,2,1,0:T(8,128)(2,1)S(1)}, bf16[4,5,8,3072]{3,2,1,0:T(8,128)(2,1)S(1)}, u32[]{:S(2)}, u32[]{:S(2)}) collective-permute-start(bf16[4,5,8,3072]{3,2,1,0:T(8,128)(2,1)S(1)} %pad_maximum_fusion.refs_0_), channel_id=1, source_target_pairs={{0,8},{8,0},{16,24},{24,16},{1,9},{9,1},{17,25},{25,17},{2,10},{10... | collective-permute-start | bytes 2949128 | tf_op jit(solution)/shard_map/ppermute | solution.py:18
  46.2 36.1 %collective-permute-start.5 = (bf16[4,5,8,3072]{3,2,1,0:T(8,128)(2,1)S(1)}, bf16[4,5,8,3072]{3,2,1,0:T(8,128)(2,1)}, u32[]{:S(2)}, u32[]{:S(2)}) collective-permute-start(bf16[4,5,8,3072]{3,2,1,0:T(8,128)(2,1)S(1)} %pad_maximum_fusion.refs_0_), channel_id=1, source_target_pairs={{0,16},{8,24},{16,0},{24,8},{1,17},{9,25},{17,1},{25,9},{2,18},{10... | collective-permute-start | bytes 2949128 | tf_op jit(solution)/shard_map/ppermute | solution.py:18
  47.8 43.1 %collective-permute-start.12 = (bf16[4,5,8,3072]{3,2,1,0:T(8,128)(2,1)S(1)}, bf16[4,5,8,3072]{3,2,1,0:T(8,128)(2,1)}, u32[]{:S(2)}, u32[]{:S(2)}) collective-permute-start(bf16[4,5,8,3072]{3,2,1,0:T(8,128)(2,1)S(1)} %pad_maximum_fusion.1.refs_4_), channel_id=1, source_target_pairs={{0,16},{8,24},{16,0},{24,8},{1,17},{9,25},{17,1},{25,9},{2,18},{10... | collective-permute-start | bytes 2949128 | tf_op jit(solution)/shard_map/ppermute | solution.py:18
  48.4 29.2 %collective-permute-start.14 = (bf16[384,1152]{1,0:T(8,128)(2,1)}, bf16[384,1152]{1,0:T(8,128)(2,1)}, u32[]{:S(2)}, u32[]{:S(2)}) collective-permute-start(bf16[384,1152]{1,0:T(8,128)(2,1)} %refs_0_.1), channel_id=1, source_target_pairs={{0,2},{2,4},{4,6},{6,7},{7,5},{5,3},{3,1},{1,0},{8,10},{10,12},{12... | collective-permute-start | bytes 2654216 | tf_op jit(solution)/shard_map/ppermute | solution.py:36
  53.6 0.8 copy-start.6
  54.4 23.2 %collective-permute-start.15 = (bf16[384,1152]{1,0:T(8,128)(2,1)}, bf16[384,1152]{1,0:T(8,128)(2,1)}, u32[]{:S(2)}, u32[]{:S(2)}) collective-permute-start(bf16[384,1152]{1,0:T(8,128)(2,1)} %refs_0_.1), channel_id=1, source_target_pairs={{2,0},{4,2},{6,4},{7,6},{5,7},{3,5},{1,3},{0,1},{10,8},{12,10},{14... | collective-permute-start | bytes 2654216 | tf_op jit(solution)/shard_map/ppermute | solution.py:37
  60.3 1.3 copy-start.2
  61.6 5.0 %copy-start.5 = (bf16[3,3,3,512,512]{4,3,2,1,0:T(8,128)(2,1)S(1)}, bf16[3,3,3,512,512]{4,3,2,1,0:T(8,128)(2,1)}, u32[]{:S(2)}) copy-start(bf16[3,3,3,512,512]{4,3,2,1,0:T(8,128)(2,1)} %param.11) | copy-start | bytes 42467332
  66.7 24.3 %copy-start.3 = (bf16[1,5,16,16,512]{4,3,2,1,0:T(8,128)(2,1)S(1)}, bf16[1,5,16,16,512]{4,3,2,1,0:T(8,128)(2,1)}, u32[]{:S(2)}) copy-start(bf16[1,5,16,16,512]{4,3,2,1,0:T(8,128)(2,1)} %param.8) | copy-start | bytes 3932164
  66.7 24.3 %copy-start.7 = (bf16[2,16,16,512]{3,2,1,0:T(8,128)(2,1)S(1)}, bf16[2,16,16,512]{3,2,1,0:T(8,128)(2,1)}, u32[]{:S(2)}) copy-start(bf16[2,16,16,512]{3,2,1,0:T(8,128)(2,1)} %copy-done.6) | copy-start | bytes 1572868
  77.6 61.3 %collective-permute-start.11 = (bf16[4,5,8,3072]{3,2,1,0:T(8,128)(2,1)S(1)}, bf16[4,5,8,3072]{3,2,1,0:T(8,128)(2,1)}, u32[]{:S(2)}, u32[]{:S(2)}) collective-permute-start(bf16[4,5,8,3072]{3,2,1,0:T(8,128)(2,1)S(1)} %pad_maximum_fusion.1.refs_4_), channel_id=1, source_target_pairs={{0,8},{8,0},{16,24},{24,16},{1,9},{9,1},{17,25},{25,17},{2,10},{10... | collective-permute-start | bytes 2949128 | tf_op jit(solution)/shard_map/ppermute | solution.py:18
  77.7 58.9 %collective-permute-start.16 = (bf16[384,1152]{1,0:T(8,128)(2,1)}, bf16[384,1152]{1,0:T(8,128)(2,1)}, u32[]{:S(2)}, u32[]{:S(2)}) collective-permute-start(bf16[384,1152]{1,0:T(8,128)(2,1)} %collective-permute-done.14.refs_1_), channel_id=1, source_target_pairs={{0,2},{2,4},{4,6},{6,7},{7,5},{5,3},{3,1},{1,0},{8,10},{10,12},{12... | collective-permute-start | bytes 2654216 | tf_op jit(solution)/shard_map/ppermute | solution.py:36
  81.1 56.4 %collective-permute-start.17 = (bf16[384,1152]{1,0:T(8,128)(2,1)}, bf16[384,1152]{1,0:T(8,128)(2,1)}, u32[]{:S(2)}, u32[]{:S(2)}) collective-permute-start(bf16[384,1152]{1,0:T(8,128)(2,1)} %collective-permute-done.15.refs_2_), channel_id=1, source_target_pairs={{2,0},{4,2},{6,4},{7,6},{5,7},{3,5},{1,3},{0,1},{10,8},{12,10},{14... | collective-permute-start | bytes 2654216 | tf_op jit(solution)/shard_map/ppermute | solution.py:37
  82.3 56.6 %collective-permute-start.6 = (bf16[4,5,8,3072]{3,2,1,0:T(8,128)(2,1)}, bf16[4,5,8,3072]{3,2,1,0:T(8,128)(2,1)}, u32[]{:S(2)}, u32[]{:S(2)}) collective-permute-start(bf16[4,5,8,3072]{3,2,1,0:T(8,128)(2,1)} %collective-permute-done.5.refs_2_), channel_id=1, source_target_pairs={{0,8},{8,0},{16,24},{24,16},{1,9},{9,1},{17,25},{25,17},{2,10},{10... | collective-permute-start | bytes 2949128 | tf_op jit(solution)/shard_map/ppermute | solution.py:18
  91.0 48.0 %collective-permute-start.13 = (bf16[4,5,8,3072]{3,2,1,0:T(8,128)(2,1)}, bf16[4,5,8,3072]{3,2,1,0:T(8,128)(2,1)}, u32[]{:S(2)}, u32[]{:S(2)}) collective-permute-start(bf16[4,5,8,3072]{3,2,1,0:T(8,128)(2,1)} %collective-permute-done.12.refs_6_), channel_id=1, source_target_pairs={{0,8},{8,0},{16,24},{24,16},{1,9},{9,1},{17,25},{25,17},{2,10},{10... | collective-permute-start | bytes 2949128 | tf_op jit(solution)/shard_map/ppermute | solution.py:18
  110.2 28.7 %copy-start.4 = (f32[3072]{0:T(1024)S(1)}, f32[3072]{0:T(1024)}, u32[]{:S(2)}) copy-start(f32[3072]{0:T(1024)} %param.14) | copy-start | bytes 36868
  111.5 25.0 %all-to-all-start = ((bf16[32,5,8,65]{3,2,1,0:T(8,128)(2,1)}), bf16[32,5,8,65]{3,2,1,0:T(8,128)(2,1)S(1)}, u32[]{:S(2)}, u32[]{:S(2)}) async-start(bf16[32,5,8,65]{3,2,1,0:T(8,128)(2,1)} %bitcast.47), calls=%async_computation | async-start | bytes 655360 | tf_op jit(solution)/shard_map/all_to_all | solution.py:454
  136.6 21.5 %collective-permute-start.18 = (bf16[384,1152]{1,0:T(8,128)(2,1)}, bf16[384,1152]{1,0:T(8,128)(2,1)S(1)}, u32[]{:S(2)}, u32[]{:S(2)}) collective-permute-start(bf16[384,1152]{1,0:T(8,128)(2,1)} %collective-permute-done.16.refs_3_), channel_id=1, source_target_pairs={{0,2},{2,4},{4,6},{6,7},{7,5},{5,3},{3,1},{1,0},{8,10},{10,12},{12... | collective-permute-start | bytes 2654216 | tf_op jit(solution)/shard_map/ppermute | solution.py:36
  137.5 22.0 %collective-permute-start.19 = (bf16[384,1152]{1,0:T(8,128)(2,1)}, bf16[384,1152]{1,0:T(8,128)(2,1)S(1)}, u32[]{:S(2)}, u32[]{:S(2)}) collective-permute-start(bf16[384,1152]{1,0:T(8,128)(2,1)} %collective-permute-done.17.refs_4_), channel_id=1, source_target_pairs={{2,0},{4,2},{6,4},{7,6},{5,7},{3,5},{1,3},{0,1},{10,8},{12,10},{14... | collective-permute-start | bytes 2654216 | tf_op jit(solution)/shard_map/ppermute | solution.py:37
  138.9 1.0 copy-start.1
  158.1 15.8 %collective-permute-start.20 = (bf16[192,1152]{1,0:T(8,128)(2,1)S(1)}, bf16[192,1152]{1,0:T(8,128)(2,1)S(1)}, u32[]{:S(2)}, u32[]{:S(2)}) collective-permute-start(bf16[192,1152]{1,0:T(8,128)(2,1)S(1)} %slice.28), channel_id=1, source_target_pairs={{0,2},{2,4},{4,6},{6,7},{7,5},{5,3},{3,1},{1,0},{8,10},{10,12},{12... | collective-permute-start | bytes 1327112 | tf_op jit(solution)/shard_map/ppermute | solution.py:40
  159.5 14.5 %collective-permute-start.21 = (bf16[192,1152]{1,0:T(8,128)(2,1)S(1)}, bf16[192,1152]{1,0:T(8,128)(2,1)S(1)}, u32[]{:S(2)}, u32[]{:S(2)}) collective-permute-start(bf16[192,1152]{1,0:T(8,128)(2,1)S(1)} %slice.29), channel_id=1, source_target_pairs={{2,0},{4,2},{6,4},{7,6},{5,7},{3,5},{1,3},{0,1},{10,8},{12,10},{14... | collective-permute-start | bytes 1327112 | tf_op jit(solution)/shard_map/ppermute | solution.py:41
